TPU v7x, 32 devices: a whole 2x2x4 slice. The times are simulated.
32 devices in a mesh: row: 4 (over y, x), col: 8 (over z, core).
Axes of the slice: x: 2, y: 2, z: 4, core: 2. Of those that a mesh axis runs over, the one named last changes fastest.
Arguments:
- hidden_in: bfloat16 [16384, 2048], P('col', 'row'), may hold values from -6 to 6
- attention_gain: bfloat16 [2048], P('row'), may hold values from 0.5 to 1.5
- query_weight: bfloat16 [2048, 2048], P('col', 'row'), may hold values from -0.125 to 0.125
- key_weight: bfloat16 [2048, 2048], P('col', 'row'), may hold values from -0.125 to 0.125
- value_weight: bfloat16 [2048, 2048], P('col', 'row'), may hold values from -0.125 to 0.125
- projection: bfloat16 [2048, 2048], P('col', 'row'), may hold values from -1 to 1
- query_gain: bfloat16 [128], replicated, may hold values from 0.5 to 1.5
- key_gain: bfloat16 [128], replicated, may hold values from 0.5 to 1.5
- feedforward_gain: bfloat16 [2048], P('row'), may hold values from 0.5 to 1.5
- router_weight: bfloat16 [2048, 64], P('col', 'row'), may hold values from -0.125 to 0.125
- gate_weight: bfloat16 [64, 2048, 1024], P(('row', 'col')), may hold values from -0.125 to 0.125
- up_weight: bfloat16 [64, 2048, 1024], P(('row', 'col')), may hold values from -0.125 to 0.125
- down_weight: bfloat16 [64, 2048, 1024], P(('row', 'col')), may hold values from -4.1875 to 4.1875
- segments: int32 [8, 2048], P('col'), may hold values from 0 to 11, never falling along the last dimension, each value on 1 to 800 neighbouring positions
- routes: int32 [16384, 8], P('col'), may hold values from 0 to 63, all different within a row
- priority: int32 [8, 2048], P('col'), may hold values from 0 to 2047, each once within a row
- cotangent: bfloat16 [16384, 2048], P('col', 'row'), may hold values from -6 to 6
Outputs:
- output: bfloat16 [16384, 2048], P('col', 'row')
- grad_input: float32 [16384, 2048], P('col', 'row')
- grad_attention_gain: float32 [2048], P('row')
- grad_query: float32 [2048, 2048], P('col', 'row')
- grad_key: float32 [2048, 2048], P('col', 'row')
- grad_value: float32 [2048, 2048], P('col', 'row')
- grad_projection: float32 [2048, 2048], P('col', 'row')
- grad_query_gain: float32 [128], replicated
- grad_key_gain: float32 [128], replicated
- grad_feedforward_gain: float32 [2048], P('row')
- grad_router: float32 [2048, 64], P('col', 'row')
- grad_gate: float32 [64, 2048, 1024], P(('row', 'col'))
- grad_up: float32 [64, 2048, 1024], P(('row', 'col'))
- grad_down: float32 [64, 2048, 1024], P(('row', 'col'))
Inputs may be any that keep to these rules, and one draw needn't show every extreme that they name: `segments`: segment numbers never fall along a sequence; a document covers at most 800 positions, and each sequence has one of that length. `routes`: each token names 8 different experts. `priority`: each row is a permutation of the positions of one group's 2048 tokens.
All inputs are finite; a program needn't handle non-finite values.
Results may differ from a plain program's by a relative error of at most 0.02.
Values may be sent and summed in bfloat16 or wider, within the bound.
A program may use at most 448 MiB of HBM per device.

v0:
```python
import jax
import jax.numpy as jnp
from jax import lax
from jax.sharding import PartitionSpec as P

D = 2048
HS = 128
E = 64
TOPK = 8
SEQ = 2048
QBLOCK = 512


EPSILON = 1e-06


def token_total(values):
    return lax.psum(values, "row")


def full_features(values):
    return lax.all_gather(values, "row", axis=1, tiled=True)


def feature_share(values):
    return lax.psum_scatter(values, "row", scatter_dimension=1, tiled=True)


def rotary_tables(tokens):
    half_size = HS // 2
    inverse = 50000.0 ** (-(jnp.arange(half_size, dtype=jnp.float32) * 2.0) / HS)
    angles = jnp.arange(SEQ, dtype=jnp.float32)[:, None] * inverse[None, :]
    repeats = tokens // SEQ
    cosine_table = jnp.tile(jnp.cos(angles), (repeats, 1))[:, None, :]
    sine_table = jnp.tile(jnp.sin(angles), (repeats, 1))[:, None, :]
    return (cosine_table, sine_table)


def rotate(values, cosine_table, sine_table):
    half_size = HS // 2
    first_half = values[..., :half_size]
    second = values[..., half_size:]
    return jnp.concatenate(
        [
            first_half * cosine_table - second * sine_table,
            second * cosine_table + first_half * sine_table,
        ],
        axis=-1,
    )


def prepare_heads(raw_heads, head_gain, cosine_table, sine_table):
    heads = raw_heads.reshape(raw_heads.shape[0], -1, HS)
    factor = lax.rsqrt(jnp.mean(heads * heads, axis=-1, keepdims=True) + EPSILON)
    return rotate(heads * factor * head_gain, cosine_table, sine_table)


def block_operands(queries, key_heads, value_heads, segment_flat, block_index):
    offset = block_index * QBLOCK
    seq_begin = offset // SEQ * SEQ
    query_block = lax.dynamic_slice_in_dim(queries, offset, QBLOCK, 0)
    query_docs = lax.dynamic_slice_in_dim(segment_flat, offset, QBLOCK, 0)
    same_doc = (query_docs[:, None] == segment_flat[None, :])[None]
    scores = jnp.einsum(
        "qhd,khd->hqk", query_block, key_heads, preferred_element_type=jnp.float32
    ) * HS ** (-0.5)
    return (offset, seq_begin, query_block, key_heads, value_heads, same_doc, scores)


def attention_forward(queries, key_heads, value_heads, segment_flat):
    tokens = queries.shape[0]

    def one_block(block_index):
        offset, seq_begin, query_block, key_block, value_block, same_doc, scores = block_operands(
            queries, key_heads, value_heads, segment_flat, block_index
        )
        scores = jnp.where(same_doc, scores, -1e30)
        highest = jnp.max(scores, axis=-1, keepdims=True)
        raised = jnp.exp(scores - highest)
        summed = jnp.sum(raised, axis=-1, keepdims=True)
        weights = (raised / summed).astype(jnp.bfloat16)
        mixed_block = jnp.einsum(
            "hqk,khd->qhd", weights, value_block, preferred_element_type=jnp.float32
        )
        return (mixed_block.astype(jnp.bfloat16), highest[..., 0] + jnp.log(summed[..., 0]))

    mixed_heads, logsum = lax.map(one_block, jnp.arange(tokens // QBLOCK))
    return (mixed_heads.reshape(tokens, -1), logsum)


def attention_backward(queries, key_heads, value_heads, segment_flat, logsum, grad_mixed):
    tokens = queries.shape[0]

    def one_block(state, block_index):
        grad_keys, grad_values = state
        offset, seq_begin, query_block, key_block, value_block, same_doc, scores = block_operands(
            queries, key_heads, value_heads, segment_flat, block_index
        )
        weights = jnp.where(same_doc, jnp.exp(scores - logsum[block_index][:, :, None]), 0.0)
        rounded = weights.astype(jnp.bfloat16)
        grad_block = lax.dynamic_slice_in_dim(grad_mixed, offset, QBLOCK, 0)
        grad_weights = jnp.einsum(
            "qhd,khd->hqk", grad_block, value_block, preferred_element_type=jnp.float32
        )
        inner_sum = jnp.sum(weights * grad_weights, axis=-1, keepdims=True)
        grad_scores = (weights * (grad_weights - inner_sum)).astype(jnp.bfloat16)
        grad_query = jnp.einsum(
            "hqk,khd->qhd", grad_scores, key_block, preferred_element_type=jnp.float32
        ) * HS ** (-0.5)
        key_part = jnp.einsum(
            "hqk,qhd->khd", grad_scores, query_block, preferred_element_type=jnp.float32
        ) * HS ** (-0.5)
        value_part = jnp.einsum(
            "hqk,qhd->khd", rounded, grad_block, preferred_element_type=jnp.float32
        )
        grad_keys = grad_keys + key_part
        grad_values = grad_values + value_part
        return ((grad_keys, grad_values), grad_query)

    empty_keys = jnp.zeros(key_heads.shape, jnp.float32)
    (grad_keys, grad_values), grad_queries = lax.scan(
        one_block, (empty_keys, empty_keys), jnp.arange(tokens // QBLOCK)
    )
    return (grad_queries.reshape(queries.shape), grad_keys, grad_values)


def build_slots(routes, ranks, first_expert, experts_here, capacity):
    tokens = routes.shape[0]
    wanted = first_expert + jnp.arange(experts_here, dtype=jnp.int32)
    member = jnp.any(routes[:, :, None] == wanted[None, None, :], axis=1).astype(jnp.int32)
    by_rank = jnp.zeros((tokens,), jnp.int32).at[ranks].set(jnp.arange(tokens, dtype=jnp.int32))
    ranked = member[by_rank]
    before = jnp.cumsum(ranked, axis=0) - ranked
    slot_index = before[ranks]
    target = jnp.where((member == 1) & (slot_index < capacity), slot_index, capacity)
    column_id = jnp.broadcast_to(jnp.arange(experts_here, dtype=jnp.int32)[None, :], target.shape)
    token_id = jnp.broadcast_to(jnp.arange(tokens, dtype=jnp.int32)[:, None], target.shape)
    slot_table = (
        jnp.zeros((experts_here, capacity), jnp.int32)
        .at[column_id, target]
        .set(token_id, mode="drop")
    )
    filled = (
        jnp.zeros((experts_here, capacity), jnp.float32).at[column_id, target].set(1.0, mode="drop")
    )
    return (slot_table, filled)


def send_direct(per_expert, pieces, col_count):
    experts_here, capacity, feature_count = per_expert.shape
    spread = jnp.repeat(per_expert, pieces, axis=0).reshape(col_count, -1, capacity, feature_count)
    return lax.all_to_all(
        jnp.swapaxes(spread, 0, 1), "col", split_axis=1, concat_axis=1, tiled=True
    )


def send_slots(per_expert, pieces, col_count):
    return send_direct(per_expert, pieces, col_count)


def return_slots(piece_rows, pieces, col_count):
    local_count, row_total, feature_count = piece_rows.shape
    returned = lax.all_to_all(
        piece_rows.reshape(local_count, col_count, row_total // col_count, feature_count),
        "col",
        split_axis=1,
        concat_axis=1,
        tiled=True,
    )
    returned = jnp.swapaxes(returned, 0, 1).reshape(
        -1, pieces, row_total // col_count, feature_count
    )
    return jnp.sum(returned.astype(jnp.float32), axis=1)


def per_device(
    hidden_in,
    attention_gain,
    query_weight,
    key_weight,
    value_weight,
    projection,
    query_gain,
    key_gain,
    feedforward_gain,
    router_weight,
    gate_weight,
    up_weight,
    down_weight,
    segments,
    routes,
    priority,
    cotangent,
):
    tokens, width_here = hidden_in.shape
    row_count = lax.axis_size("row")
    col_count = lax.axis_size("col")
    local_pieces = gate_weight.shape[0]
    pieces = max(1, row_count * col_count // E)
    experts_here = E // row_count
    capacity = tokens * TOPK // E
    row_index = lax.axis_index("row")
    offset = row_index * width_here
    segment_flat = segments.reshape(-1)
    cosine_table, sine_table = rotary_tables(tokens)
    first_gain = attention_gain.astype(jnp.float32)
    second_gain = feedforward_gain.astype(jnp.float32)
    query_scale = query_gain.astype(jnp.float32)
    key_scale = key_gain.astype(jnp.float32)
    residual = hidden_in.astype(jnp.float32)
    first_factor = lax.rsqrt(token_total(jnp.sum(residual * residual, axis=1)) / D + EPSILON)[
        :, None
    ]
    normed_one = full_features((residual * first_factor * first_gain).astype(jnp.bfloat16))
    query_full, key_full, value_full, projection_full, router_full = (
        lax.all_gather(query_weight, "col", axis=0, tiled=True),
        lax.all_gather(key_weight, "col", axis=0, tiled=True),
        lax.all_gather(value_weight, "col", axis=0, tiled=True),
        lax.all_gather(projection, "col", axis=0, tiled=True),
        lax.all_gather(router_weight, "col", axis=0, tiled=True),
    )
    query_raw = jnp.dot(normed_one, query_full, preferred_element_type=jnp.float32)
    key_raw = jnp.dot(normed_one, key_full, preferred_element_type=jnp.float32)
    value_raw = jnp.dot(normed_one, value_full, preferred_element_type=jnp.float32)
    query_heads = prepare_heads(query_raw, query_scale, cosine_table, sine_table).astype(
        jnp.bfloat16
    )
    key_heads = prepare_heads(key_raw, key_scale, cosine_table, sine_table).astype(jnp.bfloat16)
    value_heads = value_raw.astype(jnp.bfloat16).reshape(tokens, -1, HS)
    mixed_heads, logsum = attention_forward(query_heads, key_heads, value_heads, segment_flat)
    branch = feature_share(
        jnp.einsum("tj,mj->tm", mixed_heads, projection_full, preferred_element_type=jnp.float32)
    )
    middle = residual + branch
    second_factor = lax.rsqrt(token_total(jnp.sum(middle * middle, axis=1)) / D + EPSILON)[:, None]
    normed_two = full_features((middle * second_factor * second_gain).astype(jnp.bfloat16))
    logits = jnp.dot(normed_two, router_full, preferred_element_type=jnp.float32)
    raised = jnp.exp(logits)
    router_probs = raised / token_total(jnp.sum(raised, axis=1))[:, None]
    slot_table, filled = build_slots(
        routes, priority[0], row_index * experts_here, experts_here, capacity
    )
    fill_rows = filled[:, :, None]
    dispatched = normed_two[slot_table] * fill_rows.astype(jnp.bfloat16)
    piece_rows = send_slots(dispatched, pieces, col_count).reshape(local_pieces, -1, D)
    gate_values = jnp.einsum(
        "prd,pdf->prf", piece_rows, gate_weight, preferred_element_type=jnp.float32
    )
    upward = jnp.einsum("prd,pdf->prf", piece_rows, up_weight, preferred_element_type=jnp.float32)
    activated = (jax.nn.silu(gate_values) * upward).astype(jnp.bfloat16)
    produced = jnp.einsum(
        "prf,pdf->prd", activated, down_weight, preferred_element_type=jnp.float32
    ).astype(jnp.bfloat16)
    expert_out = return_slots(produced, pieces, col_count)
    slot_prob = jnp.take_along_axis(router_probs.T, slot_table, axis=1) * filled
    combined = (
        jnp.zeros((tokens, D), jnp.float32)
        .at[slot_table.reshape(-1)]
        .add((expert_out * slot_prob[:, :, None]).reshape(-1, D))
    )
    output = (middle + feature_share(combined)).astype(jnp.bfloat16)
    grad_out = cotangent.astype(jnp.float32)
    grad_full = full_features(cotangent)
    grad_slots = grad_full[slot_table]
    slot_grad_prob = jnp.sum(expert_out * grad_slots.astype(jnp.float32), axis=-1) * filled
    column_id = jnp.broadcast_to(
        jnp.arange(experts_here, dtype=jnp.int32)[:, None], slot_table.shape
    )
    grad_prob = (
        jnp.zeros((tokens, experts_here), jnp.float32).at[slot_table, column_id].add(slot_grad_prob)
    )
    outgoing = (grad_slots * slot_prob[:, :, None]).astype(jnp.bfloat16)
    grad_rows = send_slots(outgoing, pieces, col_count).reshape(local_pieces, -1, D)
    grad_down = jnp.einsum("prd,prf->pdf", grad_rows, activated, preferred_element_type=jnp.float32)
    grad_hidden = jnp.einsum(
        "prd,pdf->prf", grad_rows, down_weight, preferred_element_type=jnp.float32
    )
    squashed = jax.nn.sigmoid(gate_values)
    grad_gate_pre = (
        grad_hidden * upward * squashed * (1.0 + gate_values * (1.0 - squashed))
    ).astype(jnp.bfloat16)
    grad_up_pre = (grad_hidden * gate_values * squashed).astype(jnp.bfloat16)
    grad_gate = jnp.einsum(
        "prd,prf->pdf", piece_rows, grad_gate_pre, preferred_element_type=jnp.float32
    )
    grad_up = jnp.einsum(
        "prd,prf->pdf", piece_rows, grad_up_pre, preferred_element_type=jnp.float32
    )
    grad_inputs = (
        jnp.einsum("prf,pdf->prd", grad_gate_pre, gate_weight, preferred_element_type=jnp.float32)
        + jnp.einsum("prf,pdf->prd", grad_up_pre, up_weight, preferred_element_type=jnp.float32)
    ).astype(jnp.bfloat16)
    returned = return_slots(grad_inputs, pieces, col_count) * fill_rows
    grad_normed = (
        jnp.zeros((tokens, D), jnp.float32).at[slot_table.reshape(-1)].add(returned.reshape(-1, D))
    )
    router_inner = token_total(jnp.sum(router_probs * grad_prob, axis=1))
    grad_logits = (router_probs * (grad_prob - router_inner[:, None])).astype(jnp.bfloat16)
    grad_normed = grad_normed + jnp.einsum(
        "te,de->td", grad_logits, router_full, preferred_element_type=jnp.float32
    )
    grad_router = jnp.einsum(
        "td,te->de", normed_two, grad_logits, preferred_element_type=jnp.float32
    )
    grad_normed_two = feature_share(grad_normed)
    scaled_two = grad_normed_two * second_gain
    second_inner = token_total(jnp.sum(scaled_two * middle, axis=1))[:, None]
    grad_middle = (
        grad_out + scaled_two * second_factor - middle * second_factor**3 * second_inner / D
    )
    grad_feedforward_gain = jnp.sum(grad_normed_two * middle * second_factor, axis=0)
    grad_branch = full_features(grad_middle.astype(jnp.bfloat16))
    grad_mixed = jnp.einsum(
        "tm,mj->tj", grad_branch, projection_full, preferred_element_type=jnp.float32
    ).astype(jnp.bfloat16)
    grad_projection = jnp.einsum(
        "tm,tj->mj", grad_branch, mixed_heads, preferred_element_type=jnp.float32
    )
    grad_queries, grad_keys, grad_values = attention_backward(
        query_heads,
        key_heads,
        value_heads,
        segment_flat,
        logsum,
        grad_mixed.reshape(tokens, -1, HS),
    )
    query_pull = jax.vjp(
        lambda raw_heads, head_gain: prepare_heads(raw_heads, head_gain, cosine_table, sine_table),
        query_raw,
        query_scale,
    )[1]
    key_pull = jax.vjp(
        lambda raw_heads, head_gain: prepare_heads(raw_heads, head_gain, cosine_table, sine_table),
        key_raw,
        key_scale,
    )[1]
    grad_query_raw, grad_query_gain = query_pull(grad_queries)
    grad_key_raw, grad_key_gain = key_pull(grad_keys)
    grad_query_raw = grad_query_raw.astype(jnp.bfloat16)
    grad_key_raw = grad_key_raw.astype(jnp.bfloat16)
    grad_value_raw = grad_values.reshape(tokens, -1).astype(jnp.bfloat16)
    grad_normed_one = jnp.einsum(
        "tj,dj->td", grad_query_raw, query_full, preferred_element_type=jnp.float32
    )
    grad_normed_one = grad_normed_one + jnp.einsum(
        "tj,dj->td", grad_key_raw, key_full, preferred_element_type=jnp.float32
    )
    grad_normed_one = grad_normed_one + jnp.einsum(
        "tj,dj->td", grad_value_raw, value_full, preferred_element_type=jnp.float32
    )
    grad_query = jnp.einsum(
        "td,tj->dj", normed_one, grad_query_raw, preferred_element_type=jnp.float32
    )
    grad_key = jnp.einsum("td,tj->dj", normed_one, grad_key_raw, preferred_element_type=jnp.float32)
    grad_value = jnp.einsum(
        "td,tj->dj", normed_one, grad_value_raw, preferred_element_type=jnp.float32
    )
    grad_first = feature_share(grad_normed_one)
    scaled_one = grad_first * first_gain
    first_inner = token_total(jnp.sum(scaled_one * residual, axis=1))[:, None]
    grad_input = (
        grad_middle + scaled_one * first_factor - residual * first_factor**3 * first_inner / D
    )
    grad_attention_gain = jnp.sum(grad_first * residual * first_factor, axis=0)
    padded_first = lax.dynamic_update_slice(
        jnp.zeros((D,), jnp.float32), grad_attention_gain, (offset,)
    )
    padded_second = lax.dynamic_update_slice(
        jnp.zeros((D,), jnp.float32), grad_feedforward_gain, (offset,)
    )
    totals = lax.psum((padded_first, padded_second, grad_query_gain, grad_key_gain), ("row", "col"))
    summed_grads = (
        lax.psum_scatter(grad_query, "col", scatter_dimension=0, tiled=True),
        lax.psum_scatter(grad_key, "col", scatter_dimension=0, tiled=True),
        lax.psum_scatter(grad_value, "col", scatter_dimension=0, tiled=True),
        lax.psum_scatter(grad_projection, "col", scatter_dimension=0, tiled=True),
        lax.psum_scatter(grad_router, "col", scatter_dimension=0, tiled=True),
    )
    return (
        output,
        grad_input,
        lax.dynamic_slice_in_dim(totals[0], offset, width_here),
        summed_grads[0],
        summed_grads[1],
        summed_grads[2],
        summed_grads[3],
        totals[2],
        totals[3],
        lax.dynamic_slice_in_dim(totals[1], offset, width_here),
        summed_grads[4],
        grad_gate,
        grad_up,
        grad_down,
    )


def solution(mesh):
    return jax.shard_map(
        per_device,
        mesh=mesh,
        in_specs=(
            P("col", "row"),
            P("row"),
            P("col", "row"),
            P("col", "row"),
            P("col", "row"),
            P("col", "row"),
            P(),
            P(),
            P("row"),
            P("col", "row"),
            P(("row", "col"), None, None),
            P(("row", "col"), None, None),
            P(("row", "col"), None, None),
            P("col", None),
            P("col", None),
            P("col", None),
            P("col", "row"),
        ),
        out_specs=(
            P("col", "row"),
            P("col", "row"),
            P("row"),
            P("col", "row"),
            P("col", "row"),
            P("col", "row"),
            P("col", "row"),
            P(),
            P(),
            P("row"),
            P("col", "row"),
            P(("row", "col"), None, None),
            P(("row", "col"), None, None),
            P(("row", "col"), None, None),
        ),
        check_vma=False,
    )
```

profile of v0, /device:TPU:0, one launch (start us, length us, event | category | flops | bytes accessed | tf_op | source)
XLA Modules:
  0.0 3638.4 jit_solution(13799031216829421035)
XLA Ops:
  41.5 89.2 %all-gather.9.cloned.1.call-done = bf16[2048,2048]{1,0:T(8,128)(2,1)} async-done(((bf16[2048,512]{1,0:T(8,128)(2,1)}), bf16[2048,2048]{1,0:T(8,128)(2,1)}) %all-gather.9.cloned.1.call-update) | async-done | bytes 8388624 | tf_op jit(solution)/shard_map/all_gather | solution.py:22
  219.4 73.5 %while.27 = (s32[]{:T(128)}, bf16[4,512,4,128]{3,2,1,0:T(4,128)(2,1)}, f32[4,4,512]{2,1,0:T(4,128)}, s32[4]{0:T(128)S(1)}, s32[2048]{0:T(1024)S(1)}, /*index=5*/...) while((s32[]{:T(128)}, ...), condition=%wide.region_7.8_spmd, body=%wide.region_4.7_spmd.sunk | while | flops 2199123968 | bytes 69286112 | solution.py:87
  307.3 152.6 %reduce-scatter.10.cloned.1.call-done = f32[2048,512]{1,0:T(8,128)} async-done(((f32[2048,2048]{1,0:T(8,128)}), f32[2048,512]{1,0:T(8,128)}) %reduce-scatter.10.cloned.1.call-update) | async-done | bytes 4194320 | tf_op jit(solution)/shard_map/reduce_scatter | solution.py:26
  506.4 120.0 %scatter_custom_fusion.4 = f32[4096]{0:T(1024)S(1)} fusion(s32[32768]{0:T(1024)S(1)} %reshape.511, f32[32768]{0:T(1024)S(1)} %broadcast.389, f32[]{:T(128)} %constant.39.clone.1), kind=kCustom, calls=%fused_computation.169 | custom fusion | bytes 16388
  627.5 120.0 %scatter_custom_fusion.3 = s32[4096]{0:T(1024)S(1)} fusion(s32[32768]{0:T(1024)S(1)} %reshape.511, s32[32768]{0:T(1024)S(1)} %reshape.513, s32[]{:T(128)} %constant.37.clone.1), kind=kCustom, calls=%fused_computation.171 | custom fusion | bytes 16388
  777.2 32.8 gather_fusion.4
  810.0 35.8 gather_fusion.2
  866.3 89.6 %all-gather.21.cloned.1.call-done = bf16[2048,2048]{1,0:T(8,128)(2,1)} async-done(((bf16[2048,512]{1,0:T(8,128)(2,1)}), bf16[2048,2048]{1,0:T(8,128)(2,1)}) %all-gather.21.cloned.1.call-update) | async-done | bytes 8388624 | tf_op jit(solution)/shard_map/all_gather | solution.py:22
  956.0 35.8 gather_fusion.3
  1006.4 222.8 %all-to-all-done = bf16[2,8,256,2048]{3,2,0,1:T(8,128)(2,1)} async-done(((bf16[2,8,256,2048]{3,2,0,1:T(8,128)(2,1)}), bf16[2,8,256,2048]{3,2,0,1:T(8,128)(2,1)}, u32[]{:S(2)}, u32[]{:S(2)}) %all-to-all-start) | async-done | bytes 16777248 | tf_op jit(solution)/shard_map/all_to_all | solution.py:152
  1243.5 23.8 fusion.76
  1287.9 310.9 %all-to-all-done.2 = bf16[2,8,256,2048]{3,2,0,1:T(8,128)(2,1)} async-done(((bf16[2,8,256,2048]{3,2,0,1:T(8,128)(2,1)}), bf16[2,8,256,2048]{3,2,0,1:T(8,128)(2,1)}, u32[]{:S(2)}, u32[]{:S(2)}) %all-to-all-start.2) | async-done | bytes 16777248 | tf_op jit(solution)/shard_map/all_to_all | solution.py:152
  1612.9 35.1 multiply_convert_fusion.1
  1648.0 24.8 convolution_convert_fusion
  1692.9 26.5 fusion.78
  1719.4 27.8 add_convert_fusion
  1761.4 295.1 %all-to-all-done.1 = bf16[2,8,256,2048]{3,2,0,1:T(8,128)(2,1)} async-done(((bf16[2,8,256,2048]{3,2,0,1:T(8,128)(2,1)}), bf16[2,8,256,2048]{3,2,0,1:T(8,128)(2,1)}, u32[]{:S(2)}, u32[]{:S(2)}) %all-to-all-start.1) | async-done | bytes 16777248 | tf_op jit(solution)/shard_map/all_to_all | solution.py:163
  2117.8 308.1 %all-to-all-done.3 = bf16[2,8,256,2048]{3,2,0,1:T(8,128)(2,1)} async-done(((bf16[2,8,256,2048]{3,2,0,1:T(8,128)(2,1)}), bf16[2,8,256,2048]{3,2,0,1:T(8,128)(2,1)}, u32[]{:S(2)}, u32[]{:S(2)}) %all-to-all-start.3) | async-done | bytes 16777248 | tf_op jit(solution)/shard_map/all_to_all | solution.py:163
  2444.5 63.9 %scatter_fusion = f32[2048,2048]{1,0:T(8,128)} fusion(f32[2048,2048]{1,0:T(8,128)} %fusion.77, s32[4096]{0:T(1024)S(1)} %bitcast.240, f32[4096,2048]{1,0:T(8,128)} %bitcast_multiply_fusion), kind=kCustom, calls=%fused_computation.7 | custom fusion | flops 8388608 | bytes 100679680 | tf_op jit(solution)/shard_map/scatter-add | solution.py:295
  2528.1 59.4 %scatter_custom_fusion.1 = f32[2048,2048]{1,0:T(8,128)} fusion(s32[4096]{0:T(1024)S(1)} %bitcast.241, f32[4096,2048]{1,0:T(8,128)} %bitcast_multiply_fusion.1, f32[]{:T(128)} %constant.39.clone.1), kind=kCustom, calls=%fused_computation.73 | custom fusion | flops 8388608 | bytes 16777728 | tf_op jit(solution)/shard_map/scatter-add | solution.py:259
  2587.6 72.6 %reduce-scatter.14.cloned.1.call-done = f32[2048,512]{1,0:T(8,128)} async-done(((f32[2048,2048]{1,0:T(8,128)}), f32[2048,512]{1,0:T(8,128)}) %reduce-scatter.14.cloned.1.call-update) | async-done | bytes 4194320 | tf_op jit(solution)/shard_map/reduce_scatter | solution.py:26
  2674.1 143.5 %reduce-scatter.12.cloned.1.call-done = f32[2048,512]{1,0:T(8,128)} async-done(((f32[2048,2048]{1,0:T(8,128)}), f32[2048,512]{1,0:T(8,128)}) %reduce-scatter.12.cloned.1.call-update) | async-done | bytes 4194320 | tf_op jit(solution)/shard_map/reduce_scatter | solution.py:26
  2825.1 87.4 %all-gather.23.cloned.1.call-done = bf16[2048,2048]{1,0:T(8,128)(2,1)} async-done(((bf16[2048,512]{1,0:T(8,128)(2,1)}), bf16[2048,2048]{1,0:T(8,128)(2,1)}) %all-gather.23.cloned.1.call-update) | async-done | bytes 8388624 | tf_op jit(solution)/shard_map/all_gather | solution.py:22
  2922.4 227.3 %while.28 = (s32[]{:T(128)}, f32[2048,4,128]{0,2,1:T(8,128)}, f32[2048,4,128]{0,2,1:T(8,128)}, f32[4,512,4,128]{3,1,0,2:T(8,128)}, s32[4]{0:T(128)S(1)}, /*index...) while((s32[]{:T(128)}, f32[2048,4,128]{0,2,1:T(8,128)}, ...), condition=%wide.region_31.32_spmd.clone, body=%wide.region_29.31_spmd.clone.sunk | while | flops 5438175232 | bytes 231807408 | solution.py:121
  3279.0 25.4 fusion.86
  3314.5 25.3 fusion.85
  3339.8 25.2 fusion.84
  3365.3 28.6 reduce-scatter.16.cloned.1.call-done
  3397.5 39.7 %all-reduce.4 = (f32[2048]{0:T(1024)S(1)}, f32[128]{0:T(128)}, f32[128]{0:T(128)}, f32[2048]{0:T(1024)S(1)}) all-reduce(f32[2048]{0:T(1024)S(1)} %dynamic_update_slice.18, f32[128]{0:T(128)S(1)} %copy-done.69, f32[128]{0:T(128)S(1)} %copy-done.68, f32[2048]{0:T(1024)S(1)} %dynamic_update_slice.19), channel_id=1, replica_groups=mesh['row'=4,'col'=8] {'row','col'}, use_global_device_ids=true, to_apply=%region_38.39 | all-reduce | flops 4352 | bytes 34816 | tf_op jit(solution)/shard_map/psum | solution.py:371
  3478.2 51.1 %reduce-scatter.22.cloned.1.call-done = f32[256,512]{1,0:T(8,128)} async-done(((f32[2048,512]{1,0:T(8,128)}), f32[256,512]{1,0:T(8,128)}) %reduce-scatter.22.cloned.1.call-update) | async-done | bytes 524304 | tf_op jit(solution)/shard_map/reduce_scatter | solution.py:375
  3529.3 51.1 %reduce-scatter.20.cloned.1.call-done = f32[256,512]{1,0:T(8,128)} async-done(((f32[2048,512]{1,0:T(8,128)}), f32[256,512]{1,0:T(8,128)}) %reduce-scatter.20.cloned.1.call-update) | async-done | bytes 524304 | tf_op jit(solution)/shard_map/reduce_scatter | solution.py:374
  3580.5 51.1 %reduce-scatter.18.cloned.1.call-done = f32[256,512]{1,0:T(8,128)} async-done(((f32[2048,512]{1,0:T(8,128)}), f32[256,512]{1,0:T(8,128)}) %reduce-scatter.18.cloned.1.call-update) | async-done | bytes 524304 | tf_op jit(solution)/shard_map/reduce_scatter | solution.py:373
  (450 shorter events, 933.3 us)
Async XLA Ops:
  7.2 34.3 all-gather.15.cloned.1.call-start
  7.9 122.8 %all-gather.9.cloned.1.call-start = ((), (), s32[]{:S(2)}) async-start(), calls=%async_computation.13 | async-start | bytes 10485760 | tf_op jit(solution)/shard_map/all_gather | solution.py:22
  27.0 134.4 %all-gather.11.cloned.1.call-start = ((), (), s32[]{:S(2)}) async-start(), calls=%async_computation.14 | async-start | bytes 2359296 | tf_op jit(solution)/shard_map/all_gather | solution.py:216
  27.7 163.7 %all-gather.13.cloned.1.call-start = ((), (), s32[]{:S(2)}) async-start(), calls=%async_computation.15 | async-start | bytes 2359296 | tf_op jit(solution)/shard_map/all_gather | solution.py:217
  28.3 264.6 %all-gather.17.cloned.1.call-start = ((), (), s32[]{:S(2)}) async-start(), calls=%async_computation.17 | async-start | bytes 2359296 | tf_op jit(solution)/shard_map/all_gather | solution.py:219
  28.9 431.0 %reduce-scatter.10.cloned.1.call-start = ((), (), s32[]{:S(2)}) async-start(), calls=%async_computation.18 | async-start | bytes 20971520 | tf_op jit(solution)/shard_map/reduce_scatter | solution.py:26
  29.0 182.5 %copy-start.66 = (f32[128]{0:T(128)}, f32[128]{0:T(128)S(1)}, u32[]{:S(2)}) copy-start(f32[128]{0:T(128)S(1)} %convert_element_type.151) | copy-start | bytes 1540
  306.7 455.7 %all-gather.19.cloned.1.call-start = ((), (), s32[]{:S(2)}) async-start(), calls=%async_computation.19 | async-start | bytes 10485760 | tf_op jit(solution)/shard_map/all_gather | solution.py:22
  505.1 243.1 %copy-start.61 = (bf16[256,16]{0,1:T(8,128)(2,1)S(1)}, bf16[256,16]{0,1:T(8,128)(2,1)}, u32[]{:S(2)}) copy-start(bf16[256,16]{0,1:T(8,128)(2,1)} %param.30) | copy-start | bytes 24580
  627.1 182.9 %copy-start.38 = (f32[16,256]{1,0:T(8,128)}, f32[16,256]{1,0:T(8,128)S(1)}, u32[]{:S(2)}) copy-start(f32[16,256]{1,0:T(8,128)S(1)} %reshape.439) | copy-start | bytes 49156
  810.0 181.8 %copy-start.42 = (f32[16,256]{1,0:T(8,128)}, f32[16,256]{1,0:T(8,128)S(1)}, u32[]{:S(2)}) copy-start(f32[16,256]{1,0:T(8,128)S(1)} %get-tuple-element.377) | copy-start | bytes 49156
  859.8 369.4 %all-to-all-start = ((bf16[2,8,256,2048]{3,2,0,1:T(8,128)(2,1)}), bf16[2,8,256,2048]{3,2,0,1:T(8,128)(2,1)}, u32[]{:S(2)}, u32[]{:S(2)}) async-start(bf16[2,8,256,2048]{3,2,0,1:T(8,128)(2,1)} %multiply_bitcast_fusion), calls=%async_computation.1 | async-start | bytes 33554432 | tf_op jit(solution)/shard_map/all_to_all | solution.py:152
  865.6 90.4 %all-gather.21.cloned.1.call-start = ((), (), s32[]{:S(2)}) async-start(), calls=%async_computation.21 | async-start | bytes 10485760 | tf_op jit(solution)/shard_map/all_gather | solution.py:22
  1229.2 369.6 %all-to-all-start.2 = ((bf16[2,8,256,2048]{3,2,0,1:T(8,128)(2,1)}), bf16[2,8,256,2048]{3,2,0,1:T(8,128)(2,1)}, u32[]{:S(2)}, u32[]{:S(2)}) async-start(bf16[2,8,256,2048]{3,2,0,1:T(8,128)(2,1)} %fusion.32), calls=%async_computation.4 | async-start | bytes 33554432 | tf_op jit(solution)/shard_map/all_to_all | solution.py:152
  1687.0 369.6 %all-to-all-start.1 = ((bf16[2,8,256,2048]{3,2,0,1:T(8,128)(2,1)}), bf16[2,8,256,2048]{3,2,0,1:T(8,128)(2,1)}, u32[]{:S(2)}, u32[]{:S(2)}) async-start(bf16[2,8,256,2048]{3,2,0,1:T(8,128)(2,1)} %copy.173), calls=%async_computation.2 | async-start | bytes 33554432 | tf_op jit(solution)/shard_map/all_to_all | solution.py:163
  1761.4 300.9 %copy-start.37 = (s32[16,256,1]{1,0,2:T(8,128)S(1)}, s32[16,256,1]{1,0,2:T(8,128)}, u32[]{:S(2)}) copy-start(s32[16,256,1]{1,0,2:T(8,128)} %get-tuple-element.374) | copy-start | bytes 49156
  1761.4 301.0 %copy-start.72 = (s32[2]{0:T(128)S(1)}, s32[2]{0:T(128)}, u32[]{:S(2)}) copy-start(s32[2]{0:T(128)} %constant.156) | copy-start | bytes 28
  1761.4 301.0 %copy-start.71 = (s32[2]{0:T(128)S(1)}, s32[2]{0:T(128)}, u32[]{:S(2)}) copy-start(s32[2]{0:T(128)} %constant.159) | copy-start | bytes 28
  1761.4 301.1 %copy-start.41 = (s32[4096]{0:T(1024)S(1)}, s32[4096]{0:T(1024)}, u32[]{:S(2)}) copy-start(s32[4096]{0:T(1024)} %copy-done.40) | copy-start | bytes 49156
  2056.5 369.4 %all-to-all-start.3 = ((bf16[2,8,256,2048]{3,2,0,1:T(8,128)(2,1)}), bf16[2,8,256,2048]{3,2,0,1:T(8,128)(2,1)}, u32[]{:S(2)}, u32[]{:S(2)}) async-start(bf16[2,8,256,2048]{3,2,0,1:T(8,128)(2,1)} %copy.175), calls=%async_computation.5 | async-start | bytes 33554432 | tf_op jit(solution)/shard_map/all_to_all | solution.py:163
  2062.3 598.0 %reduce-scatter.14.cloned.1.call-start = ((), (), s32[]{:S(2)}) async-start(), calls=%async_computation.22 | async-start | bytes 20971520 | tf_op jit(solution)/shard_map/reduce_scatter | solution.py:26
  2109.2 316.7 %copy-start.36 = (f32[4096]{0:T(1024)S(1)}, f32[4096]{0:T(1024)}, u32[]{:S(2)}) copy-start(f32[4096]{0:T(1024)} %copy-done.35) | copy-start | bytes 49156
  2508.4 309.1 %reduce-scatter.12.cloned.1.call-start = ((), (), s32[]{:S(2)}) async-start(), calls=%async_computation.20 | async-start | bytes 20971520 | tf_op jit(solution)/shard_map/reduce_scatter | solution.py:26
  2587.5 230.0 %copy-start.17 = (bf16[2048,512]{1,0:T(8,128)(2,1)S(1)}, bf16[2048,512]{1,0:T(8,128)(2,1)}, u32[]{:S(2)}) copy-start(bf16[2048,512]{1,0:T(8,128)(2,1)} %param.37) | copy-start | bytes 6291460
  2587.6 230.0 %copy-start.55 = (f32[2048]{0:T(1024)S(1)}, f32[2048]{0:T(1024)}, u32[]{:S(2)}) copy-start(f32[2048]{0:T(1024)} %get-tuple-element.380) | copy-start | bytes 24580
  2587.6 324.9 %all-gather.23.cloned.1.call-start = ((), (), s32[]{:S(2)}) async-start(), calls=%async_computation.23 | async-start | bytes 10485760 | tf_op jit(solution)/shard_map/all_gather | solution.py:22
  2825.0 568.9 %reduce-scatter.16.cloned.1.call-start = ((), (), s32[]{:S(2)}) async-start(), calls=%async_computation.24 | async-start | bytes 20971520 | tf_op jit(solution)/shard_map/reduce_scatter | solution.py:26
  3240.1 214.8 %reduce-scatter.26.cloned.1.call-start = ((), (), s32[]{:S(2)}) async-start(), calls=%async_computation.29 | async-start | bytes 147456 | tf_op jit(solution)/shard_map/reduce_scatter | solution.py:377
  3246.1 232.1 %reduce-scatter.24.cloned.1.call-start = ((), (), s32[]{:S(2)}) async-start(), calls=%async_computation.28 | async-start | bytes 4718592 | tf_op jit(solution)/shard_map/reduce_scatter | solution.py:376
  3257.2 272.2 %reduce-scatter.22.cloned.1.call-start = ((), (), s32[]{:S(2)}) async-start(), calls=%async_computation.27 | async-start | bytes 4718592 | tf_op jit(solution)/shard_map/reduce_scatter | solution.py:375
  3267.3 313.2 %reduce-scatter.20.cloned.1.call-start = ((), (), s32[]{:S(2)}) async-start(), calls=%async_computation.26 | async-start | bytes 4718592 | tf_op jit(solution)/shard_map/reduce_scatter | solution.py:374
  3279.0 352.6 %reduce-scatter.18.cloned.1.call-start = ((), (), s32[]{:S(2)}) async-start(), calls=%async_computation.25 | async-start | bytes 4718592 | tf_op jit(solution)/shard_map/reduce_scatter | solution.py:373
  (87 other events, 2324.0 us)
Sparse Core Ops, SparseCore 0:
  9.6 31.8 all-gather.14
  43.9 86.7 all-gather.8
  132.3 29.1 all-gather.10
  162.9 28.5 all-gather.12
  192.9 28.5 all-gather.16
  306.8 153.0 reduce-scatter.9
  479.1 87.3 all-gather.18
  868.2 87.7 all-gather.20
  2508.6 151.6 reduce-scatter.13
  2663.7 153.7 reduce-scatter.11
  2825.1 87.3 all-gather.22
  3240.2 153.7 reduce-scatter.15
  3396.8 30.6 reduce-scatter.25
  3430.1 48.0 reduce-scatter.23
  3480.9 48.3 reduce-scatter.21
  3532.0 48.3 reduce-scatter.19
  3583.2 48.3 reduce-scatter.17
where the time goes:
time: 3650 us; the launch traced here: 3640 us
  waiting for transfers between devices  2020 us (55%)
  matrix products  591 us (16%)
  local copies, waits for them, and re-layouts  468 us (13%)
  other arithmetic  394 us (11%)
  blocking collectives  112 us (3%)
    all_to_all x2, waiting for transfers between devices, return_slots(): lax.all_to_all(piece_rows.reshape(local_count, col_count, row_total // co...  603 us
    all_to_all x2, waiting for transfers between devices, send_direct(): lax.all_to_all(jnp.swapaxes(spread, 0, 1), 'col', split_axis=1, concat_ax...  534 us
    reduce_scatter x4, waiting for transfers between devices, feature_share(): return lax.psum_scatter(values, 'row', scatter_dimension=1, tiled=True)  397 us
    all_gather x4, waiting for transfers between devices, full_features(): return lax.all_gather(values, 'row', axis=1, tiled=True)  266 us
    unnamed x159, local copies, waits for them, and re-layouts  248 us
  transfers between devices with their start and end apart: 21, of which 18 were waited for; matrix products, arithmetic and copies ran while one was open for 23% of the time, Pallas kernels for 0%

commit v1 on v0

v1 whole, which is shorter than its diff:
```python
import functools

import jax
import jax.numpy as jnp
from jax import lax
from jax.experimental import pallas as pl
from jax.experimental.pallas import tpu as pltpu
from jax.sharding import Mesh, PartitionSpec as P

D = 2048
HS = 128
E = 64
TOPK = 8
SEQ = 2048
EPSILON = 1e-06
SCALE = HS ** (-0.5)
CHUNKS = 2
TOKENS_AXES = ("z", "core")
SWAP_AXES = ("row", "core")
ALL_AXES = ("row", "z", "core")
BF = jnp.bfloat16
F32 = jnp.float32
VMEM_BYTES = 60 * 1024 * 1024


def call(body, grid, in_specs, out_specs, out_shape, scratch=(), flops=0, moved=0, prefetch=0, name=None):
    return pl.pallas_call(
        body,
        out_shape=out_shape,
        grid_spec=pltpu.PrefetchScalarGridSpec(
            num_scalar_prefetch=prefetch,
            grid=grid,
            in_specs=in_specs,
            out_specs=out_specs,
            scratch_shapes=list(scratch),
        ),
        compiler_params=pltpu.CompilerParams(
            dimension_semantics=("arbitrary",) * len(grid), vmem_limit_bytes=VMEM_BYTES
        ),
        cost_estimate=pl.CostEstimate(flops=flops, bytes_accessed=moved, transcendentals=0),
        name=name,
    )


def shape(dims, dtype):
    return jax.ShapeDtypeStruct(dims, dtype)


def dot(left, right, left_dim=1, right_dim=0):
    return lax.dot_general(
        left, right, (((left_dim,), (right_dim,)), ((), ())), preferred_element_type=F32
    )


def rotary_tables():
    half_size = HS // 2
    inverse = 50000.0 ** (-(jnp.arange(half_size, dtype=F32) * 2.0) / HS)
    angles = jnp.arange(SEQ, dtype=F32)[:, None] * inverse[None, :]
    cosine, sine = jnp.cos(angles), jnp.sin(angles)
    return (
        jnp.concatenate([cosine, cosine], axis=1),
        jnp.concatenate([-sine, sine], axis=1),
    )


def project_body(x_ref, gain_ref, w_ref, cos_ref, sin_ref, hg_ref, normed_ref, heads_ref, raw_ref):
    x = x_ref[...].astype(F32)
    factor = lax.rsqrt(jnp.mean(x * x, axis=1, keepdims=True) + EPSILON)
    normed = (x * factor * gain_ref[...]).astype(BF)
    normed_ref[...] = normed
    raw = dot(normed, w_ref[...])
    turned = raw_ref.shape[1]
    raw_ref[...] = raw[:, :turned]
    cosine, sine = cos_ref[...], sin_ref[...]
    for head in range(turned // HS):
        part = raw[:, head * HS : (head + 1) * HS]
        unit = part * lax.rsqrt(jnp.mean(part * part, axis=1, keepdims=True) + EPSILON)
        scaled = unit * hg_ref[:, head * HS : (head + 1) * HS]
        heads_ref[:, head * HS : (head + 1) * HS] = (
            scaled * cosine + pltpu.roll(scaled, HS // 2, 1) * sine
        ).astype(BF)
    heads_ref[:, turned:] = raw[:, turned:].astype(BF)


def project(hidden, gain, weights, cosine, sine, head_gains):
    tokens, width = hidden.shape
    columns = weights.shape[1]
    turned = columns // 3 * 2
    tile = 256
    return call(
        project_body,
        (tokens // tile,),
        [
            pl.BlockSpec((tile, width), lambda t: (t, 0)),
            pl.BlockSpec((1, width), lambda t: (0, 0)),
            pl.BlockSpec((width, columns), lambda t: (0, 0)),
            pl.BlockSpec((tile, HS), lambda t: (t, 0)),
            pl.BlockSpec((tile, HS), lambda t: (t, 0)),
            pl.BlockSpec((1, turned), lambda t: (0, 0)),
        ],
        [
            pl.BlockSpec((tile, width), lambda t: (t, 0)),
            pl.BlockSpec((tile, columns), lambda t: (t, 0)),
            pl.BlockSpec((tile, turned), lambda t: (t, 0)),
        ],
        [shape((tokens, width), BF), shape((tokens, columns), BF), shape((tokens, turned), F32)],
        flops=2 * tokens * width * columns,
        moved=6 * tokens * width + 2 * width * columns + 6 * tokens * columns,
        name="project",
    )(hidden, gain, weights, cosine, sine, head_gains)


QUERY_TILE = 256
KEY_TILE = 256


def key_ranges(segment):
    first = segment[::QUERY_TILE]
    last = segment[QUERY_TILE - 1 :: QUERY_TILE]
    key_first = segment[::KEY_TILE]
    key_last = segment[KEY_TILE - 1 :: KEY_TILE]
    meets = (key_first[None, :] <= last[:, None]) & (key_last[None, :] >= first[:, None])
    order = jnp.arange(meets.shape[1], dtype=jnp.int32)[None, :]
    low = jnp.min(jnp.where(meets, order, meets.shape[1]), axis=1)
    high = jnp.max(jnp.where(meets, order + 1, 0), axis=1)
    return low.astype(jnp.int32), high.astype(jnp.int32)


def key_rows(step):
    return pl.ds(pl.multiple_of(step * KEY_TILE, KEY_TILE), KEY_TILE)


def attend_body(low, high, q_ref, k_ref, v_ref, qs_ref, ks_ref, out_ref, sum_ref):
    block = pl.program_id(1)
    query = q_ref[...]
    query_docs = qs_ref[...]

    def step(index, state):
        total, mixed = state
        rows = key_rows(index)
        scores = dot(query, k_ref[rows, :], 1, 1) * SCALE
        raised = jnp.where(query_docs == ks_ref[:, rows], jnp.exp(scores), 0.0)
        total = total + jnp.sum(raised, axis=1, keepdims=True)
        mixed = mixed + dot(raised.astype(BF), v_ref[rows, :])
        return total, mixed

    total, mixed = lax.fori_loop(
        low[block],
        high[block],
        step,
        (jnp.zeros((QUERY_TILE, 1), F32), jnp.zeros((QUERY_TILE, HS), F32)),
    )
    out_ref[...] = (mixed / total).astype(BF)
    sum_ref[0] = total


def attend(heads, segment, low, high):
    tokens, columns = heads.shape
    count = columns // 3 // HS
    return call(
        attend_body,
        (count, tokens // QUERY_TILE),
        [
            pl.BlockSpec((QUERY_TILE, HS), lambda h, b, lo, hi: (b, h)),
            pl.BlockSpec((tokens, HS), lambda h, b, lo, hi: (0, count + h)),
            pl.BlockSpec((tokens, HS), lambda h, b, lo, hi: (0, 2 * count + h)),
            pl.BlockSpec((QUERY_TILE, 1), lambda h, b, lo, hi: (b, 0)),
            pl.BlockSpec((1, tokens), lambda h, b, lo, hi: (0, 0)),
        ],
        [
            pl.BlockSpec((QUERY_TILE, HS), lambda h, b, lo, hi: (b, h)),
            pl.BlockSpec((1, QUERY_TILE, 1), lambda h, b, lo, hi: (h, b, 0)),
        ],
        [shape((tokens, count * HS), BF), shape((count, tokens, 1), F32)],
        flops=4 * count * tokens * tokens * HS // 2,
        moved=8 * tokens * columns,
        prefetch=2,
        name="attend",
    )(low, high, heads, heads, heads, segment[:, None], segment[None, :])


def head_back(grad, raw, gain, cosine, sine):
    turned = grad * cosine - pltpu.roll(grad, HS // 2, 1) * sine
    factor = lax.rsqrt(jnp.mean(raw * raw, axis=1, keepdims=True) + EPSILON)
    unit = raw * factor
    gain_part = jnp.sum(turned * unit, axis=0, keepdims=True)
    pulled = turned * gain
    inner = jnp.mean(pulled * unit, axis=1, keepdims=True)
    return (pulled - unit * inner) * factor, gain_part


def attend_back_body(
    low, high, q_ref, k_ref, v_ref, g_ref, o_ref, s_ref, qs_ref, ks_ref, qr_ref, kr_ref,
    cos_ref, sin_ref, hg_ref, gq_ref, gk_ref, gv_ref, gain_ref, keys_ref, values_ref,
):
    block = pl.program_id(1)

    @pl.when(block == 0)
    def _():
        keys_ref[...] = jnp.zeros_like(keys_ref)
        values_ref[...] = jnp.zeros_like(values_ref)

    @pl.when((block == 0) & (pl.program_id(0) == 0))
    def _():
        gain_ref[...] = jnp.zeros_like(gain_ref)

    query, grad = q_ref[...], g_ref[...]
    query_docs = qs_ref[...]
    scale_back = 1.0 / s_ref[0]
    inner = jnp.sum(grad.astype(F32) * o_ref[...].astype(F32), axis=1, keepdims=True)

    def step(index, grad_query):
        rows = key_rows(index)
        key = k_ref[rows, :]
        scores = dot(query, key, 1, 1) * SCALE
        weights = jnp.where(query_docs == ks_ref[:, rows], jnp.exp(scores) * scale_back, 0.0)
        grad_weights = dot(grad, v_ref[rows, :], 1, 1)
        grad_scores = (weights * (grad_weights - inner)).astype(BF)
        values_ref[rows, :] += dot(weights.astype(BF), grad, 0, 0)
        keys_ref[rows, :] += dot(grad_scores, query, 0, 0)
        return grad_query + dot(grad_scores, key)

    grad_query = lax.fori_loop(
        low[block], high[block], step, jnp.zeros((QUERY_TILE, HS), F32)
    )
    rows = pl.ds(pl.multiple_of(block * QUERY_TILE, QUERY_TILE), QUERY_TILE)
    back, part = head_back(
        grad_query * SCALE, qr_ref[...], hg_ref[0:1, :], cos_ref[rows, :], sin_ref[rows, :]
    )
    gq_ref[...] = back.astype(BF)
    gain_ref[0:1, :] += part

    @pl.when(block == pl.num_programs(1) - 1)
    def _():
        back, part = head_back(
            keys_ref[...] * SCALE, kr_ref[...], hg_ref[1:2, :], cos_ref[...], sin_ref[...]
        )
        gk_ref[...] = back.astype(BF)
        gain_ref[1:2, :] += part
        gv_ref[...] = values_ref[...].astype(BF)


def attend_back(heads, grad_mixed, mixed, sums, segment, low, high, raw, cosine, sine, gains):
    tokens, columns = heads.shape
    count = columns // 3 // HS
    whole = lambda h, b, lo, hi: (0, 0)
    tile = lambda h, b, lo, hi: (b, h)
    column = lambda h, b, lo, hi: (0, h)
    return call(
        attend_back_body,
        (count, tokens // QUERY_TILE),
        [
            pl.BlockSpec((QUERY_TILE, HS), tile),
            pl.BlockSpec((tokens, HS), lambda h, b, lo, hi: (0, count + h)),
            pl.BlockSpec((tokens, HS), lambda h, b, lo, hi: (0, 2 * count + h)),
            pl.BlockSpec((QUERY_TILE, HS), tile),
            pl.BlockSpec((QUERY_TILE, HS), tile),
            pl.BlockSpec((1, QUERY_TILE, 1), lambda h, b, lo, hi: (h, b, 0)),
            pl.BlockSpec((QUERY_TILE, 1), lambda h, b, lo, hi: (b, 0)),
            pl.BlockSpec((1, tokens), whole),
            pl.BlockSpec((QUERY_TILE, HS), tile),
            pl.BlockSpec((tokens, HS), lambda h, b, lo, hi: (0, count + h)),
            pl.BlockSpec((tokens, HS), whole),
            pl.BlockSpec((tokens, HS), whole),
            pl.BlockSpec((2, HS), whole),
        ],
        [
            pl.BlockSpec((QUERY_TILE, HS), tile),
            pl.BlockSpec((tokens, HS), column),
            pl.BlockSpec((tokens, HS), column),
            pl.BlockSpec((2, HS), whole),
        ],
        [shape((tokens, count * HS), BF)] * 3 + [shape((2, HS), F32)],
        scratch=[pltpu.VMEM((tokens, HS), F32), pltpu.VMEM((tokens, HS), F32)],
        flops=10 * count * tokens * tokens * HS // 2,
        moved=24 * tokens * columns,
        prefetch=2,
        name="attend_back",
    )(
        low, high, heads, heads, heads, grad_mixed, mixed, sums, segment[:, None],
        segment[None, :], raw, raw, cosine, sine, gains,
    )


def dispatch_body(slot_ref, x_ref, out_ref):
    local, capacity = out_ref.shape[1], out_ref.shape[3]
    tokens = x_ref.shape[1]
    rows = x_ref[0]
    order = lax.broadcasted_iota(jnp.int32, (capacity, tokens), 0)
    for index in range(local):
        hot = jnp.where(order == slot_ref[0, 0, index : index + 1, :], 1.0, 0.0).astype(BF)
        out_ref[0, index, 0] = dot(hot, rows).astype(BF)


def dispatch(slots, rows, capacity):
    groups, targets, local, tokens = slots.shape
    features = rows.shape[2]
    return call(
        dispatch_body,
        (groups, targets),
        [
            pl.BlockSpec((1, 1, local, tokens), lambda g, d: (g, d, 0, 0)),
            pl.BlockSpec((1, tokens, features), lambda g, d: (g, 0, 0)),
        ],
        pl.BlockSpec((1, local, 1, capacity, features), lambda g, d: (d, 0, g, 0, 0)),
        shape((targets, local, groups, capacity, features), BF),
        flops=2 * groups * targets * local * capacity * tokens * features,
        moved=2 * groups * features * (tokens + targets * local * capacity),
        name="dispatch",
    )(slots, rows)


def combine_body(slot_ref, rows_ref, out_ref):
    targets, local, _, capacity, features = rows_ref.shape
    tile = out_ref.shape[1]
    order = lax.broadcasted_iota(jnp.int32, (tile, capacity), 1)
    slots = slot_ref[0]
    total = jnp.zeros((tile, features), F32)
    for target in range(targets):
        hot = jnp.concatenate(
            [
                jnp.where(
                    order == slots[:, target * local + i : target * local + i + 1], 1.0, 0.0
                ).astype(BF)
                for i in range(local)
            ],
            axis=1,
        )
        total = total + dot(hot, rows_ref[target].reshape(local * capacity, features))
    out_ref[0] = total.astype(BF)


def combine(slots_by_token, rows):
    groups, tokens, experts = slots_by_token.shape
    targets, local, _, capacity, features = rows.shape
    tile = 512
    return call(
        combine_body,
        (groups, tokens // tile),
        [
            pl.BlockSpec((1, tile, experts), lambda g, t: (g, t, 0)),
            pl.BlockSpec((targets, local, 1, capacity, features), lambda g, t: (0, 0, g, 0, 0)),
        ],
        pl.BlockSpec((1, tile, features), lambda g, t: (g, t, 0)),
        shape((groups, tokens, features), BF),
        flops=2 * groups * targets * local * capacity * tokens * features,
        moved=2 * groups * features * (tokens + targets * local * capacity),
        name="combine",
    )(slots_by_token, rows)


def block_rows(ref, row=0):
    _, cores, _, groups, capacity, features = ref.shape
    return ref[row].reshape(cores * groups * capacity, features)


def gate_up_body(*refs):
    x_refs, (gate_w, up_w, gate_ref, up_ref, act_ref) = refs[:CHUNKS], refs[CHUNKS:]
    width = x_refs[0].shape[-1]
    gate = up = None
    for row in range(x_refs[0].shape[0]):
        for chunk, x_ref in enumerate(x_refs):
            x = block_rows(x_ref, row)
            features = pl.ds((row * CHUNKS + chunk) * width, width)
            gate_part = dot(x, gate_w[0, features, :])
            up_part = dot(x, up_w[0, features, :])
            gate = gate_part if gate is None else gate + gate_part
            up = up_part if up is None else up + up_part
    gate_ref[0] = gate.astype(BF)
    up_ref[0] = up.astype(BF)
    act_ref[0] = (gate / (1.0 + jnp.exp(-gate)) * up).astype(BF)


def gate_up(chunks, gate_weight, up_weight):
    rows, cores, local, groups, capacity, width = chunks[0].shape
    _, features, hidden = gate_weight.shape
    slots = groups * capacity
    tile = min(512, hidden)
    out = shape((local, cores * slots, hidden), BF)
    out_spec = pl.BlockSpec((1, slots, tile), lambda i, n, k: (i, k, n))
    w_spec = pl.BlockSpec((1, features, tile), lambda i, n, k: (i, 0, n))
    return call(
        gate_up_body,
        (local, hidden // tile, cores),
        [
            pl.BlockSpec((rows, 1, 1, groups, capacity, width), lambda i, n, k: (0, k, i, 0, 0, 0))
        ]
        * CHUNKS
        + [w_spec, w_spec],
        [out_spec] * 3,
        [out] * 3,
        flops=4 * local * cores * slots * features * hidden,
        moved=local * (8 * features * hidden + 4 * cores * slots * features),
        name="gate_up",
    )(*chunks, gate_weight, up_weight)


def produce_body(*refs):
    act_ref, w_ref, prob_ref = refs[:3]
    c_refs, out_refs, inner_ref = refs[3 : 3 + CHUNKS], refs[3 + CHUNKS : -1], refs[-1]
    width = c_refs[0].shape[-1]

    @pl.when(pl.program_id(2) == 0)
    def _():
        inner_ref[...] = jnp.zeros_like(inner_ref)

    act, prob = act_ref[0], prob_ref[0]
    inner = jnp.zeros(prob.shape, F32)
    for chunk in range(CHUNKS):
        made = dot(act, w_ref[0, pl.ds(chunk * width, width), :], 1, 1)
        inner += jnp.sum(made * block_rows(c_refs[chunk]).astype(F32), axis=1, keepdims=True)
        out_refs[chunk][...] = (made * prob).astype(BF).reshape(out_refs[chunk].shape)
    inner_ref[0] += inner


def produce(activated, down_weight, prob, cots):
    rows, cores, local, groups, capacity, width = cots[0].shape
    hidden = activated.shape[2]
    slots = groups * capacity
    row_spec = pl.BlockSpec((1, 1, 1, groups, capacity, width), lambda i, k, r: (r, k, i, 0, 0, 0))
    column = pl.BlockSpec((1, slots, 1), lambda i, k, r: (i, k, 0))
    outs = call(
        produce_body,
        (local, cores, rows),
        [
            pl.BlockSpec((1, slots, hidden), lambda i, k, r: (i, k, 0)),
            pl.BlockSpec((1, width * CHUNKS, hidden), lambda i, k, r: (i, r, 0)),
            column,
        ]
        + [row_spec] * CHUNKS,
        [row_spec] * CHUNKS + [column],
        [shape(cots[0].shape, BF)] * CHUNKS + [shape((local, cores * slots, 1), F32)],
        flops=2 * local * cores * slots * D * hidden,
        moved=local * (2 * D * hidden + 8 * cores * slots * D),
        name="produce",
    )(activated, down_weight, prob, *cots)
    return outs[:CHUNKS], outs[CHUNKS]


def act_back_body(*refs):
    c_refs = refs[:CHUNKS]
    w_ref, prob_ref, gate_ref, up_ref, gate_out, up_out = refs[CHUNKS:]
    width = c_refs[0].shape[-1]
    prob = prob_ref[0]
    grad = None
    for row in range(c_refs[0].shape[0]):
        for chunk, c_ref in enumerate(c_refs):
            c = (block_rows(c_ref, row).astype(F32) * prob).astype(BF)
            part = dot(c, w_ref[0, pl.ds((row * CHUNKS + chunk) * width, width), :])
            grad = part if grad is None else grad + part
    gate, up = gate_ref[0].astype(F32), up_ref[0].astype(F32)
    squashed = 1.0 / (1.0 + jnp.exp(-gate))
    gate_out[0] = (grad * up * squashed * (1.0 + gate * (1.0 - squashed))).astype(BF)
    up_out[0] = (grad * gate * squashed).astype(BF)


def act_back(cots, down_weight, prob, gate, up):
    rows, cores, local, groups, capacity, width = cots[0].shape
    _, features, hidden = down_weight.shape
    slots = groups * capacity
    tile = min(512, hidden)
    spec = pl.BlockSpec((1, slots, tile), lambda i, n, k: (i, k, n))
    return call(
        act_back_body,
        (local, hidden // tile, cores),
        [
            pl.BlockSpec((rows, 1, 1, groups, capacity, width), lambda i, n, k: (0, k, i, 0, 0, 0))
        ]
        * CHUNKS
        + [
            pl.BlockSpec((1, features, tile), lambda i, n, k: (i, 0, n)),
            pl.BlockSpec((1, slots, 1), lambda i, n, k: (i, k, 0)),
            spec,
            spec,
        ],
        [spec] * 2,
        [shape(gate.shape, BF)] * 2,
        flops=2 * local * cores * slots * features * hidden,
        moved=local * (2 * features * hidden + 2 * cores * slots * features),
        name="act_back",
    )(*cots, down_weight, prob, gate, up)


def down_grad_body(*refs):
    c_refs, (prob_ref, act_ref, out_ref) = refs[:CHUNKS], refs[CHUNKS:]
    width = c_refs[0].shape[-1]
    for chunk, c_ref in enumerate(c_refs):
        c = (block_rows(c_ref).astype(F32) * prob_ref[0]).astype(BF)
        out_ref[0, pl.ds(chunk * width, width), :] = dot(c, act_ref[0], 0, 0)


def down_grad(cots, prob, activated):
    rows, cores, local, groups, capacity, width = cots[0].shape
    slots, hidden = activated.shape[1:]
    return call(
        down_grad_body,
        (local, rows),
        [
            pl.BlockSpec((1, cores, 1, groups, capacity, width), lambda i, r: (r, 0, i, 0, 0, 0))
        ]
        * CHUNKS
        + [
            pl.BlockSpec((1, slots, 1), lambda i, r: (i, 0, 0)),
            pl.BlockSpec((1, slots, hidden), lambda i, r: (i, 0, 0)),
        ],
        pl.BlockSpec((1, width * CHUNKS, hidden), lambda i, r: (i, r, 0)),
        shape((local, rows * width * CHUNKS, hidden), F32),
        flops=2 * local * slots * D * hidden,
        moved=local * (4 * D * hidden + 2 * slots * D),
        name="down_grad",
    )(*cots, prob, activated)


def gate_grad_body(*refs):
    x_refs, (gate_ref, up_ref, gate_out, up_out) = refs[:CHUNKS], refs[CHUNKS:]
    width = x_refs[0].shape[-1]
    for chunk, x_ref in enumerate(x_refs):
        x = block_rows(x_ref)
        features = pl.ds(chunk * width, width)
        gate_out[0, features, :] = dot(x, gate_ref[0], 0, 0)
        up_out[0, features, :] = dot(x, up_ref[0], 0, 0)


def gate_grad(chunks, grad_gate_pre, grad_up_pre):
    rows, cores, local, groups, capacity, width = chunks[0].shape
    slots, hidden = grad_gate_pre.shape[1:]
    wide = pl.BlockSpec((1, slots, hidden), lambda i, r: (i, 0, 0))
    out = pl.BlockSpec((1, width * CHUNKS, hidden), lambda i, r: (i, r, 0))
    return call(
        gate_grad_body,
        (local, rows),
        [
            pl.BlockSpec((1, cores, 1, groups, capacity, width), lambda i, r: (r, 0, i, 0, 0, 0))
        ]
        * CHUNKS
        + [wide, wide],
        [out, out],
        [shape((local, rows * width * CHUNKS, hidden), F32)] * 2,
        flops=4 * local * slots * D * hidden,
        moved=local * (8 * D * hidden + 2 * slots * D),
        name="gate_grad",
    )(*chunks, grad_gate_pre, grad_up_pre)


def rows_back_body(gate_ref, up_ref, gate_w, up_w, out_ref):
    made = dot(gate_ref[0], gate_w[0], 1, 1) + dot(up_ref[0], up_w[0], 1, 1)
    out_ref[...] = made.astype(BF).reshape(out_ref.shape)


def rows_back(grad_gate_pre, grad_up_pre, gate_weight, up_weight, chunk, dims):
    rows, cores, local, groups, capacity, width = dims
    hidden = gate_weight.shape[2]
    slots = groups * capacity
    pre = pl.BlockSpec((1, slots, hidden), lambda i, k, r: (i, k, 0))
    weight = pl.BlockSpec((1, width, hidden), lambda i, k, r: (i, r * CHUNKS + chunk, 0))
    return call(
        rows_back_body,
        (local, cores, rows),
        [pre, pre, weight, weight],
        pl.BlockSpec((1, 1, 1, groups, capacity, width), lambda i, k, r: (r, k, i, 0, 0, 0)),
        shape(dims, BF),
        flops=4 * local * cores * slots * width * rows * hidden,
        moved=local * (4 * rows * width * hidden + 6 * cores * slots * width * rows),
        name="rows_back",
    )(grad_gate_pre, grad_up_pre, gate_weight, up_weight)


def swap(rows):
    return lax.all_to_all(rows, SWAP_AXES, split_axis=0, concat_axis=0, tiled=True)


def slot_positions(routes, ranks, capacity):
    experts = jnp.arange(E, dtype=jnp.int32)
    member = jnp.any(routes.T[:, None, :] == experts[None, :, None], axis=0)
    earlier = (ranks[:, None] < ranks[None, :]).astype(BF)
    position = jnp.dot(member.astype(BF), earlier, preferred_element_type=F32)
    return jnp.where(member & (position < capacity), position, -1.0)


def per_device(
    hidden_in,
    attention_gain,
    query_weight,
    key_weight,
    value_weight,
    projection,
    query_gain,
    key_gain,
    feedforward_gain,
    router_weight,
    gate_weight,
    up_weight,
    down_weight,
    segments,
    routes,
    priority,
    cotangent,
):
    tokens, width_here = hidden_in.shape
    row_count = lax.axis_size("row")
    z_count = lax.axis_size("z")
    core_count = lax.axis_size("core")
    local = gate_weight.shape[0]
    piece_count = row_count * z_count * core_count * local
    pieces = max(1, piece_count // E)
    capacity = tokens * TOPK // E
    width = width_here // CHUNKS
    row_index = lax.axis_index("row")
    z_index = lax.axis_index("z")
    core_index = lax.axis_index("core")
    offset = row_index * width_here
    head_columns = query_weight.shape[1]
    head_count = head_columns // HS

    hidden_full = lax.all_gather(hidden_in, "row", axis=1, tiled=True)
    gain_full = lax.all_gather(attention_gain, "row", axis=0, tiled=True)
    qkv_full = lax.all_gather(
        jnp.concatenate([query_weight, key_weight, value_weight], axis=1),
        TOKENS_AXES,
        axis=0,
        tiled=True,
    )
    projection_full = lax.all_gather(projection, TOKENS_AXES, axis=0, tiled=True)
    router_full = lax.all_gather(
        lax.all_gather(router_weight.T, TOKENS_AXES, axis=1, tiled=True), "row", axis=0, tiled=True
    )
    router_here = lax.dynamic_slice_in_dim(router_full, offset, width_here, 1)

    position = slot_positions(routes, priority[0], capacity)
    by_group = lax.all_gather(position.astype(BF), "z", axis=0)
    by_piece = jnp.repeat(by_group, pieces, axis=1).reshape(
        z_count, row_count, z_count, core_count * local, tokens
    )
    mine = lax.dynamic_index_in_dim(by_piece, z_index, 2, keepdims=False).astype(jnp.int32)
    slots = mine.reshape(z_count, row_count * core_count, local, tokens)
    slots_by_token = jnp.swapaxes(
        mine.reshape(z_count, row_count * core_count * local, tokens), 1, 2
    )
    dims = (row_count, core_count, local, z_count, capacity, width)

    def send(values):
        received = []
        for chunk in range(CHUNKS):
            part = values[:, chunk * width : (chunk + 1) * width]
            spread = lax.all_gather(part, "z", axis=0)
            received.append(swap(dispatch(slots, spread, capacity)).reshape(dims))
        return received

    def gather_back(chunks):
        parts = []
        for chunk in chunks:
            summed = combine(
                slots_by_token, swap(chunk.reshape((row_count * core_count,) + dims[2:]))
            )
            parts.append(
                lax.psum_scatter(summed, "z", scatter_dimension=0, tiled=True).reshape(
                    tokens, width
                )
            )
        return jnp.concatenate(parts, axis=1).astype(F32)

    cots = send(cotangent)

    cosine, sine = rotary_tables()
    first_gain = attention_gain.astype(F32)
    second_gain = feedforward_gain.astype(F32)
    head_gains = jnp.stack([query_gain, key_gain]).astype(F32)
    residual = hidden_in.astype(F32)
    gain_row = gain_full.astype(F32)[None, :]
    normed_one, heads, raw = project(
        hidden_full,
        gain_row,
        qkv_full,
        cosine,
        sine,
        jnp.repeat(head_gains, head_count, axis=0).reshape(1, -1),
    )
    segment = segments[0]
    low, high = key_ranges(segment)
    mixed, sums = attend(heads, segment, low, high)
    branch = lax.psum_scatter(
        dot(mixed, projection_full, 1, 1).astype(BF), "row", scatter_dimension=1, tiled=True
    )
    middle = residual + branch.astype(F32)
    second_factor = lax.rsqrt(lax.psum(jnp.sum(middle * middle, axis=1), "row") / D + EPSILON)[
        :, None
    ]
    normed_two = (middle * second_factor * second_gain).astype(BF)

    logits = jnp.sum(lax.all_gather(dot(router_here, normed_two, 1, 1), "row", axis=0), axis=0)
    raised = jnp.exp(logits)
    router_probs = raised / jnp.sum(raised, axis=0, keepdims=True)

    rows = send(normed_two)
    experts_here = E // row_count
    own_slots = lax.dynamic_slice_in_dim(position, row_index * experts_here, experts_here, 0)
    own_probs = lax.dynamic_slice_in_dim(router_probs, row_index * experts_here, experts_here, 0)
    order = jnp.arange(capacity, dtype=jnp.int32).astype(F32)
    slot_prob = jnp.sum(
        jnp.where(own_slots[:, None, :] == order[None, :, None], own_probs[:, None, :], 0.0), axis=2
    )
    prob_groups = jnp.repeat(
        lax.all_gather(slot_prob, TOKENS_AXES, axis=0), pieces, axis=1
    ).reshape(z_count, core_count, z_count, core_count, local, capacity)
    prob_here = lax.dynamic_index_in_dim(
        lax.dynamic_index_in_dim(prob_groups, z_index, 2, keepdims=False),
        core_index,
        2,
        keepdims=False,
    )
    prob = jnp.transpose(prob_here, (2, 1, 0, 3)).reshape(
        local, core_count * z_count * capacity, 1
    )
    gate, up, activated = gate_up(rows, gate_weight, up_weight)
    grad_gate_pre, grad_up_pre = act_back(cots, down_weight, prob, gate, up)
    grad_rows = [
        rows_back(grad_gate_pre, grad_up_pre, gate_weight, up_weight, chunk, dims)
        for chunk in range(CHUNKS)
    ]
    grad_normed_two = gather_back(grad_rows)
    produced, inner = produce(activated, down_weight, prob, cots)
    grad_down = down_grad(cots, prob, activated)
    grad_gate, grad_up = gate_grad(rows, grad_gate_pre, grad_up_pre)
    output = (middle + gather_back(produced)).astype(BF)

    every = lax.all_gather(
        inner.reshape(local, core_count, z_count, capacity), ALL_AXES, axis=0
    )
    of_group = lax.dynamic_index_in_dim(
        lax.dynamic_index_in_dim(every, core_index, 2, keepdims=False), z_index, 2, keepdims=False
    )
    slot_grads = jnp.sum(of_group.reshape(E, pieces, capacity), axis=1)
    grad_prob = jnp.sum(
        jnp.where(position[:, None, :] == order[None, :, None], slot_grads[:, :, None], 0.0), axis=1
    )
    grad_logits = (
        router_probs * (grad_prob - jnp.sum(router_probs * grad_prob, axis=0, keepdims=True))
    ).astype(BF)
    grad_normed_two = grad_normed_two + dot(grad_logits, router_here, 0, 0)
    router_part = dot(grad_logits, normed_two)
    router_swapped = lax.all_to_all(
        router_part.reshape(row_count, experts_here, width_here), "row", 0, 0, tiled=True
    )
    grad_router = lax.psum_scatter(
        jnp.swapaxes(router_swapped, 0, 1).reshape(experts_here, D),
        TOKENS_AXES,
        scatter_dimension=1,
        tiled=True,
    ).T

    scaled_two = grad_normed_two * second_gain
    second_inner = lax.psum(jnp.sum(scaled_two * middle, axis=1), "row")[:, None]
    grad_middle = (
        cotangent.astype(F32)
        + scaled_two * second_factor
        - middle * second_factor**3 * second_inner / D
    )
    grad_feedforward_gain = jnp.sum(grad_normed_two * middle * second_factor, axis=0)

    grad_branch = lax.all_gather(grad_middle.astype(BF), "row", axis=1, tiled=True)
    grad_mixed = dot(grad_branch, projection_full).astype(BF)
    grad_projection = dot(grad_branch, mixed, 0, 0).astype(BF)
    grad_query_raw, grad_key_raw, grad_value_raw, head_gain_grads = attend_back(
        heads, grad_mixed, mixed, sums, segment, low, high, raw, cosine, sine, head_gains
    )
    grad_raw = jnp.concatenate([grad_query_raw, grad_key_raw, grad_value_raw], axis=1)
    first_part = dot(grad_raw, qkv_full, 1, 1)
    first_inner = lax.psum(
        jnp.sum(first_part * gain_row * hidden_full.astype(F32), axis=1), "row"
    )[:, None]
    grad_first = lax.psum_scatter(
        first_part.astype(BF), "row", scatter_dimension=1, tiled=True
    ).astype(F32)
    grad_qkv = dot(normed_one, grad_raw, 0, 0).astype(BF)
    first_factor = lax.rsqrt(
        jnp.mean(jnp.square(hidden_full.astype(F32)), axis=1, keepdims=True) + EPSILON
    )
    scaled_one = grad_first * first_gain
    grad_input = (
        grad_middle + scaled_one * first_factor - residual * first_factor**3 * first_inner / D
    )
    grad_attention_gain = jnp.sum(grad_first * residual * first_factor, axis=0)

    padded_first = lax.dynamic_update_slice(jnp.zeros((D,), F32), grad_attention_gain, (offset,))
    padded_second = lax.dynamic_update_slice(jnp.zeros((D,), F32), grad_feedforward_gain, (offset,))
    totals = lax.psum((padded_first, padded_second, head_gain_grads), ALL_AXES)
    grad_projection = lax.psum_scatter(
        grad_projection, TOKENS_AXES, scatter_dimension=0, tiled=True
    ).astype(F32)
    grad_qkv = lax.psum_scatter(grad_qkv, TOKENS_AXES, scatter_dimension=0, tiled=True).astype(F32)
    return (
        output,
        grad_input,
        lax.dynamic_slice_in_dim(totals[0], offset, width_here),
        grad_qkv[:, :head_columns],
        grad_qkv[:, head_columns : 2 * head_columns],
        grad_qkv[:, 2 * head_columns :],
        grad_projection,
        totals[2][0],
        totals[2][1],
        lax.dynamic_slice_in_dim(totals[1], offset, width_here),
        grad_router,
        grad_gate,
        grad_up,
        grad_down,
    )


def solution(mesh):
    rows, columns = mesh.shape["row"], mesh.shape["col"]
    split_mesh = Mesh(
        mesh.devices.reshape(rows, columns // 2, 2), ("row", "z", "core")
    )
    both = P(TOKENS_AXES, "row")
    expert = P(ALL_AXES, None, None)
    grouped = P(TOKENS_AXES, None)
    return jax.shard_map(
        per_device,
        mesh=split_mesh,
        in_specs=(
            both, P("row"), both, both, both, both, P(), P(), P("row"), both,
            expert, expert, expert, grouped, grouped, grouped, both,
        ),
        out_specs=(
            both, both, P("row"), both, both, both, both, P(), P(), P("row"), both,
            expert, expert, expert,
        ),
        check_vma=False,
    )
```

time: 3650 us -> 1980 us (0.54)
  waiting for transfers between devices: 2020 us -> 745 us
  Pallas kernels: 0 us -> 628 us
  matrix products: 591 us -> 81.6 us
  local copies, waits for them, and re-layouts: 468 us -> 33.7 us
  other arithmetic: 394 us -> 59.3 us
  blocking collectives: 112 us -> 347 us
    all_to_all x4 -> x8, waiting for transfers between devices: 1140 us -> 266 us  [the longest x7 266 us: swap(): lax.all_to_all(rows, SWAP_AXES, split_axis=0, concat_axis=0, tiled=True)]
    pallas_call x0 -> x18, Pallas kernels: none -> 628 us  [the longest x4 124 us: combine(): call(combine_body, (groups, tokens // tile), [pl.BlockSpec((1, tile, expe...]
    dot_general x52 -> x9, matrix products: 591 us -> 81.6 us  [the longest x8 77.7 us: dot(): lax.dot_general(left, right, (((left_dim,), (right_dim,)), ((), ())), pre...]
    reduce_scatter x9, waiting for transfers between devices: 574 us -> 130 us  [the longest x1 86.6 us: per_device(): lax.psum_scatter(dot(mixed, projection_full, 1, 1).astype(BF), 'row', sca...]
    unnamed x159 -> x89, local copies, waits for them, and re-layouts: 248 us -> 11.4 us
    all_gather x1 -> x5, blocking collectives: 14.2 us -> 167 us  [the longest x1 82.7 us: per_device(): lax.all_gather(lax.all_gather(router_weight.T, TOKENS_AXES, axis=1, tiled...]
    scatter-add x2 -> x0, other arithmetic: 123 us -> none  [the longest x1 63.9 us: per_device(): jnp.zeros((tokens, D), jnp.float32).at[slot_table.reshape(-1)]]
    gather x6 -> x0, local copies, waits for them, and re-layouts: 115 us -> none  [the longest x1 35.8 us: per_device(): dispatched = normed_two[slot_table] * fill_rows.astype(jnp.bfloat16)]
  transfers between devices with their start and end apart: 21 -> 27, of which waited for: 18 -> 14; matrix products, arithmetic and copies ran while one was open for 23% -> 7% of each run, Pallas kernels for 0% -> 29%
where the time goes in v1:
time: 1980 us; the launch traced here: 1960 us
  waiting for transfers between devices  745 us (38%)
  Pallas kernels  628 us (32%)
  blocking collectives  347 us (18%)
  matrix products  81.6 us (4%)
  other arithmetic  59.3 us (3%)
  starting transfers between devices  53 us (3%)
  local copies, waits for them, and re-layouts  33.7 us (2%)
    all_to_all x7, waiting for transfers between devices, swap(): lax.all_to_all(rows, SWAP_AXES, split_axis=0, concat_axis=0, tiled=True)  266 us
    all_gather x4, waiting for transfers between devices, send(): spread = lax.all_gather(part, 'z', axis=0)  130 us
    pallas_call x4, Pallas kernels, combine(): call(combine_body, (groups, tokens // tile), [pl.BlockSpec((1, tile, expe...  124 us
    all_to_all x1, blocking collectives, swap(): lax.all_to_all(rows, SWAP_AXES, split_axis=0, concat_axis=0, tiled=True)  113 us
    pallas_call x4, Pallas kernels, dispatch(): call(dispatch_body, (groups, targets), [pl.BlockSpec((1, 1, local, tokens...  110 us
    all_gather x1, waiting for transfers between devices, per_device(): hidden_full = lax.all_gather(hidden_in, 'row', axis=1, tiled=True)  87.8 us
    reduce_scatter x1, waiting for transfers between devices, per_device(): lax.psum_scatter(dot(mixed, projection_full, 1, 1).astype(BF), 'row', sca...  86.6 us
    all_gather x1, waiting for transfers between devices, per_device(): lax.all_gather(grad_middle.astype(BF), 'row', axis=1, tiled=True)  85.5 us
  transfers between devices with their start and end apart: 27, of which 14 were waited for; matrix products, arithmetic and copies ran while one was open for 7% of the time, Pallas kernels for 29%

profile of v1, /device:TPU:0, one launch (start us, length us, event | category | flops | bytes accessed | tf_op | source)
XLA Modules:
  0.0 1963.8 jit_solution(15857637592537778948)
XLA Ops:
  34.3 43.4 %all-gather.21.cloned.1.call-done.w_ref = bf16[2048,1536]{1,0:T(8,128)(2,1)} async-done(((bf16[256,1536]{1,0:T(8,128)(2,1)}), bf16[2048,1536]{1,0:T(8,128)(2,1)}) %all-gather.21.cloned.1.call-update) | async-done | bytes 6291472 | tf_op jit(solution)/shard_map/all_gather | solution.py:617
  77.7 87.8 %all-gather.19.cloned.1.call-done.x_ref = bf16[2048,2048]{1,0:T(8,128)(2,1)} async-done(((bf16[2048,512]{1,0:T(8,128)(2,1)}), bf16[2048,2048]{1,0:T(8,128)(2,1)}) %all-gather.19.cloned.1.call-update) | async-done | bytes 8388624 | tf_op jit(solution)/shard_map/all_gather | solution.py:615
  187.9 45.9 %attend.1 = (bf16[2048,512]{1,0:T(8,128)(2,1)}, f32[4,2048,1]{2,1,0:T(8,128)}) custom-call(s32[8]{0:T(128)} %get-tuple-element.57.low, s32[8]{0:T(128)} %get-tuple-element.56.high, bf16[2048,1536]{1,0:T(8,128)(2,1)} %get-tuple-element.33.q_ref.k_ref.v_ref, bf16[2048,1536]{1,0:T(8,128)(2,1)} %get-tuple-element.33.q_ref.k_ref.v_ref, ...), custom_call_target="tpu_custom_call" | custom-call | flops 4294967296 | bytes 25165824 | tf_op jit(solution)/shard_map/attend/pallas_call | solution.py:160
  251.2 86.6 %reduce-scatter.10.cloned.1.call-done = bf16[2048,512]{1,0:T(8,128)(2,1)} async-done(((bf16[2048,2048]{1,0:T(8,128)(2,1)}), bf16[2048,512]{1,0:T(8,128)(2,1)}) %reduce-scatter.10.cloned.1.call-update) | async-done | bytes 2097168 | tf_op jit(solution)/shard_map/reduce_scatter | solution.py:681
  355.0 65.0 %all-gather.35.cloned.1.call-done = bf16[8192,256]{1,0:T(8,128)(2,1)} async-done(((bf16[2048,256]{1,0:T(8,128)(2,1)}), bf16[8192,256]{1,0:T(8,128)(2,1)}) %all-gather.35.cloned.1.call-update) | async-done | bytes 4194320 | tf_op jit(solution)/shard_map/all_gather | solution.py:645
  419.9 27.6 %dispatch.6 = bf16[8,2,4,256,256]{4,3,2,1,0:T(8,128)(2,1)} custom-call(s32[4,8,2,2048]{3,2,1,0:T(2,128)} %copy.84.slot_ref, bf16[4,2048,256]{2,1,0:T(8,128)(2,1)} %bitcast.83), custom_call_target="tpu_custom_call" | custom-call | flops 17179869184 | bytes 12582912 | tf_op jit(solution)/shard_map/dispatch/pallas_call | solution.py:298
  453.2 47.5 %all-gather.31.cloned.1.call-done = bf16[8192,256]{1,0:T(8,128)(2,1)} async-done(((bf16[2048,256]{1,0:T(8,128)(2,1)}), bf16[8192,256]{1,0:T(8,128)(2,1)}) %all-gather.31.cloned.1.call-update) | async-done | bytes 4194320 | tf_op jit(solution)/shard_map/all_gather | solution.py:645
  500.8 27.6 %dispatch.5 = bf16[8,2,4,256,256]{4,3,2,1,0:T(8,128)(2,1)} custom-call(s32[4,8,2,2048]{3,2,1,0:T(2,128)} %copy.84.slot_ref, bf16[4,2048,256]{2,1,0:T(8,128)(2,1)} %bitcast.86), custom_call_target="tpu_custom_call" | custom-call | flops 17179869184 | bytes 12582912 | tf_op jit(solution)/shard_map/dispatch/pallas_call | solution.py:298
  581.7 27.6 %dispatch.4 = bf16[8,2,4,256,256]{4,3,2,1,0:T(8,128)(2,1)} custom-call(s32[4,8,2,2048]{3,2,1,0:T(2,128)} %copy.84.slot_ref, bf16[4,2048,256]{2,1,0:T(8,128)(2,1)} %bitcast.85), custom_call_target="tpu_custom_call" | custom-call | flops 17179869184 | bytes 12582912 | tf_op jit(solution)/shard_map/dispatch/pallas_call | solution.py:298
  609.3 36.3 %all-to-all-done.1 = bf16[8,2,4,256,256]{4,3,2,1,0:T(8,128)(2,1)} async-done(((bf16[8,2,4,256,256]{4,3,2,1,0:T(8,128)(2,1)}), bf16[8,2,4,256,256]{4,3,2,1,0:T(8,128)(2,1)}, u32[]{:S(2)}, u32[]{:S(2)}) %all-to-all-start.1) | async-done | bytes 8388640 | tf_op jit(solution)/shard_map/all_to_all | solution.py:569
  665.3 82.7 %all_gather.77 = bf16[64,2048]{1,0:T(8,128)(2,1)S(1)} all-gather(bf16[16,2048]{1,0:T(8,128)(2,1)S(1)} %all_gather.76), channel_id=1, replica_groups=mesh['row'=4,'z'=4,'core'=2] {'row'}, dimensions={0}, use_global_device_ids=true | all-gather | bytes 327680 | tf_op jit(solution)/shard_map/all_gather | solution.py:624
  750.3 27.5 %dispatch.7 = bf16[8,2,4,256,256]{4,3,2,1,0:T(8,128)(2,1)} custom-call(s32[4,8,2,2048]{3,2,1,0:T(2,128)} %copy.84.slot_ref, bf16[4,2048,256]{2,1,0:T(8,128)(2,1)} %bitcast.84), custom_call_target="tpu_custom_call" | custom-call | flops 17179869184 | bytes 12582912 | tf_op jit(solution)/shard_map/dispatch/pallas_call | solution.py:298
  807.3 45.5 %gate_up.1 = (bf16[2,2048,1024]{2,1,0:T(8,128)(2,1)}, bf16[2,2048,1024]{2,1,0:T(8,128)(2,1)}, bf16[2,2048,1024]{2,1,0:T(8,128)(2,1)}) custom-call(bf16[4,2,2,4,256,256]{5,4,3,2,1,0:T(8,128)(2,1)} %bitcast.12.refs_0_, bf16[4,2,2,4,256,256]{5,4,3,2,1,0:T(8,128)(2,1)} %bitcast.14.refs_1_, bf16[2,2048,1024]{2,1,0:T(8,128)(2,1)} %gate_w.3, ...), custom_call_target="tpu_custom_call" | custom-call | flops 34359738368 | bytes 67108864 | tf_op jit(solution)/shard_map/gate_up/pallas_call | solution.py:382
  876.8 34.8 %act_back.1 = (bf16[2,2048,1024]{2,1,0:T(8,128)(2,1)}, bf16[2,2048,1024]{2,1,0:T(8,128)(2,1)}) custom-call(bf16[4,2,2,4,256,256]{5,4,3,2,1,0:T(8,128)(2,1)} %bitcast.20.refs_3_.refs_0_, bf16[4,2,2,4,256,256]{5,4,3,2,1,0:T(8,128)(2,1)} %bitcast.22.refs_4_.refs_1_, bf16[2,2048,1024]{2,1,0:T(8,128)(2,1)} %refs_2_.3, f32[2,2048,1]{2,1,0:T(8,128)} %reshape.171.refs_2_.refs_3_, ...), custom_call_target="tpu_custom_call" | custom-call | flops 17179869184 | bytes 25165824 | tf_op jit(solution)/shard_map/act_back/pallas_call | solution.py:463
  911.6 29.1 %rows_back.2 = bf16[4,2,2,4,256,256]{5,4,3,2,1,0:T(8,128)(2,1)} custom-call(bf16[2,2048,1024]{2,1,0:T(8,128)(2,1)} %get-tuple-element.40.gate_ref.refs_2_, bf16[2,2048,1024]{2,1,0:T(8,128)(2,1)} %get-tuple-element.41.up_ref.refs_3_, bf16[2,2048,1024]{2,1,0:T(8,128)(2,1)} %gate_w.3, bf16[2,2048,1024]{2,1,0:T(8,128)(2,1)} %up_w.3), custom_call_target="tpu_custom_call" | custom-call | flops 17179869184 | bytes 33554432 | tf_op jit(solution)/shard_map/rows_back/pallas_call | solution.py:556
  948.5 29.1 %rows_back.3 = bf16[4,2,2,4,256,256]{5,4,3,2,1,0:T(8,128)(2,1)} custom-call(bf16[2,2048,1024]{2,1,0:T(8,128)(2,1)} %get-tuple-element.40.gate_ref.refs_2_, bf16[2,2048,1024]{2,1,0:T(8,128)(2,1)} %get-tuple-element.41.up_ref.refs_3_, bf16[2,2048,1024]{2,1,0:T(8,128)(2,1)} %gate_w.3, bf16[2,2048,1024]{2,1,0:T(8,128)(2,1)} %up_w.3), custom_call_target="tpu_custom_call" | custom-call | flops 17179869184 | bytes 33554432 | tf_op jit(solution)/shard_map/rows_back/pallas_call | solution.py:556
  977.6 62.3 %all-to-all-done.6.rows_ref = bf16[8,2,4,256,256]{4,3,2,1,0:T(8,128)(2,1)} async-done(((bf16[8,2,4,256,256]{4,3,2,1,0:T(8,128)(2,1)}), bf16[8,2,4,256,256]{4,3,2,1,0:T(8,128)(2,1)}, u32[]{:S(2)}, u32[]{:S(2)}) %all-to-all-start.6) | async-done | bytes 8388640 | tf_op jit(solution)/shard_map/all_to_all | solution.py:569
  1045.3 30.9 %combine.6 = bf16[4,2048,256]{2,1,0:T(8,128)(2,1)} custom-call(s32[4,2048,16]{2,1,0:T(8,128)} %bitcast.64, bf16[8,2,4,256,256]{4,3,2,1,0:T(8,128)(2,1)} %all-to-all-done.6.rows_ref), custom_call_target="tpu_custom_call" | custom-call | flops 17179869184 | bytes 12582912 | tf_op jit(solution)/shard_map/combine/pallas_call | solution.py:337
  1076.3 62.6 %all-to-all-done.7.rows_ref = bf16[8,2,4,256,256]{4,3,2,1,0:T(8,128)(2,1)} async-done(((bf16[8,2,4,256,256]{4,3,2,1,0:T(8,128)(2,1)}), bf16[8,2,4,256,256]{4,3,2,1,0:T(8,128)(2,1)}, u32[]{:S(2)}, u32[]{:S(2)}) %all-to-all-start.7) | async-done | bytes 8388640 | tf_op jit(solution)/shard_map/all_to_all | solution.py:569
  1138.9 30.9 %combine.7 = bf16[4,2048,256]{2,1,0:T(8,128)(2,1)} custom-call(s32[4,2048,16]{2,1,0:T(8,128)} %bitcast.65, bf16[8,2,4,256,256]{4,3,2,1,0:T(8,128)(2,1)} %all-to-all-done.7.rows_ref), custom_call_target="tpu_custom_call" | custom-call | flops 17179869184 | bytes 12582912 | tf_op jit(solution)/shard_map/combine/pallas_call | solution.py:337
  1169.9 33.4 %produce.1 = (bf16[4,2,2,4,256,256]{5,4,3,2,1,0:T(8,128)(2,1)}, bf16[4,2,2,4,256,256]{5,4,3,2,1,0:T(8,128)(2,1)}, f32[2,2048,1]{2,1,0:T(8,128)}) custom-call(bf16[2,2048,1024]{2,1,0:T(8,128)(2,1)} %get-tuple-element.35.refs_0_.refs_3_, bf16[2,2048,1024]{2,1,0:T(8,128)(2,1)} %refs_2_.3, f32[2,2048,1]{2,1,0:T(8,128)} %reshape.171.refs_2_.refs_3_, ...), custom_call_target="tpu_custom_call" | custom-call | flops 17179869184 | bytes 75497472 | tf_op jit(solution)/shard_map/produce/pallas_call | solution.py:422
  1205.7 45.4 %all_gather.86 = f32[32,2,2,4,256]{4,3,2,1,0:T(4,128)S(1)} all-gather(f32[1,2,2,4,256]{4,3,2,1,0:T(4,128)S(1)} %all_gather_reshape.3), channel_id=1, replica_groups=mesh['row'=4,'z'=4,'core'=2] {'row','z','core'}, dimensions={0}, use_global_device_ids=true | all-gather | bytes 540672 | tf_op jit(solution)/shard_map/all_gather | solution.py:726
  1289.9 85.5 %all-gather.25.cloned.1.call-done = bf16[2048,2048]{1,0:T(8,128)(2,1)} async-done(((bf16[2048,512]{1,0:T(8,128)(2,1)}), bf16[2048,2048]{1,0:T(8,128)(2,1)}) %all-gather.25.cloned.1.call-update) | async-done | bytes 8388624 | tf_op jit(solution)/shard_map/all_gather | solution.py:760
  1394.7 81.9 %attend_back.1 = (bf16[2048,512]{1,0:T(8,128)(2,1)}, bf16[2048,512]{1,0:T(8,128)(2,1)}, bf16[2048,512]{1,0:T(8,128)(2,1)}, f32[2,128]{1,0:T(2,128)}) custom-call(s32[8]{0:T(128)} %get-tuple-element.57.low, s32[8]{0:T(128)} %get-tuple-element.56.high, bf16[2048,1536]{1,0:T(8,128)(2,1)} %get-tuple-element.33.q_ref.k_ref.v_ref, ...), custom_call_target="tpu_custom_call" | custom-call | flops 10737418240 | bytes 75497472 | tf_op jit(solution)/shard_map/attend_back/pallas_call | solution.py:249
  1499.8 113.1 %all_to_all.45.rows_ref = bf16[8,2,4,256,256]{4,3,2,1,0:T(8,128)(2,1)} all-to-all(bf16[8,2,4,256,256]{4,3,2,1,0:T(8,128)(2,1)} %bitcast.59), channel_id=1, replica_groups=mesh['row'=4,'z'=4,'core'=2] {'row','core'}, dimensions={0} | all-to-all | bytes 16777216 | tf_op jit(solution)/shard_map/all_to_all | solution.py:569
  1618.0 30.9 %combine.4 = bf16[4,2048,256]{2,1,0:T(8,128)(2,1)} custom-call(s32[4,2048,16]{2,1,0:T(8,128)} %bitcast.66, bf16[8,2,4,256,256]{4,3,2,1,0:T(8,128)(2,1)} %all_to_all.45.rows_ref), custom_call_target="tpu_custom_call" | custom-call | flops 17179869184 | bytes 12582912 | tf_op jit(solution)/shard_map/combine/pallas_call | solution.py:337
  1649.0 62.8 %all-to-all-done.5.rows_ref = bf16[8,2,4,256,256]{4,3,2,1,0:T(8,128)(2,1)} async-done(((bf16[8,2,4,256,256]{4,3,2,1,0:T(8,128)(2,1)}), bf16[8,2,4,256,256]{4,3,2,1,0:T(8,128)(2,1)}, u32[]{:S(2)}, u32[]{:S(2)}) %all-to-all-start.5) | async-done | bytes 8388640 | tf_op jit(solution)/shard_map/all_to_all | solution.py:569
  1711.8 30.9 %combine.5 = bf16[4,2048,256]{2,1,0:T(8,128)(2,1)} custom-call(s32[4,2048,16]{2,1,0:T(8,128)} %bitcast.67, bf16[8,2,4,256,256]{4,3,2,1,0:T(8,128)(2,1)} %all-to-all-done.5.rows_ref), custom_call_target="tpu_custom_call" | custom-call | flops 17179869184 | bytes 12582912 | tf_op jit(solution)/shard_map/combine/pallas_call | solution.py:337
  1772.8 42.9 %gate_grad.1 = (f32[2,2048,1024]{2,1,0:T(8,128)}, f32[2,2048,1024]{2,1,0:T(8,128)}) custom-call(bf16[4,2,2,4,256,256]{5,4,3,2,1,0:T(8,128)(2,1)} %bitcast.12.refs_0_, bf16[4,2,2,4,256,256]{5,4,3,2,1,0:T(8,128)(2,1)} %bitcast.14.refs_1_, bf16[2,2048,1024]{2,1,0:T(8,128)(2,1)} %get-tuple-element.40.gate_ref.refs_2_, ...), custom_call_target="tpu_custom_call" | custom-call | flops 34359738368 | bytes 50331648 | tf_op jit(solution)/shard_map/gate_grad/pallas_call | solution.py:529
  1815.7 30.0 %down_grad.1 = f32[2,2048,1024]{2,1,0:T(8,128)} custom-call(bf16[4,2,2,4,256,256]{5,4,3,2,1,0:T(8,128)(2,1)} %bitcast.20.refs_3_.refs_0_, bf16[4,2,2,4,256,256]{5,4,3,2,1,0:T(8,128)(2,1)} %bitcast.22.refs_4_.refs_1_, f32[2,2048,1]{2,1,0:T(8,128)} %reshape.171.refs_2_.refs_3_, bf16[2,2048,1024]{2,1,0:T(8,128)(2,1)} %get-tuple-element.35.refs_0_.refs_3_), custom_call_target="tpu_custom_call" | custom-call | flops 17179869184 | bytes 33554432 | tf_op jit(solution)/shard_map/down_grad/pallas_call | solution.py:495
  1862.5 43.8 %reduce-scatter.20.cloned.1.call-done = bf16[2048,512]{1,0:T(8,128)(2,1)} async-done(((bf16[2048,2048]{1,0:T(8,128)(2,1)}), bf16[2048,512]{1,0:T(8,128)(2,1)}) %reduce-scatter.20.cloned.1.call-update) | async-done | bytes 2097168 | tf_op jit(solution)/shard_map/reduce_scatter | solution.py:771
  1915.5 39.6 %all-reduce = (f32[2048]{0:T(1024)S(1)}, f32[2,128]{1,0:T(2,128)S(1)}, f32[2048]{0:T(1024)S(1)}) all-reduce(f32[2048]{0:T(1024)S(1)} %dynamic_update_slice.6, f32[2,128]{1,0:T(2,128)S(1)} %copy-done.38, f32[2048]{0:T(1024)S(1)} %dynamic_update_slice.7), channel_id=1, replica_groups=mesh['row'=4,'z'=4,'core'=2] {'row','z','core'}, use_global_device_ids=true, to_apply=%region_22.23 | all-reduce | flops 4352 | bytes 34816 | tf_op jit(solution)/shard_map/psum | solution.py:786
  (224 shorter events, 377.7 us)
Async XLA Ops:
  7.2 70.5 %all-gather.21.cloned.1.call-start = ((), (), s32[]{:S(2)}) async-start(), calls=%async_computation.19 | async-start | bytes 7077888 | tf_op jit(solution)/shard_map/all_gather | solution.py:617
  9.3 156.2 %all-gather.19.cloned.1.call-start = ((), (), s32[]{:S(2)}) async-start(), calls=%async_computation.18 | async-start | bytes 10485760 | tf_op jit(solution)/shard_map/all_gather | solution.py:615
  10.1 223.7 %all-gather.23.cloned.1.call-start = ((), (), s32[]{:S(2)}) async-start(), calls=%async_computation.20 | async-start | bytes 2359296 | tf_op jit(solution)/shard_map/all_gather | solution.py:623
  10.8 236.6 %all-gather.27.cloned.1.call-start = ((), (), s32[]{:S(2)}) async-start(), calls=%async_computation.31 | async-start | bytes 1310720 | tf_op jit(solution)/shard_map/all_gather | solution.py:630
  15.5 322.2 %reduce-scatter.10.cloned.1.call-start = ((), (), s32[]{:S(2)}) async-start(), calls=%async_computation.21 | async-start | bytes 10485760 | tf_op jit(solution)/shard_map/reduce_scatter | solution.py:681
  31.6 156.3 %copy-start.29 = (f32[2,128]{1,0:T(2,128)}, f32[2,128]{1,0:T(2,128)S(1)}, u32[]{:S(2)}) copy-start(f32[2,128]{1,0:T(2,128)S(1)} %maximum_convert_fusion.hg_ref) | copy-start | bytes 3076
  244.0 175.9 %all-gather.35.cloned.1.call-start = ((), (), s32[]{:S(2)}) async-start(), calls=%async_computation.35 | async-start | bytes 5242880 | tf_op jit(solution)/shard_map/all_gather | solution.py:645
  247.3 253.5 %all-gather.31.cloned.1.call-start = ((), (), s32[]{:S(2)}) async-start(), calls=%async_computation.33 | async-start | bytes 5242880 | tf_op jit(solution)/shard_map/all_gather | solution.py:645
  247.3 102.5 %copy-start.26 = (f32[512]{0:T(512)}, f32[512]{0:T(512)S(1)}, u32[]{:S(2)}) copy-start(f32[512]{0:T(512)S(1)} %convert_element_type.101) | copy-start | bytes 6148
  447.5 99.0 %all-to-all-start.2 = ((bf16[8,2,4,256,256]{4,3,2,1,0:T(8,128)(2,1)}), bf16[8,2,4,256,256]{4,3,2,1,0:T(8,128)(2,1)}, u32[]{:S(2)}, u32[]{:S(2)}) async-start(bf16[8,2,4,256,256]{4,3,2,1,0:T(8,128)(2,1)} %dispatch.6), calls=%async_computation.3 | async-start | bytes 16777216 | tf_op jit(solution)/shard_map/all_to_all | solution.py:569
  452.5 129.2 %all-gather.29.cloned.1.call-start = ((), (), s32[]{:S(2)}) async-start(), calls=%async_computation.32 | async-start | bytes 5242880 | tf_op jit(solution)/shard_map/all_gather | solution.py:645
  546.5 99.0 %all-to-all-start.1 = ((bf16[8,2,4,256,256]{4,3,2,1,0:T(8,128)(2,1)}), bf16[8,2,4,256,256]{4,3,2,1,0:T(8,128)(2,1)}, u32[]{:S(2)}, u32[]{:S(2)}) async-start(bf16[8,2,4,256,256]{4,3,2,1,0:T(8,128)(2,1)} %dispatch.5), calls=%async_computation.2 | async-start | bytes 16777216 | tf_op jit(solution)/shard_map/all_to_all | solution.py:569
  551.5 198.8 %all-gather.37.cloned.1.call-start = ((), (), s32[]{:S(2)}) async-start(), calls=%async_computation.36 | async-start | bytes 5242880 | tf_op jit(solution)/shard_map/all_gather | solution.py:645
  609.3 139.4 %copy-start.4 = (bf16[2048,512]{1,0:T(8,128)(2,1)S(1)}, bf16[2048,512]{1,0:T(8,128)(2,1)}, u32[]{:S(2)}) copy-start(bf16[2048,512]{1,0:T(8,128)(2,1)} %copy-done.3) | copy-start | bytes 6291460
  645.6 132.2 %all-to-all-start = ((bf16[8,2,4,256,256]{4,3,2,1,0:T(8,128)(2,1)}), bf16[8,2,4,256,256]{4,3,2,1,0:T(8,128)(2,1)}, u32[]{:S(2)}, u32[]{:S(2)}) async-start(bf16[8,2,4,256,256]{4,3,2,1,0:T(8,128)(2,1)} %dispatch.4), calls=%async_computation.1 | async-start | bytes 16777216 | tf_op jit(solution)/shard_map/all_to_all | solution.py:569
  650.5 133.2 %all-gather.33.cloned.1.call-start = ((), (), s32[]{:S(2)}) async-start(), calls=%async_computation.34 | async-start | bytes 2621440 | tf_op jit(solution)/shard_map/all_gather | solution.py:690
  777.8 99.0 %all-to-all-start.3 = ((bf16[8,2,4,256,256]{4,3,2,1,0:T(8,128)(2,1)}), bf16[8,2,4,256,256]{4,3,2,1,0:T(8,128)(2,1)}, u32[]{:S(2)}, u32[]{:S(2)}) async-start(bf16[8,2,4,256,256]{4,3,2,1,0:T(8,128)(2,1)} %dispatch.7), calls=%async_computation.4 | async-start | bytes 16777216 | tf_op jit(solution)/shard_map/all_to_all | solution.py:569
  940.7 99.1 %all-to-all-start.6 = ((bf16[8,2,4,256,256]{4,3,2,1,0:T(8,128)(2,1)}), bf16[8,2,4,256,256]{4,3,2,1,0:T(8,128)(2,1)}, u32[]{:S(2)}, u32[]{:S(2)}) async-start(bf16[8,2,4,256,256]{4,3,2,1,0:T(8,128)(2,1)} %bitcast.61), calls=%async_computation.9 | async-start | bytes 16777216 | tf_op jit(solution)/shard_map/all_to_all | solution.py:569
  1039.9 99.0 %all-to-all-start.7 = ((bf16[8,2,4,256,256]{4,3,2,1,0:T(8,128)(2,1)}), bf16[8,2,4,256,256]{4,3,2,1,0:T(8,128)(2,1)}, u32[]{:S(2)}, u32[]{:S(2)}) async-start(bf16[8,2,4,256,256]{4,3,2,1,0:T(8,128)(2,1)} %bitcast.60), calls=%async_computation.11 | async-start | bytes 16777216 | tf_op jit(solution)/shard_map/all_to_all | solution.py:569
  1044.8 226.7 %reduce-scatter.16.cloned.1.call-start = ((), (), s32[]{:S(2)}) async-start(), calls=%async_computation.24 | async-start | bytes 5242880 | tf_op jit(solution)/shard_map/reduce_scatter | solution.py:656
  1076.2 195.3 %reduce-scatter.18.cloned.1.call-start = ((), (), s32[]{:S(2)}) async-start(), calls=%async_computation.25 | async-start | bytes 5242880 | tf_op jit(solution)/shard_map/reduce_scatter | solution.py:656
  1169.8 205.6 %all-gather.25.cloned.1.call-start = ((), (), s32[]{:S(2)}) async-start(), calls=%async_computation.26 | async-start | bytes 10485760 | tf_op jit(solution)/shard_map/all_gather | solution.py:760
  1169.9 101.4 %copy-start.19 = (f32[2048]{0:T(1024)S(1)}, f32[2048]{0:T(1024)}, u32[]{:S(2)}) copy-start(f32[2048]{0:T(1024)} %copy-done.18) | copy-start | bytes 24580
  1289.8 95.7 %copy-start.41 = (bf16[2048,512]{1,0:T(8,128)(2,1)S(1)}, bf16[2048,512]{1,0:T(8,128)(2,1)}, u32[]{:S(2)}) copy-start(bf16[2048,512]{1,0:T(8,128)(2,1)} %all-gather.23.cloned.1.call-done) | copy-start | bytes 6291460
  1289.9 568.5 %reduce-scatter.24.cloned.1.call-start = ((), (), s32[]{:S(2)}) async-start(), calls=%async_computation.29 | async-start | bytes 2359296 | tf_op jit(solution)/shard_map/reduce_scatter | solution.py:787
  1385.3 474.9 %reduce-scatter.22.cloned.1.call-start = ((), (), s32[]{:S(2)}) async-start(), calls=%async_computation.28 | async-start | bytes 7077888 | tf_op jit(solution)/shard_map/reduce_scatter | solution.py:790
  1612.8 99.0 %all-to-all-start.5 = ((bf16[8,2,4,256,256]{4,3,2,1,0:T(8,128)(2,1)}), bf16[8,2,4,256,256]{4,3,2,1,0:T(8,128)(2,1)}, u32[]{:S(2)}, u32[]{:S(2)}) async-start(bf16[8,2,4,256,256]{4,3,2,1,0:T(8,128)(2,1)} %bitcast.58), calls=%async_computation.7 | async-start | bytes 16777216 | tf_op jit(solution)/shard_map/all_to_all | solution.py:569
  1617.8 244.7 %reduce-scatter.12.cloned.1.call-start = ((), (), s32[]{:S(2)}) async-start(), calls=%async_computation.22 | async-start | bytes 5242880 | tf_op jit(solution)/shard_map/reduce_scatter | solution.py:656
  1649.0 213.5 %reduce-scatter.14.cloned.1.call-start = ((), (), s32[]{:S(2)}) async-start(), calls=%async_computation.23 | async-start | bytes 5242880 | tf_op jit(solution)/shard_map/reduce_scatter | solution.py:656
  1742.7 163.6 %reduce-scatter.20.cloned.1.call-start = ((), (), s32[]{:S(2)}) async-start(), calls=%async_computation.27 | async-start | bytes 10485760 | tf_op jit(solution)/shard_map/reduce_scatter | solution.py:771
  1769.2 76.6 %all-to-all-start.8 = ((f32[4,16,512]{2,1,0:T(8,128)}), f32[4,16,512]{2,1,0:T(8,128)S(1)}, u32[]{:S(2)}, u32[]{:S(2)}) async-start(f32[4,16,512]{2,1,0:T(8,128)} %bitcast.34), calls=%async_computation.16 | async-start | bytes 262144 | tf_op jit(solution)/shard_map/all_to_all | solution.py:741
  1772.5 184.4 %reduce-scatter.26.cloned.1.call-start = ((), (), s32[]{:S(2)}) async-start(), calls=%async_computation.30 | async-start | bytes 147456 | tf_op jit(solution)/shard_map/reduce_scatter | solution.py:744
  (38 other events, 1096.2 us)
Sparse Core Ops, SparseCore 0:
  10.2 67.4 all-gather.20
  79.5 85.9 all-gather.18
  167.1 29.1 all-gather.22
  198.3 27.4 all-gather.26
  244.1 93.5 reduce-scatter.9
  339.2 80.7 all-gather.34
  421.5 79.2 all-gather.30
  502.3 79.2 all-gather.28
  583.2 79.7 all-gather.36
  750.4 32.6 all-gather.32
  1076.3 75.6 reduce-scatter.15
  1169.9 78.6 reduce-scatter.17
  1290.0 85.3 all-gather.24
  1385.4 36.0 reduce-scatter.23
  1499.9 82.6 reduce-scatter.21
  1649.1 75.3 reduce-scatter.11
  1742.9 73.1 reduce-scatter.13
  1818.9 87.3 reduce-scatter.19
  1909.1 30.6 reduce-scatter.25

commit v2 on v1

--- a/solution.py
+++ b/solution.py
@@ -63,12 +63,23 @@
     )
 
 
-def project_body(x_ref, gain_ref, w_ref, cos_ref, sin_ref, hg_ref, normed_ref, heads_ref, raw_ref):
-    x = x_ref[...].astype(F32)
-    factor = lax.rsqrt(jnp.mean(x * x, axis=1, keepdims=True) + EPSILON)
-    normed = (x * factor * gain_ref[...]).astype(BF)
-    normed_ref[...] = normed
-    raw = dot(normed, w_ref[...])
+def project_body(starts, *refs):
+    count = starts.shape[0]
+    x_refs, refs = refs[:count], refs[count:]
+    gain_ref, w_ref, cos_ref, sin_ref, hg_ref, normed_ref, heads_ref, raw_ref, factor_ref = refs
+    width = x_refs[0].shape[1]
+    square = sum(
+        jnp.sum(jnp.square(x_ref[...].astype(F32)), axis=1, keepdims=True) for x_ref in x_refs
+    )
+    factor = lax.rsqrt(square / (width * count) + EPSILON)
+    factor_ref[...] = factor
+    raw = None
+    for index, x_ref in enumerate(x_refs):
+        features = pl.ds(pl.multiple_of(starts[index], width), width)
+        normed = (x_ref[...].astype(F32) * factor * gain_ref[:, features]).astype(BF)
+        normed_ref[:, features] = normed
+        part = dot(normed, w_ref[features, :])
+        raw = part if raw is None else raw + part
     turned = raw_ref.shape[1]
     raw_ref[...] = raw[:, :turned]
     cosine, sine = cos_ref[...], sin_ref[...]
@@ -82,36 +93,171 @@
     heads_ref[:, turned:] = raw[:, turned:].astype(BF)
 
 
-def project(hidden, gain, weights, cosine, sine, head_gains):
-    tokens, width = hidden.shape
-    columns = weights.shape[1]
+def project(starts, pieces, gain, weights, cosine, sine, head_gains):
+    tokens, piece = pieces[0].shape
+    width, columns = weights.shape
     turned = columns // 3 * 2
     tile = 256
+    own = lambda t, s: (t, 0)
+    whole = lambda t, s: (0, 0)
     return call(
         project_body,
         (tokens // tile,),
-        [
-            pl.BlockSpec((tile, width), lambda t: (t, 0)),
-            pl.BlockSpec((1, width), lambda t: (0, 0)),
-            pl.BlockSpec((width, columns), lambda t: (0, 0)),
-            pl.BlockSpec((tile, HS), lambda t: (t, 0)),
-            pl.BlockSpec((tile, HS), lambda t: (t, 0)),
-            pl.BlockSpec((1, turned), lambda t: (0, 0)),
-        ],
-        [
-            pl.BlockSpec((tile, width), lambda t: (t, 0)),
-            pl.BlockSpec((tile, columns), lambda t: (t, 0)),
-            pl.BlockSpec((tile, turned), lambda t: (t, 0)),
-        ],
-        [shape((tokens, width), BF), shape((tokens, columns), BF), shape((tokens, turned), F32)],
+        [pl.BlockSpec((tile, piece), own)] * len(pieces)
+        + [
+            pl.BlockSpec((1, width), whole),
+            pl.BlockSpec((width, columns), whole),
+            pl.BlockSpec((tile, HS), own),
+            pl.BlockSpec((tile, HS), own),
+            pl.BlockSpec((1, turned), whole),
+        ],
+        [
+            pl.BlockSpec((tile, width), own),
+            pl.BlockSpec((tile, columns), own),
+            pl.BlockSpec((tile, turned), own),
+            pl.BlockSpec((tile, 1), own),
+        ],
+        [
+            shape((tokens, width), BF),
+            shape((tokens, columns), BF),
+            shape((tokens, turned), F32),
+            shape((tokens, 1), F32),
+        ],
         flops=2 * tokens * width * columns,
         moved=6 * tokens * width + 2 * width * columns + 6 * tokens * columns,
+        prefetch=1,
         name="project",
-    )(hidden, gain, weights, cosine, sine, head_gains)
+    )(starts, *pieces, gain, weights, cosine, sine, head_gains)
+
+
+def mix_back_body(starts, *refs):
+    count = starts.shape[0]
+    g_refs, (w_ref, out_ref) = refs[:count], refs[count:]
+    width = g_refs[0].shape[1]
+    total = None
+    for index, g_ref in enumerate(g_refs):
+        part = dot(g_ref[...], w_ref[pl.ds(pl.multiple_of(starts[index], width), width), :])
+        total = part if total is None else total + part
+    out_ref[...] = total.astype(BF)
+
+
+def mix_back(starts, pieces, weights):
+    tokens, piece = pieces[0].shape
+    width, columns = weights.shape
+    tile = 256
+    return call(
+        mix_back_body,
+        (tokens // tile,),
+        [pl.BlockSpec((tile, piece), lambda t, s: (t, 0))] * len(pieces)
+        + [pl.BlockSpec((width, columns), lambda t, s: (0, 0))],
+        pl.BlockSpec((tile, columns), lambda t, s: (t, 0)),
+        shape((tokens, columns), BF),
+        flops=2 * tokens * width * columns,
+        moved=2 * tokens * width + 2 * width * columns + 2 * tokens * columns,
+        prefetch=1,
+        name="mix_back",
+    )(starts, *pieces, weights)
+
+
+def projection_grad_body(starts, *refs):
+    count = starts.shape[0]
+    g_refs, (mixed_ref, out_ref, total_ref) = refs[:count], refs[count:]
+    width = g_refs[0].shape[1]
+
+    @pl.when(pl.program_id(0) == 0)
+    def _():
+        total_ref[...] = jnp.zeros_like(total_ref)
+
+    for index, g_ref in enumerate(g_refs):
+        rows = pl.ds(pl.multiple_of(starts[index], width), width)
+        total_ref[rows, :] += dot(g_ref[...], mixed_ref[...], 0, 0)
+
+    @pl.when(pl.program_id(0) == pl.num_programs(0) - 1)
+    def _():
+        out_ref[...] = total_ref[...].astype(BF)
+
+
+def projection_grad(starts, pieces, mixed):
+    tokens, piece = pieces[0].shape
+    columns = mixed.shape[1]
+    width = piece * len(pieces)
+    tile = 512
+    return call(
+        projection_grad_body,
+        (tokens // tile,),
+        [pl.BlockSpec((tile, piece), lambda t, s: (t, 0))] * len(pieces)
+        + [pl.BlockSpec((tile, columns), lambda t, s: (t, 0))],
+        pl.BlockSpec((width, columns), lambda t, s: (0, 0)),
+        shape((width, columns), BF),
+        scratch=[pltpu.VMEM((width, columns), F32)],
+        flops=2 * tokens * width * columns,
+        moved=2 * tokens * width + 2 * width * columns + 2 * tokens * columns,
+        prefetch=1,
+        name="projection_grad",
+    )(starts, *pieces, mixed)
+
+
+def permute(values, mask):
+    return lax.ppermute(values, "row", [(i, i ^ mask) for i in range(4)])
+
+
+def row_gather(values):
+    width = values.shape[1]
+    if lax.axis_size("row") != 4:
+        return [lax.all_gather(values, "row", axis=1, tiled=True)], jnp.zeros((1,), jnp.int32)
+    half = width // 2
+    left, right = values[:, :half], values[:, half:]
+    left_1, right_2 = permute(left, 1), permute(right, 2)
+    left_2, right_1 = permute(left, 2), permute(right, 1)
+    left_3, right_3 = permute(left_1, 2), permute(right_2, 1)
+    me = lax.axis_index("row")
+    starts = jnp.stack(
+        [(me ^ mask) * width + side * half for mask in range(4) for side in range(2)]
+    ).astype(jnp.int32)
+    return [left, right, left_1, right_1, left_2, right_2, left_3, right_3], starts
+
+
+def row_scatter_order(weights):
+    if lax.axis_size("row") != 4:
+        return weights
+    width = weights.shape[0] // 4
+    half = width // 2
+    me = lax.axis_index("row")
+    order = [(1, 0), (3, 0), (2, 1), (3, 1), (2, 0), (1, 1), (0, 0), (0, 1)]
+    return jnp.concatenate(
+        [
+            lax.dynamic_slice_in_dim(weights, (me ^ mask) * width + side * half, half, 0)
+            for mask, side in order
+        ],
+        axis=0,
+    )
+
+
+def row_scatter(left, ordered):
+    if lax.axis_size("row") != 4:
+        return lax.psum_scatter(
+            dot(left, ordered, 1, 1).astype(BF), "row", scatter_dimension=1, tiled=True
+        ).astype(F32)
+    width = ordered.shape[0] // 4
+    half = width // 2
+    part = lambda index: dot(left, ordered[index * width : (index + 1) * width], 1, 1)
+    from_x = permute(part(0).astype(BF), 1).astype(F32)
+    from_y = permute(part(1).astype(BF), 2).astype(F32)
+    onward, own = part(2), part(3)
+    last_left = permute((onward[:, :half] + from_x[:, half:]).astype(BF), 2).astype(F32)
+    last_right = permute((onward[:, half:] + from_y[:, half:]).astype(BF), 1).astype(F32)
+    return jnp.concatenate(
+        [
+            own[:, :half] + from_x[:, :half] + last_left,
+            own[:, half:] + from_y[:, :half] + last_right,
+        ],
+        axis=1,
+    )
 
 
 QUERY_TILE = 256
 KEY_TILE = 256
+EXP2_SCALE = SCALE * 1.4426950408889634
 
 
 def key_ranges(segment):
@@ -130,48 +276,58 @@
     return pl.ds(pl.multiple_of(step * KEY_TILE, KEY_TILE), KEY_TILE)
 
 
+def head(ref, index, rows=slice(None)):
+    return ref[rows, index * HS : (index + 1) * HS]
+
+
 def attend_body(low, high, q_ref, k_ref, v_ref, qs_ref, ks_ref, out_ref, sum_ref):
-    block = pl.program_id(1)
-    query = q_ref[...]
+    block = pl.program_id(0)
+    count = q_ref.shape[1] // HS
     query_docs = qs_ref[...]
 
     def step(index, state):
-        total, mixed = state
         rows = key_rows(index)
-        scores = dot(query, k_ref[rows, :], 1, 1) * SCALE
-        raised = jnp.where(query_docs == ks_ref[:, rows], jnp.exp(scores), 0.0)
-        total = total + jnp.sum(raised, axis=1, keepdims=True)
-        mixed = mixed + dot(raised.astype(BF), v_ref[rows, :])
-        return total, mixed
-
-    total, mixed = lax.fori_loop(
+        allowed = query_docs == ks_ref[:, rows]
+        scores = [dot(head(q_ref, h), head(k_ref, h, rows), 1, 1) for h in range(count)]
+        raised = [jnp.where(allowed, jnp.exp2(each * EXP2_SCALE), 0.0) for each in scores]
+        return tuple(
+            (
+                total + jnp.sum(each, axis=1, keepdims=True),
+                mixed + dot(each.astype(BF), head(v_ref, h, rows)),
+            )
+            for h, (each, (total, mixed)) in enumerate(zip(raised, state))
+        )
+
+    state = lax.fori_loop(
         low[block],
         high[block],
         step,
-        (jnp.zeros((QUERY_TILE, 1), F32), jnp.zeros((QUERY_TILE, HS), F32)),
-    )
-    out_ref[...] = (mixed / total).astype(BF)
-    sum_ref[0] = total
+        ((jnp.zeros((QUERY_TILE, 1), F32), jnp.zeros((QUERY_TILE, HS), F32)),) * count,
+    )
+    for h, (total, mixed) in enumerate(state):
+        out_ref[:, h * HS : (h + 1) * HS] = (mixed / total).astype(BF)
+        sum_ref[h] = total
 
 
 def attend(heads, segment, low, high):
     tokens, columns = heads.shape
-    count = columns // 3 // HS
+    width = columns // 3
+    count = width // HS
     return call(
         attend_body,
-        (count, tokens // QUERY_TILE),
-        [
-            pl.BlockSpec((QUERY_TILE, HS), lambda h, b, lo, hi: (b, h)),
-            pl.BlockSpec((tokens, HS), lambda h, b, lo, hi: (0, count + h)),
-            pl.BlockSpec((tokens, HS), lambda h, b, lo, hi: (0, 2 * count + h)),
-            pl.BlockSpec((QUERY_TILE, 1), lambda h, b, lo, hi: (b, 0)),
-            pl.BlockSpec((1, tokens), lambda h, b, lo, hi: (0, 0)),
-        ],
-        [
-            pl.BlockSpec((QUERY_TILE, HS), lambda h, b, lo, hi: (b, h)),
-            pl.BlockSpec((1, QUERY_TILE, 1), lambda h, b, lo, hi: (h, b, 0)),
-        ],
-        [shape((tokens, count * HS), BF), shape((count, tokens, 1), F32)],
+        (tokens // QUERY_TILE,),
+        [
+            pl.BlockSpec((QUERY_TILE, width), lambda b, lo, hi: (b, 0)),
+            pl.BlockSpec((tokens, width), lambda b, lo, hi: (0, 1)),
+            pl.BlockSpec((tokens, width), lambda b, lo, hi: (0, 2)),
+            pl.BlockSpec((QUERY_TILE, 1), lambda b, lo, hi: (b, 0)),
+            pl.BlockSpec((1, tokens), lambda b, lo, hi: (0, 0)),
+        ],
+        [
+            pl.BlockSpec((QUERY_TILE, width), lambda b, lo, hi: (b, 0)),
+            pl.BlockSpec((count, QUERY_TILE, 1), lambda b, lo, hi: (0, b, 0)),
+        ],
+        [shape((tokens, width), BF), shape((count, tokens, 1), F32)],
         flops=4 * count * tokens * tokens * HS // 2,
         moved=8 * tokens * columns,
         prefetch=2,
@@ -191,87 +347,98 @@
 
 def attend_back_body(
     low, high, q_ref, k_ref, v_ref, g_ref, o_ref, s_ref, qs_ref, ks_ref, qr_ref, kr_ref,
-    cos_ref, sin_ref, hg_ref, gq_ref, gk_ref, gv_ref, gain_ref, keys_ref, values_ref,
+    cos_ref, sin_ref, hg_ref, gq_ref, gk_ref, gv_ref, gain_ref, keys_ref, values_ref, inner_ref,
 ):
-    block = pl.program_id(1)
+    block = pl.program_id(0)
+    count = q_ref.shape[1] // HS
 
     @pl.when(block == 0)
     def _():
         keys_ref[...] = jnp.zeros_like(keys_ref)
         values_ref[...] = jnp.zeros_like(values_ref)
-
-    @pl.when((block == 0) & (pl.program_id(0) == 0))
+        gain_ref[...] = jnp.zeros_like(gain_ref)
+
+    for h in range(count):
+        inner_ref[h] = jnp.sum(
+            head(g_ref, h).astype(F32) * head(o_ref, h).astype(F32), axis=1, keepdims=True
+        )
+
+    def step(index, state):
+        rows = key_rows(index)
+        allowed = qs_ref[...] == ks_ref[:, rows]
+        scores = [dot(head(q_ref, h), head(k_ref, h, rows), 1, 1) for h in range(count)]
+        grads = [dot(head(g_ref, h), head(v_ref, h, rows), 1, 1) for h in range(count)]
+        new = []
+        for h in range(count):
+            columns = slice(h * HS, (h + 1) * HS)
+            weights = jnp.where(
+                allowed, jnp.exp2(scores[h] * EXP2_SCALE) * (1.0 / s_ref[h]), 0.0
+            )
+            grad_scores = (weights * (grads[h] - inner_ref[h])).astype(BF)
+            values_ref[rows, columns] += dot(weights.astype(BF), head(g_ref, h), 0, 0)
+            keys_ref[rows, columns] += dot(grad_scores, head(q_ref, h), 0, 0)
+            new.append(state[h] + dot(grad_scores, head(k_ref, h, rows)))
+        return tuple(new)
+
+    grad_queries = lax.fori_loop(
+        low[block], high[block], step, (jnp.zeros((QUERY_TILE, HS), F32),) * count
+    )
+    rows = pl.ds(pl.multiple_of(block * QUERY_TILE, QUERY_TILE), QUERY_TILE)
+    for h, grad_query in enumerate(grad_queries):
+        back, part = head_back(
+            grad_query * SCALE, head(qr_ref, h), hg_ref[0:1, :], cos_ref[rows, :], sin_ref[rows, :]
+        )
+        gq_ref[:, h * HS : (h + 1) * HS] = back.astype(BF)
+        gain_ref[0:1, :] += part
+
+    @pl.when(block == pl.num_programs(0) - 1)
     def _():
-        gain_ref[...] = jnp.zeros_like(gain_ref)
-
-    query, grad = q_ref[...], g_ref[...]
-    query_docs = qs_ref[...]
-    scale_back = 1.0 / s_ref[0]
-    inner = jnp.sum(grad.astype(F32) * o_ref[...].astype(F32), axis=1, keepdims=True)
-
-    def step(index, grad_query):
-        rows = key_rows(index)
-        key = k_ref[rows, :]
-        scores = dot(query, key, 1, 1) * SCALE
-        weights = jnp.where(query_docs == ks_ref[:, rows], jnp.exp(scores) * scale_back, 0.0)
-        grad_weights = dot(grad, v_ref[rows, :], 1, 1)
-        grad_scores = (weights * (grad_weights - inner)).astype(BF)
-        values_ref[rows, :] += dot(weights.astype(BF), grad, 0, 0)
-        keys_ref[rows, :] += dot(grad_scores, query, 0, 0)
-        return grad_query + dot(grad_scores, key)
-
-    grad_query = lax.fori_loop(
-        low[block], high[block], step, jnp.zeros((QUERY_TILE, HS), F32)
-    )
-    rows = pl.ds(pl.multiple_of(block * QUERY_TILE, QUERY_TILE), QUERY_TILE)
-    back, part = head_back(
-        grad_query * SCALE, qr_ref[...], hg_ref[0:1, :], cos_ref[rows, :], sin_ref[rows, :]
-    )
-    gq_ref[...] = back.astype(BF)
-    gain_ref[0:1, :] += part
-
-    @pl.when(block == pl.num_programs(1) - 1)
-    def _():
-        back, part = head_back(
-            keys_ref[...] * SCALE, kr_ref[...], hg_ref[1:2, :], cos_ref[...], sin_ref[...]
-        )
-        gk_ref[...] = back.astype(BF)
-        gain_ref[1:2, :] += part
+        for h in range(count):
+            back, part = head_back(
+                head(keys_ref, h) * SCALE, head(kr_ref, h), hg_ref[1:2, :], cos_ref[...],
+                sin_ref[...],
+            )
+            gk_ref[:, h * HS : (h + 1) * HS] = back.astype(BF)
+            gain_ref[1:2, :] += part
         gv_ref[...] = values_ref[...].astype(BF)
 
 
 def attend_back(heads, grad_mixed, mixed, sums, segment, low, high, raw, cosine, sine, gains):
     tokens, columns = heads.shape
-    count = columns // 3 // HS
-    whole = lambda h, b, lo, hi: (0, 0)
-    tile = lambda h, b, lo, hi: (b, h)
-    column = lambda h, b, lo, hi: (0, h)
+    width = columns // 3
+    count = width // HS
+    whole = lambda b, lo, hi: (0, 0)
+    tile = lambda b, lo, hi: (b, 0)
     return call(
         attend_back_body,
-        (count, tokens // QUERY_TILE),
-        [
-            pl.BlockSpec((QUERY_TILE, HS), tile),
-            pl.BlockSpec((tokens, HS), lambda h, b, lo, hi: (0, count + h)),
-            pl.BlockSpec((tokens, HS), lambda h, b, lo, hi: (0, 2 * count + h)),
-            pl.BlockSpec((QUERY_TILE, HS), tile),
-            pl.BlockSpec((QUERY_TILE, HS), tile),
-            pl.BlockSpec((1, QUERY_TILE, 1), lambda h, b, lo, hi: (h, b, 0)),
-            pl.BlockSpec((QUERY_TILE, 1), lambda h, b, lo, hi: (b, 0)),
+        (tokens // QUERY_TILE,),
+        [
+            pl.BlockSpec((QUERY_TILE, width), tile),
+            pl.BlockSpec((tokens, width), lambda b, lo, hi: (0, 1)),
+            pl.BlockSpec((tokens, width), lambda b, lo, hi: (0, 2)),
+            pl.BlockSpec((QUERY_TILE, width), tile),
+            pl.BlockSpec((QUERY_TILE, width), tile),
+            pl.BlockSpec((count, QUERY_TILE, 1), lambda b, lo, hi: (0, b, 0)),
+            pl.BlockSpec((QUERY_TILE, 1), tile),
             pl.BlockSpec((1, tokens), whole),
-            pl.BlockSpec((QUERY_TILE, HS), tile),
-            pl.BlockSpec((tokens, HS), lambda h, b, lo, hi: (0, count + h)),
+            pl.BlockSpec((QUERY_TILE, width), tile),
+            pl.BlockSpec((tokens, width), lambda b, lo, hi: (0, 1)),
             pl.BlockSpec((tokens, HS), whole),
             pl.BlockSpec((tokens, HS), whole),
             pl.BlockSpec((2, HS), whole),
         ],
         [
-            pl.BlockSpec((QUERY_TILE, HS), tile),
-            pl.BlockSpec((tokens, HS), column),
-            pl.BlockSpec((tokens, HS), column),
+            pl.BlockSpec((QUERY_TILE, width), tile),
+            pl.BlockSpec((tokens, width), whole),
+            pl.BlockSpec((tokens, width), whole),
             pl.BlockSpec((2, HS), whole),
         ],
-        [shape((tokens, count * HS), BF)] * 3 + [shape((2, HS), F32)],
-        scratch=[pltpu.VMEM((tokens, HS), F32), pltpu.VMEM((tokens, HS), F32)],
+        [shape((tokens, width), BF)] * 3 + [shape((2, HS), F32)],
+        scratch=[
+            pltpu.VMEM((tokens, width), F32),
+            pltpu.VMEM((tokens, width), F32),
+            pltpu.VMEM((count, QUERY_TILE, 1), F32),
+        ],
         flops=10 * count * tokens * tokens * HS // 2,
         moved=24 * tokens * columns,
         prefetch=2,
@@ -612,7 +779,7 @@
     head_columns = query_weight.shape[1]
     head_count = head_columns // HS
 
-    hidden_full = lax.all_gather(hidden_in, "row", axis=1, tiled=True)
+    hidden_pieces, hidden_starts = row_gather(hidden_in)
     gain_full = lax.all_gather(attention_gain, "row", axis=0, tiled=True)
     qkv_full = lax.all_gather(
         jnp.concatenate([query_weight, key_weight, value_weight], axis=1),
@@ -667,8 +834,9 @@
     head_gains = jnp.stack([query_gain, key_gain]).astype(F32)
     residual = hidden_in.astype(F32)
     gain_row = gain_full.astype(F32)[None, :]
-    normed_one, heads, raw = project(
-        hidden_full,
+    normed_one, heads, raw, first_factor = project(
+        hidden_starts,
+        hidden_pieces,
         gain_row,
         qkv_full,
         cosine,
@@ -678,10 +846,7 @@
     segment = segments[0]
     low, high = key_ranges(segment)
     mixed, sums = attend(heads, segment, low, high)
-    branch = lax.psum_scatter(
-        dot(mixed, projection_full, 1, 1).astype(BF), "row", scatter_dimension=1, tiled=True
-    )
-    middle = residual + branch.astype(F32)
+    middle = residual + row_scatter(mixed, row_scatter_order(projection_full))
     second_factor = lax.rsqrt(lax.psum(jnp.sum(middle * middle, axis=1), "row") / D + EPSILON)[
         :, None
     ]
@@ -757,24 +922,18 @@
     )
     grad_feedforward_gain = jnp.sum(grad_normed_two * middle * second_factor, axis=0)
 
-    grad_branch = lax.all_gather(grad_middle.astype(BF), "row", axis=1, tiled=True)
-    grad_mixed = dot(grad_branch, projection_full).astype(BF)
-    grad_projection = dot(grad_branch, mixed, 0, 0).astype(BF)
+    branch_pieces, branch_starts = row_gather(grad_middle.astype(BF))
+    grad_mixed = mix_back(branch_starts, branch_pieces, projection_full)
+    grad_projection = projection_grad(branch_starts, branch_pieces, mixed)
     grad_query_raw, grad_key_raw, grad_value_raw, head_gain_grads = attend_back(
         heads, grad_mixed, mixed, sums, segment, low, high, raw, cosine, sine, head_gains
     )
     grad_raw = jnp.concatenate([grad_query_raw, grad_key_raw, grad_value_raw], axis=1)
-    first_part = dot(grad_raw, qkv_full, 1, 1)
+    grad_first = row_scatter(grad_raw, row_scatter_order(qkv_full))
     first_inner = lax.psum(
-        jnp.sum(first_part * gain_row * hidden_full.astype(F32), axis=1), "row"
+        jnp.sum(grad_first * first_gain * residual, axis=1), "row"
     )[:, None]
-    grad_first = lax.psum_scatter(
-        first_part.astype(BF), "row", scatter_dimension=1, tiled=True
-    ).astype(F32)
     grad_qkv = dot(normed_one, grad_raw, 0, 0).astype(BF)
-    first_factor = lax.rsqrt(
-        jnp.mean(jnp.square(hidden_full.astype(F32)), axis=1, keepdims=True) + EPSILON
-    )
     scaled_one = grad_first * first_gain
     grad_input = (
         grad_middle + scaled_one * first_factor - residual * first_factor**3 * first_inner / D

time: 1980 us -> 1680 us (0.85)
  waiting for transfers between devices: 745 us -> 525 us
  blocking collectives: 347 us -> 267 us
  matrix products: 81.6 us -> 61.7 us
    all_gather x2 -> x0, waiting for transfers between devices: 173 us -> none  [the longest x1 87.8 us: per_device(): hidden_full = lax.all_gather(hidden_in, 'row', axis=1, tiled=True)]
    ppermute x0 -> x20, waiting for transfers between devices: none -> 134 us  [permute(): return lax.ppermute(values, 'row', [(i, i ^ mask) for i in range(4)])]
    reduce_scatter x2 -> x0, waiting for transfers between devices: 130 us -> none  [the longest x1 86.6 us: per_device(): lax.psum_scatter(dot(mixed, projection_full, 1, 1).astype(BF), 'row', sca...]
    all_to_all x1 -> x0, blocking collectives: 113 us -> none  [swap(): lax.all_to_all(rows, SWAP_AXES, split_axis=0, concat_axis=0, tiled=True)]
    all_gather x4, waiting for transfers between devices: 130 us -> 69.9 us  [send(): spread = lax.all_gather(part, 'z', axis=0)]
    all_to_all x7 -> x8, waiting for transfers between devices: 266 us -> 303 us  [swap(): lax.all_to_all(rows, SWAP_AXES, split_axis=0, concat_axis=0, tiled=True)]
    all_gather x1, blocking collectives: 9.83 us -> 43.3 us  [per_device(): gain_full = lax.all_gather(attention_gain, 'row', axis=0, tiled=True)]
    all_gather x1, waiting for transfers between devices: 43.4 us -> 15.4 us  [per_device(): lax.all_gather(jnp.concatenate([query_weight, key_weight, value_weight],...]
  transfers between devices with their start and end apart: 27 -> 44, of which waited for: 14 -> 21; matrix products, arithmetic and copies ran while one was open for 7% -> 10% of each run, Pallas kernels for 29% -> 32%
where the time goes in v2:
time: 1680 us; the launch traced here: 1670 us
  Pallas kernels  611 us (36%)
  waiting for transfers between devices  525 us (31%)
  blocking collectives  267 us (16%)
  other arithmetic  75.2 us (4%)
  starting transfers between devices  68.8 us (4%)
  matrix products  61.7 us (4%)
  local copies, waits for them, and re-layouts  43.3 us (3%)
    all_to_all x8, waiting for transfers between devices, swap(): lax.all_to_all(rows, SWAP_AXES, split_axis=0, concat_axis=0, tiled=True)  303 us
    ppermute x20, waiting for transfers between devices, permute(): return lax.ppermute(values, 'row', [(i, i ^ mask) for i in range(4)])  134 us
    pallas_call x4, Pallas kernels, combine(): call(combine_body, (groups, tokens // tile), [pl.BlockSpec((1, tile, expe...  124 us
    pallas_call x4, Pallas kernels, dispatch(): call(dispatch_body, (groups, targets), [pl.BlockSpec((1, 1, local, tokens...  110 us
    all_gather x1, blocking collectives, per_device(): lax.all_gather(lax.all_gather(router_weight.T, TOKENS_AXES, axis=1, tiled...  83.3 us
    all_gather x4, waiting for transfers between devices, send(): spread = lax.all_gather(part, 'z', axis=0)  69.9 us
    pallas_call x2, Pallas kernels, rows_back(): call(rows_back_body, (local, cores, rows), [pre, pre, weight, weight], pl...  58.2 us
    dot_general x12, matrix products, dot(): lax.dot_general(left, right, (((left_dim,), (right_dim,)), ((), ())), pre...  57.8 us
  transfers between devices with their start and end apart: 44, of which 21 were waited for; matrix products, arithmetic and copies ran while one was open for 10% of the time, Pallas kernels for 32%

profile of v2, /device:TPU:0, one launch (start us, length us, event | category | flops | bytes accessed | tf_op | source)
XLA Modules:
  0.0 1666.8 jit_solution(11963448422181379154)
XLA Ops:
  21.9 43.3 %all-gather.7 = bf16[4,1,512]{2,1,0:T(2,128)(2,1)S(1)} all-gather(bf16[1,1,512]{2,1,0:T(2,128)(2,1)S(1)} %reshape.153), channel_id=1, replica_groups=mesh['row'=4,'z'=4,'core'=2] {'row'}, dimensions={0}, use_global_device_ids=true | all-gather | bytes 5120 | tf_op jit(solution)/shard_map/all_gather | solution.py:783
  108.4 30.9 %project.1 = (bf16[2048,2048]{1,0:T(8,128)(2,1)}, bf16[2048,1536]{1,0:T(8,128)(2,1)}, f32[2048,1024]{1,0:T(8,128)}, f32[2048,1]{1,0:T(8,128)}) custom-call(s32[8]{0:T(128)} %stack.53.starts, bf16[2048,256]{1,0:T(8,128)(2,1)} %copy-done.23, bf16[2048,256]{1,0:T(8,128)(2,1)} %copy-done.22, bf16[2048,256]{1,0:T(8,128)(2,1)} %collective-permute-done.refs_2_, ...), custom_call_target="tpu_custom_call" | custom-call | flops 12884901888 | bytes 50331648 | tf_op jit(solution)/shard_map/project/pallas_call | solution.py:103
  139.3 25.3 %attend.1 = (bf16[2048,512]{1,0:T(8,128)(2,1)}, f32[4,2048,1]{2,1,0:T(8,128)}) custom-call(s32[8]{0:T(128)} %get-tuple-element.61.low, s32[8]{0:T(128)} %get-tuple-element.60.high, bf16[2048,1536]{1,0:T(8,128)(2,1)} %get-tuple-element.34.q_ref.k_ref.v_ref, bf16[2048,1536]{1,0:T(8,128)(2,1)} %get-tuple-element.34.q_ref.k_ref.v_ref, ...), custom_call_target="tpu_custom_call" | custom-call | flops 4294967296 | bytes 25165824 | tf_op jit(solution)/shard_map/attend/pallas_call | solution.py:316
  180.3 36.7 %collective-permute-done.8 = bf16[2048,512]{1,0:T(8,128)(2,1)} collective-permute-done((bf16[2048,512]{1,0:T(8,128)(2,1)}, bf16[2048,512]{1,0:T(8,128)(2,1)}, u32[]{:S(2)}, u32[]{:S(2)}) %collective-permute-start.8) | collective-permute-done | bytes 2097184 | tf_op jit(solution)/shard_map/ppermute | solution.py:201
  267.0 27.5 %dispatch.6 = bf16[8,2,4,256,256]{4,3,2,1,0:T(8,128)(2,1)} custom-call(s32[4,8,2,2048]{3,2,1,0:T(2,128)} %copy.95.slot_ref, bf16[4,2048,256]{2,1,0:T(8,128)(2,1)} %bitcast.94), custom_call_target="tpu_custom_call" | custom-call | flops 17179869184 | bytes 12582912 | tf_op jit(solution)/shard_map/dispatch/pallas_call | solution.py:465
  300.0 44.1 %all-gather.25.cloned.1.call-done = bf16[8192,256]{1,0:T(8,128)(2,1)} async-done(((bf16[2048,256]{1,0:T(8,128)(2,1)}), bf16[8192,256]{1,0:T(8,128)(2,1)}) %all-gather.25.cloned.1.call-update) | async-done | bytes 4194320 | tf_op jit(solution)/shard_map/all_gather | solution.py:812
  344.2 27.6 %dispatch.5 = bf16[8,2,4,256,256]{4,3,2,1,0:T(8,128)(2,1)} custom-call(s32[4,8,2,2048]{3,2,1,0:T(2,128)} %copy.95.slot_ref, bf16[4,2048,256]{2,1,0:T(8,128)(2,1)} %bitcast.97), custom_call_target="tpu_custom_call" | custom-call | flops 17179869184 | bytes 12582912 | tf_op jit(solution)/shard_map/dispatch/pallas_call | solution.py:465
  399.2 25.7 %all-gather.23.cloned.1.call-done = bf16[8192,256]{1,0:T(8,128)(2,1)} async-done(((bf16[2048,256]{1,0:T(8,128)(2,1)}), bf16[8192,256]{1,0:T(8,128)(2,1)}) %all-gather.23.cloned.1.call-update) | async-done | bytes 4194320 | tf_op jit(solution)/shard_map/all_gather | solution.py:812
  424.9 27.6 %dispatch.4 = bf16[8,2,4,256,256]{4,3,2,1,0:T(8,128)(2,1)} custom-call(s32[4,8,2,2048]{3,2,1,0:T(2,128)} %copy.95.slot_ref, bf16[4,2048,256]{2,1,0:T(8,128)(2,1)} %bitcast.96), custom_call_target="tpu_custom_call" | custom-call | flops 17179869184 | bytes 12582912 | tf_op jit(solution)/shard_map/dispatch/pallas_call | solution.py:465
  452.5 40.0 %all-to-all-done.1 = bf16[8,2,4,256,256]{4,3,2,1,0:T(8,128)(2,1)} async-done(((bf16[8,2,4,256,256]{4,3,2,1,0:T(8,128)(2,1)}), bf16[8,2,4,256,256]{4,3,2,1,0:T(8,128)(2,1)}, u32[]{:S(2)}, u32[]{:S(2)}) %all-to-all-start.1) | async-done | bytes 8388640 | tf_op jit(solution)/shard_map/all_to_all | solution.py:736
  511.6 83.3 %all_gather.70 = bf16[64,2048]{1,0:T(8,128)(2,1)S(1)} all-gather(bf16[16,2048]{1,0:T(8,128)(2,1)S(1)} %all_gather.69), channel_id=1, replica_groups=mesh['row'=4,'z'=4,'core'=2] {'row'}, dimensions={0}, use_global_device_ids=true | all-gather | bytes 327680 | tf_op jit(solution)/shard_map/all_gather | solution.py:791
  597.2 27.5 %dispatch.7 = bf16[8,2,4,256,256]{4,3,2,1,0:T(8,128)(2,1)} custom-call(s32[4,8,2,2048]{3,2,1,0:T(2,128)} %copy.95.slot_ref, bf16[4,2048,256]{2,1,0:T(8,128)(2,1)} %bitcast.95), custom_call_target="tpu_custom_call" | custom-call | flops 17179869184 | bytes 12582912 | tf_op jit(solution)/shard_map/dispatch/pallas_call | solution.py:465
  654.6 45.5 %gate_up.1 = (bf16[2,2048,1024]{2,1,0:T(8,128)(2,1)}, bf16[2,2048,1024]{2,1,0:T(8,128)(2,1)}, bf16[2,2048,1024]{2,1,0:T(8,128)(2,1)}) custom-call(bf16[4,2,2,4,256,256]{5,4,3,2,1,0:T(8,128)(2,1)} %bitcast.20.refs_0_, bf16[4,2,2,4,256,256]{5,4,3,2,1,0:T(8,128)(2,1)} %bitcast.22.refs_1_, bf16[2,2048,1024]{2,1,0:T(8,128)(2,1)} %gate_w.3, ...), custom_call_target="tpu_custom_call" | custom-call | flops 34359738368 | bytes 67108864 | tf_op jit(solution)/shard_map/gate_up/pallas_call | solution.py:549
  700.1 23.7 %all-to-all-done.3 = bf16[8,2,4,256,256]{4,3,2,1,0:T(8,128)(2,1)} async-done(((bf16[8,2,4,256,256]{4,3,2,1,0:T(8,128)(2,1)}), bf16[8,2,4,256,256]{4,3,2,1,0:T(8,128)(2,1)}, u32[]{:S(2)}, u32[]{:S(2)}) %all-to-all-start.3) | async-done | bytes 8388640 | tf_op jit(solution)/shard_map/all_to_all | solution.py:736
  723.7 34.7 %act_back.1 = (bf16[2,2048,1024]{2,1,0:T(8,128)(2,1)}, bf16[2,2048,1024]{2,1,0:T(8,128)(2,1)}) custom-call(bf16[4,2,2,4,256,256]{5,4,3,2,1,0:T(8,128)(2,1)} %bitcast.28.refs_3_.refs_0_, bf16[4,2,2,4,256,256]{5,4,3,2,1,0:T(8,128)(2,1)} %bitcast.30.refs_4_.refs_1_, bf16[2,2048,1024]{2,1,0:T(8,128)(2,1)} %refs_2_.3, f32[2,2048,1]{2,1,0:T(8,128)} %reshape.157.refs_2_.refs_3_, ...), custom_call_target="tpu_custom_call" | custom-call | flops 17179869184 | bytes 25165824 | tf_op jit(solution)/shard_map/act_back/pallas_call | solution.py:630
  758.5 29.1 %rows_back.2 = bf16[4,2,2,4,256,256]{5,4,3,2,1,0:T(8,128)(2,1)} custom-call(bf16[2,2048,1024]{2,1,0:T(8,128)(2,1)} %get-tuple-element.41.gate_ref.refs_2_, bf16[2,2048,1024]{2,1,0:T(8,128)(2,1)} %get-tuple-element.42.up_ref.refs_3_, bf16[2,2048,1024]{2,1,0:T(8,128)(2,1)} %gate_w.3, bf16[2,2048,1024]{2,1,0:T(8,128)(2,1)} %up_w.3), custom_call_target="tpu_custom_call" | custom-call | flops 17179869184 | bytes 33554432 | tf_op jit(solution)/shard_map/rows_back/pallas_call | solution.py:723
  795.4 29.1 %rows_back.3 = bf16[4,2,2,4,256,256]{5,4,3,2,1,0:T(8,128)(2,1)} custom-call(bf16[2,2048,1024]{2,1,0:T(8,128)(2,1)} %get-tuple-element.41.gate_ref.refs_2_, bf16[2,2048,1024]{2,1,0:T(8,128)(2,1)} %get-tuple-element.42.up_ref.refs_3_, bf16[2,2048,1024]{2,1,0:T(8,128)(2,1)} %gate_w.3, bf16[2,2048,1024]{2,1,0:T(8,128)(2,1)} %up_w.3), custom_call_target="tpu_custom_call" | custom-call | flops 17179869184 | bytes 33554432 | tf_op jit(solution)/shard_map/rows_back/pallas_call | solution.py:723
  824.5 62.3 %all-to-all-done.6.rows_ref = bf16[8,2,4,256,256]{4,3,2,1,0:T(8,128)(2,1)} async-done(((bf16[8,2,4,256,256]{4,3,2,1,0:T(8,128)(2,1)}), bf16[8,2,4,256,256]{4,3,2,1,0:T(8,128)(2,1)}, u32[]{:S(2)}, u32[]{:S(2)}) %all-to-all-start.6) | async-done | bytes 8388640 | tf_op jit(solution)/shard_map/all_to_all | solution.py:736
  892.0 30.9 %combine.6 = bf16[4,2048,256]{2,1,0:T(8,128)(2,1)} custom-call(s32[4,2048,16]{2,1,0:T(8,128)} %bitcast.72, bf16[8,2,4,256,256]{4,3,2,1,0:T(8,128)(2,1)} %all-to-all-done.6.rows_ref), custom_call_target="tpu_custom_call" | custom-call | flops 17179869184 | bytes 12582912 | tf_op jit(solution)/shard_map/combine/pallas_call | solution.py:504
  922.9 33.0 %produce.1 = (bf16[4,2,2,4,256,256]{5,4,3,2,1,0:T(8,128)(2,1)}, bf16[4,2,2,4,256,256]{5,4,3,2,1,0:T(8,128)(2,1)}, f32[2,2048,1]{2,1,0:T(8,128)}) custom-call(bf16[2,2048,1024]{2,1,0:T(8,128)(2,1)} %get-tuple-element.36.refs_0_.refs_3_, bf16[2,2048,1024]{2,1,0:T(8,128)(2,1)} %refs_2_.3, f32[2,2048,1]{2,1,0:T(8,128)} %reshape.157.refs_2_.refs_3_, ...), custom_call_target="tpu_custom_call" | custom-call | flops 17179869184 | bytes 75497472 | tf_op jit(solution)/shard_map/produce/pallas_call | solution.py:589
  955.9 29.8 %all-to-all-done.7.rows_ref = bf16[8,2,4,256,256]{4,3,2,1,0:T(8,128)(2,1)} async-done(((bf16[8,2,4,256,256]{4,3,2,1,0:T(8,128)(2,1)}), bf16[8,2,4,256,256]{4,3,2,1,0:T(8,128)(2,1)}, u32[]{:S(2)}, u32[]{:S(2)}) %all-to-all-start.7) | async-done | bytes 8388640 | tf_op jit(solution)/shard_map/all_to_all | solution.py:736
  990.8 30.9 %combine.7 = bf16[4,2048,256]{2,1,0:T(8,128)(2,1)} custom-call(s32[4,2048,16]{2,1,0:T(8,128)} %bitcast.73, bf16[8,2,4,256,256]{4,3,2,1,0:T(8,128)(2,1)} %all-to-all-done.7.rows_ref), custom_call_target="tpu_custom_call" | custom-call | flops 17179869184 | bytes 12582912 | tf_op jit(solution)/shard_map/combine/pallas_call | solution.py:504
  1021.7 63.1 %all-to-all-done.4.rows_ref = bf16[8,2,4,256,256]{4,3,2,1,0:T(8,128)(2,1)} async-done(((bf16[8,2,4,256,256]{4,3,2,1,0:T(8,128)(2,1)}), bf16[8,2,4,256,256]{4,3,2,1,0:T(8,128)(2,1)}, u32[]{:S(2)}, u32[]{:S(2)}) %all-to-all-start.4) | async-done | bytes 8388640 | tf_op jit(solution)/shard_map/all_to_all | solution.py:736
  1089.9 31.0 %combine.4 = bf16[4,2048,256]{2,1,0:T(8,128)(2,1)} custom-call(s32[4,2048,16]{2,1,0:T(8,128)} %bitcast.74, bf16[8,2,4,256,256]{4,3,2,1,0:T(8,128)(2,1)} %all-to-all-done.4.rows_ref), custom_call_target="tpu_custom_call" | custom-call | flops 17179869184 | bytes 12582912 | tf_op jit(solution)/shard_map/combine/pallas_call | solution.py:504
  1120.9 63.0 %all-to-all-done.5.rows_ref = bf16[8,2,4,256,256]{4,3,2,1,0:T(8,128)(2,1)} async-done(((bf16[8,2,4,256,256]{4,3,2,1,0:T(8,128)(2,1)}), bf16[8,2,4,256,256]{4,3,2,1,0:T(8,128)(2,1)}, u32[]{:S(2)}, u32[]{:S(2)}) %all-to-all-start.5) | async-done | bytes 8388640 | tf_op jit(solution)/shard_map/all_to_all | solution.py:736
  1183.8 30.9 %combine.5 = bf16[4,2048,256]{2,1,0:T(8,128)(2,1)} custom-call(s32[4,2048,16]{2,1,0:T(8,128)} %bitcast.75, bf16[8,2,4,256,256]{4,3,2,1,0:T(8,128)(2,1)} %all-to-all-done.5.rows_ref), custom_call_target="tpu_custom_call" | custom-call | flops 17179869184 | bytes 12582912 | tf_op jit(solution)/shard_map/combine/pallas_call | solution.py:504
  1217.0 46.2 %all_gather.79 = f32[32,2,2,4,256]{4,3,2,1,0:T(4,128)S(1)} all-gather(f32[1,2,2,4,256]{4,3,2,1,0:T(4,128)S(1)} %all_gather_reshape.3), channel_id=1, replica_groups=mesh['row'=4,'z'=4,'core'=2] {'row','z','core'}, dimensions={0}, use_global_device_ids=true | all-gather | bytes 540672 | tf_op jit(solution)/shard_map/all_gather | solution.py:891
  1308.1 22.0 %collective-permute-done.10.refs_2_ = bf16[2048,256]{1,0:T(8,128)(2,1)S(1)} collective-permute-done((bf16[2048,256]{1,0:T(8,128)(2,1)S(1)}, bf16[2048,256]{1,0:T(8,128)(2,1)S(1)}, u32[]{:S(2)}, u32[]{:S(2)}) %collective-permute-start.10) | collective-permute-done | bytes 1048608 | tf_op jit(solution)/shard_map/ppermute | solution.py:201
  1395.9 54.4 %attend_back.1 = (bf16[2048,512]{1,0:T(8,128)(2,1)}, bf16[2048,512]{1,0:T(8,128)(2,1)}, bf16[2048,512]{1,0:T(8,128)(2,1)}, f32[2,128]{1,0:T(2,128)}) custom-call(s32[8]{0:T(128)} %get-tuple-element.61.low, s32[8]{0:T(128)} %get-tuple-element.60.high, bf16[2048,1536]{1,0:T(8,128)(2,1)} %get-tuple-element.34.q_ref.k_ref.v_ref, ...), custom_call_target="tpu_custom_call" | custom-call | flops 10737418240 | bytes 75497472 | tf_op jit(solution)/shard_map/attend_back/pallas_call | solution.py:412
  1493.5 43.4 %gate_grad.1 = (f32[2,2048,1024]{2,1,0:T(8,128)}, f32[2,2048,1024]{2,1,0:T(8,128)}) custom-call(bf16[4,2,2,4,256,256]{5,4,3,2,1,0:T(8,128)(2,1)} %bitcast.20.refs_0_, bf16[4,2,2,4,256,256]{5,4,3,2,1,0:T(8,128)(2,1)} %bitcast.22.refs_1_, bf16[2,2048,1024]{2,1,0:T(8,128)(2,1)} %get-tuple-element.41.gate_ref.refs_2_, ...), custom_call_target="tpu_custom_call" | custom-call | flops 34359738368 | bytes 50331648 | tf_op jit(solution)/shard_map/gate_grad/pallas_call | solution.py:696
  1559.1 30.0 %down_grad.1 = f32[2,2048,1024]{2,1,0:T(8,128)} custom-call(bf16[4,2,2,4,256,256]{5,4,3,2,1,0:T(8,128)(2,1)} %bitcast.28.refs_3_.refs_0_, bf16[4,2,2,4,256,256]{5,4,3,2,1,0:T(8,128)(2,1)} %bitcast.30.refs_4_.refs_1_, f32[2,2048,1]{2,1,0:T(8,128)} %reshape.157.refs_2_.refs_3_, bf16[2,2048,1024]{2,1,0:T(8,128)(2,1)} %get-tuple-element.36.refs_0_.refs_3_), custom_call_target="tpu_custom_call" | custom-call | flops 17179869184 | bytes 33554432 | tf_op jit(solution)/shard_map/down_grad/pallas_call | solution.py:662
  1601.6 37.1 %all-reduce = (f32[2048]{0:T(1024)S(1)}, f32[2,128]{1,0:T(2,128)S(1)}, f32[2048]{0:T(1024)S(1)}) all-reduce(f32[2048]{0:T(1024)S(1)} %dynamic_update_slice.6, f32[2,128]{1,0:T(2,128)S(1)} %copy-done.47, f32[2048]{0:T(1024)S(1)} %dynamic_update_slice.7), channel_id=1, replica_groups=mesh['row'=4,'z'=4,'core'=2] {'row','z','core'}, use_global_device_ids=true, to_apply=%region_19.20 | all-reduce | flops 4352 | bytes 34816 | tf_op jit(solution)/shard_map/psum | solution.py:945
  (304 shorter events, 442.0 us)
Async XLA Ops:
  7.2 69.4 %all-gather.19.cloned.1.call-start = ((), (), s32[]{:S(2)}) async-start(), calls=%async_computation.17 | async-start | bytes 2359296 | tf_op jit(solution)/shard_map/all_gather | solution.py:790
  7.9 99.9 %all-gather.17.cloned.1.call-start = ((), (), s32[]{:S(2)}) async-start(), calls=%async_computation.16 | async-start | bytes 7077888 | tf_op jit(solution)/shard_map/all_gather | solution.py:784
  10.0 166.5 %all-gather.21.cloned.1.call-start = ((), (), s32[]{:S(2)}) async-start(), calls=%async_computation.25 | async-start | bytes 1310720 | tf_op jit(solution)/shard_map/all_gather | solution.py:797
  11.9 56.8 %collective-permute-start = (bf16[2048,256]{1,0:T(8,128)(2,1)S(1)}, bf16[2048,256]{1,0:T(8,128)(2,1)}, u32[]{:S(2)}, u32[]{:S(2)}) collective-permute-start(bf16[2048,256]{1,0:T(8,128)(2,1)S(1)} %get-tuple-element.101.refs_0_), channel_id=1, source_target_pairs={{0,8},{8,0},{16,24},{24,16},{1,9},{9,1},{17,25},{25,17},{2,10},{10... | collective-permute-start | bytes 3145736 | tf_op jit(solution)/shard_map/ppermute | solution.py:201
  14.9 54.3 %collective-permute-start.3 = (bf16[2048,256]{1,0:T(8,128)(2,1)S(1)}, bf16[2048,256]{1,0:T(8,128)(2,1)}, u32[]{:S(2)}, u32[]{:S(2)}) collective-permute-start(bf16[2048,256]{1,0:T(8,128)(2,1)S(1)} %get-tuple-element.100.refs_1_), channel_id=1, source_target_pairs={{0,16},{8,24},{16,0},{24,8},{1,17},{9,25},{17,1},{25,9},{2,18},{10... | collective-permute-start | bytes 3145736 | tf_op jit(solution)/shard_map/ppermute | solution.py:201
  16.4 62.6 %collective-permute-start.1 = (bf16[2048,256]{1,0:T(8,128)(2,1)S(1)}, bf16[2048,256]{1,0:T(8,128)(2,1)}, u32[]{:S(2)}, u32[]{:S(2)}) collective-permute-start(bf16[2048,256]{1,0:T(8,128)(2,1)S(1)} %get-tuple-element.100.refs_1_), channel_id=1, source_target_pairs={{0,8},{8,0},{16,24},{24,16},{1,9},{9,1},{17,25},{25,17},{2,10},{10... | collective-permute-start | bytes 3145736 | tf_op jit(solution)/shard_map/ppermute | solution.py:201
  16.9 62.1 %collective-permute-start.2 = (bf16[2048,256]{1,0:T(8,128)(2,1)S(1)}, bf16[2048,256]{1,0:T(8,128)(2,1)}, u32[]{:S(2)}, u32[]{:S(2)}) collective-permute-start(bf16[2048,256]{1,0:T(8,128)(2,1)S(1)} %get-tuple-element.101.refs_0_), channel_id=1, source_target_pairs={{0,16},{8,24},{16,0},{24,8},{1,17},{9,25},{17,1},{25,9},{2,18},{10... | collective-permute-start | bytes 3145736 | tf_op jit(solution)/shard_map/ppermute | solution.py:201
  21.6 245.3 %all-gather.29.cloned.1.call-start = ((), (), s32[]{:S(2)}) async-start(), calls=%async_computation.29 | async-start | bytes 5242880 | tf_op jit(solution)/shard_map/all_gather | solution.py:812
  168.9 48.1 %collective-permute-start.8 = (bf16[2048,512]{1,0:T(8,128)(2,1)}, bf16[2048,512]{1,0:T(8,128)(2,1)}, u32[]{:S(2)}, u32[]{:S(2)}) collective-permute-start(bf16[2048,512]{1,0:T(8,128)(2,1)} %convolution_convert_fusion.3), channel_id=1, source_target_pairs={{0,16},{8,24},{16,0},{24,8},{1,17},{9,25},{17,1},{25,9},{2,18},{10... | collective-permute-start | bytes 6291464 | tf_op jit(solution)/shard_map/ppermute | solution.py:201
  173.0 47.8 %collective-permute-start.6 = (bf16[2048,512]{1,0:T(8,128)(2,1)}, bf16[2048,512]{1,0:T(8,128)(2,1)}, u32[]{:S(2)}, u32[]{:S(2)}) collective-permute-start(bf16[2048,512]{1,0:T(8,128)(2,1)} %convolution_convert_fusion.4), channel_id=1, source_target_pairs={{0,8},{8,0},{16,24},{24,16},{1,9},{9,1},{17,25},{25,17},{2,10},{10... | collective-permute-start | bytes 6291464 | tf_op jit(solution)/shard_map/ppermute | solution.py:201
  176.0 168.1 %all-gather.25.cloned.1.call-start = ((), (), s32[]{:S(2)}) async-start(), calls=%async_computation.27 | async-start | bytes 5242880 | tf_op jit(solution)/shard_map/all_gather | solution.py:812
  294.5 99.0 %all-to-all-start.2 = ((bf16[8,2,4,256,256]{4,3,2,1,0:T(8,128)(2,1)}), bf16[8,2,4,256,256]{4,3,2,1,0:T(8,128)(2,1)}, u32[]{:S(2)}, u32[]{:S(2)}) async-start(bf16[8,2,4,256,256]{4,3,2,1,0:T(8,128)(2,1)} %dispatch.6), calls=%async_computation.2 | async-start | bytes 16777216 | tf_op jit(solution)/shard_map/all_to_all | solution.py:736
  299.4 125.5 %all-gather.23.cloned.1.call-start = ((), (), s32[]{:S(2)}) async-start(), calls=%async_computation.26 | async-start | bytes 5242880 | tf_op jit(solution)/shard_map/all_gather | solution.py:812
  393.5 99.0 %all-to-all-start.1 = ((bf16[8,2,4,256,256]{4,3,2,1,0:T(8,128)(2,1)}), bf16[8,2,4,256,256]{4,3,2,1,0:T(8,128)(2,1)}, u32[]{:S(2)}, u32[]{:S(2)}) async-start(bf16[8,2,4,256,256]{4,3,2,1,0:T(8,128)(2,1)} %dispatch.5), calls=%async_computation.1 | async-start | bytes 16777216 | tf_op jit(solution)/shard_map/all_to_all | solution.py:736
  398.4 198.8 %all-gather.31.cloned.1.call-start = ((), (), s32[]{:S(2)}) async-start(), calls=%async_computation.30 | async-start | bytes 5242880 | tf_op jit(solution)/shard_map/all_gather | solution.py:812
  492.5 132.3 %all-to-all-start = ((bf16[8,2,4,256,256]{4,3,2,1,0:T(8,128)(2,1)}), bf16[8,2,4,256,256]{4,3,2,1,0:T(8,128)(2,1)}, u32[]{:S(2)}, u32[]{:S(2)}) async-start(bf16[8,2,4,256,256]{4,3,2,1,0:T(8,128)(2,1)} %dispatch.4), calls=%async_computation | async-start | bytes 16777216 | tf_op jit(solution)/shard_map/all_to_all | solution.py:736
  497.4 133.3 %all-gather.27.cloned.1.call-start = ((), (), s32[]{:S(2)}) async-start(), calls=%async_computation.28 | async-start | bytes 2621440 | tf_op jit(solution)/shard_map/all_gather | solution.py:855
  624.7 99.0 %all-to-all-start.3 = ((bf16[8,2,4,256,256]{4,3,2,1,0:T(8,128)(2,1)}), bf16[8,2,4,256,256]{4,3,2,1,0:T(8,128)(2,1)}, u32[]{:S(2)}, u32[]{:S(2)}) async-start(bf16[8,2,4,256,256]{4,3,2,1,0:T(8,128)(2,1)} %dispatch.7), calls=%async_computation.3 | async-start | bytes 16777216 | tf_op jit(solution)/shard_map/all_to_all | solution.py:736
  787.6 99.2 %all-to-all-start.6 = ((bf16[8,2,4,256,256]{4,3,2,1,0:T(8,128)(2,1)}), bf16[8,2,4,256,256]{4,3,2,1,0:T(8,128)(2,1)}, u32[]{:S(2)}, u32[]{:S(2)}) async-start(bf16[8,2,4,256,256]{4,3,2,1,0:T(8,128)(2,1)} %bitcast.69), calls=%async_computation.8 | async-start | bytes 16777216 | tf_op jit(solution)/shard_map/all_to_all | solution.py:736
  886.8 99.0 %all-to-all-start.7 = ((bf16[8,2,4,256,256]{4,3,2,1,0:T(8,128)(2,1)}), bf16[8,2,4,256,256]{4,3,2,1,0:T(8,128)(2,1)}, u32[]{:S(2)}, u32[]{:S(2)}) async-start(bf16[8,2,4,256,256]{4,3,2,1,0:T(8,128)(2,1)} %bitcast.67), calls=%async_computation.10 | async-start | bytes 16777216 | tf_op jit(solution)/shard_map/all_to_all | solution.py:736
  891.7 392.0 %reduce-scatter.12.cloned.1.call-start = ((), (), s32[]{:S(2)}) async-start(), calls=%async_computation.20 | async-start | bytes 5242880 | tf_op jit(solution)/shard_map/reduce_scatter | solution.py:823
  985.8 99.0 %all-to-all-start.4 = ((bf16[8,2,4,256,256]{4,3,2,1,0:T(8,128)(2,1)}), bf16[8,2,4,256,256]{4,3,2,1,0:T(8,128)(2,1)}, u32[]{:S(2)}, u32[]{:S(2)}) async-start(bf16[8,2,4,256,256]{4,3,2,1,0:T(8,128)(2,1)} %bitcast.68), calls=%async_computation.4 | async-start | bytes 16777216 | tf_op jit(solution)/shard_map/all_to_all | solution.py:736
  990.8 293.0 %reduce-scatter.14.cloned.1.call-start = ((), (), s32[]{:S(2)}) async-start(), calls=%async_computation.21 | async-start | bytes 5242880 | tf_op jit(solution)/shard_map/reduce_scatter | solution.py:823
  1084.8 99.0 %all-to-all-start.5 = ((bf16[8,2,4,256,256]{4,3,2,1,0:T(8,128)(2,1)}), bf16[8,2,4,256,256]{4,3,2,1,0:T(8,128)(2,1)}, u32[]{:S(2)}, u32[]{:S(2)}) async-start(bf16[8,2,4,256,256]{4,3,2,1,0:T(8,128)(2,1)} %bitcast.66), calls=%async_computation.6 | async-start | bytes 16777216 | tf_op jit(solution)/shard_map/all_to_all | solution.py:736
  1089.8 207.5 %reduce-scatter.8.cloned.1.call-start = ((), (), s32[]{:S(2)}) async-start(), calls=%async_computation.18 | async-start | bytes 5242880 | tf_op jit(solution)/shard_map/reduce_scatter | solution.py:823
  1120.8 176.5 %reduce-scatter.10.cloned.1.call-start = ((), (), s32[]{:S(2)}) async-start(), calls=%async_computation.19 | async-start | bytes 5242880 | tf_op jit(solution)/shard_map/reduce_scatter | solution.py:823
  1214.9 441.0 %reduce-scatter.18.cloned.1.call-start = ((), (), s32[]{:S(2)}) async-start(), calls=%async_computation.23 | async-start | bytes 2359296 | tf_op jit(solution)/shard_map/reduce_scatter | solution.py:946
  1384.5 273.2 %reduce-scatter.16.cloned.1.call-start = ((), (), s32[]{:S(2)}) async-start(), calls=%async_computation.22 | async-start | bytes 7077888 | tf_op jit(solution)/shard_map/reduce_scatter | solution.py:949
  1486.0 61.2 %collective-permute-start.18 = (bf16[2048,512]{1,0:T(8,128)(2,1)}, bf16[2048,512]{1,0:T(8,128)(2,1)}, u32[]{:S(2)}, u32[]{:S(2)}) collective-permute-start(bf16[2048,512]{1,0:T(8,128)(2,1)} %convolution_convert_fusion.1), channel_id=1, source_target_pairs={{0,16},{8,24},{16,0},{24,8},{1,17},{9,25},{17,1},{25,9},{2,18},{10... | collective-permute-start | bytes 6291464 | tf_op jit(solution)/shard_map/ppermute | solution.py:201
  1492.3 57.1 %collective-permute-start.16 = (bf16[2048,512]{1,0:T(8,128)(2,1)}, bf16[2048,512]{1,0:T(8,128)(2,1)}, u32[]{:S(2)}, u32[]{:S(2)}) collective-permute-start(bf16[2048,512]{1,0:T(8,128)(2,1)} %convolution_convert_fusion.2), channel_id=1, source_target_pairs={{0,8},{8,0},{16,24},{24,16},{1,9},{9,1},{17,25},{25,17},{2,10},{10... | collective-permute-start | bytes 6291464 | tf_op jit(solution)/shard_map/ppermute | solution.py:201
  1538.0 51.1 %all-to-all-start.8 = ((f32[4,16,512]{2,1,0:T(8,128)}), f32[4,16,512]{2,1,0:T(8,128)S(1)}, u32[]{:S(2)}, u32[]{:S(2)}) async-start(f32[4,16,512]{2,1,0:T(8,128)} %bitcast.41), calls=%async_computation.14 | async-start | bytes 262144 | tf_op jit(solution)/shard_map/all_to_all | solution.py:906
  1541.4 118.7 %reduce-scatter.20.cloned.1.call-start = ((), (), s32[]{:S(2)}) async-start(), calls=%async_computation.24 | async-start | bytes 147456 | tf_op jit(solution)/shard_map/reduce_scatter | solution.py:909
  (70 other events, 2121.2 us)
Sparse Core Ops, SparseCore 0:
  9.6 31.8 all-gather.18
  43.7 64.0 all-gather.16
  110.0 26.6 all-gather.20
  176.1 77.4 all-gather.28
  267.0 77.0 all-gather.24
  345.6 79.3 all-gather.22
  426.5 79.4 all-gather.30
  597.3 32.4 all-gather.26
  923.0 76.2 reduce-scatter.11
  1021.9 76.2 reduce-scatter.13
  1121.0 76.1 reduce-scatter.7
  1215.0 79.0 reduce-scatter.9
  1384.6 33.6 reduce-scatter.17
  1473.7 67.4 reduce-scatter.15
  1589.9 26.9 reduce-scatter.19

commit v3 on v2

v3 whole, which is shorter than its diff:
```python
import functools

import jax
import jax.numpy as jnp
from jax import lax
from jax.experimental import pallas as pl
from jax.experimental.pallas import tpu as pltpu
from jax.sharding import Mesh, PartitionSpec as P

D = 2048
HS = 128
E = 64
TOPK = 8
SEQ = 2048
EPSILON = 1e-06
SCALE = HS ** (-0.5)
CHUNKS = 2
GAIN_ROWS = 16
TOKENS_AXES = ("z", "core")
SWAP_AXES = ("row", "core")
ALL_AXES = ("row", "z", "core")
BF = jnp.bfloat16
F32 = jnp.float32
VMEM_BYTES = 60 * 1024 * 1024


def call(body, grid, in_specs, out_specs, out_shape, scratch=(), prefetch=0, name=None, deps=(), flops=0):
    deps = tuple(deps)

    def without_deps(*refs):
        body(*refs[:prefetch], *refs[prefetch + len(deps) :])

    kernel = pl.pallas_call(
        without_deps,
        out_shape=out_shape,
        grid_spec=pltpu.PrefetchScalarGridSpec(
            num_scalar_prefetch=prefetch,
            grid=grid,
            in_specs=[pl.BlockSpec(memory_space=pl.ANY)] * len(deps) + list(in_specs),
            out_specs=out_specs,
            scratch_shapes=list(scratch),
        ),
        compiler_params=pltpu.CompilerParams(
            dimension_semantics=("arbitrary",) * len(grid), vmem_limit_bytes=VMEM_BYTES
        ),
        cost_estimate=pl.CostEstimate(flops=flops, bytes_accessed=0, transcendentals=0),
        name=name,
    )
    return lambda *args: kernel(*args[:prefetch], *deps, *args[prefetch:])


def shape(dims, dtype):
    return jax.ShapeDtypeStruct(dims, dtype)


def dot(left, right, left_dim=1, right_dim=0):
    return lax.dot_general(
        left, right, (((left_dim,), (right_dim,)), ((), ())), preferred_element_type=F32
    )


def rotary_tables():
    half_size = HS // 2
    inverse = 50000.0 ** (-(jnp.arange(half_size, dtype=F32) * 2.0) / HS)
    angles = jnp.arange(SEQ, dtype=F32)[:, None] * inverse[None, :]
    cosine, sine = jnp.cos(angles), jnp.sin(angles)
    return (
        jnp.concatenate([cosine, cosine], axis=1),
        jnp.concatenate([-sine, sine], axis=1),
    )


def project_body(starts, *refs):
    count = starts.shape[0]
    x_refs, gain_refs, refs = refs[:count], refs[count : 2 * count], refs[2 * count :]
    w_ref, cos_ref, sin_ref, hg_ref, normed_ref, heads_ref, raw_ref, factor_ref = refs
    width = x_refs[0].shape[1]
    square = sum(
        jnp.sum(jnp.square(x_ref[...].astype(F32)), axis=1, keepdims=True) for x_ref in x_refs
    )
    factor = lax.rsqrt(square / (width * count) + EPSILON)
    factor_ref[...] = factor
    raw = None
    for index, x_ref in enumerate(x_refs):
        features = pl.ds(pl.multiple_of(starts[index], width), width)
        gain = gain_refs[index][0:1, :].astype(F32)
        normed = (x_ref[...].astype(F32) * factor * gain).astype(BF)
        normed_ref[:, features] = normed
        part = dot(normed, w_ref[features, :])
        raw = part if raw is None else raw + part
    turned = raw_ref.shape[1]
    raw_ref[...] = raw[:, :turned]
    cosine, sine = cos_ref[...], sin_ref[...]
    for head in range(turned // HS):
        part = raw[:, head * HS : (head + 1) * HS]
        unit = part * lax.rsqrt(jnp.mean(part * part, axis=1, keepdims=True) + EPSILON)
        scaled = unit * hg_ref[:, head * HS : (head + 1) * HS]
        heads_ref[:, head * HS : (head + 1) * HS] = (
            scaled * cosine + pltpu.roll(scaled, HS // 2, 1) * sine
        ).astype(BF)
    heads_ref[:, turned:] = raw[:, turned:].astype(BF)


def project(starts, pieces, weights, cosine, sine, head_gains, deps=()):
    tokens, piece = cosine.shape[0], pieces[0].shape[1]
    width, columns = weights.shape
    turned = columns // 3 * 2
    tile = 256
    own = lambda t, s: (t, 0)
    whole = lambda t, s: (0, 0)
    return call(
        project_body,
        (tokens // tile,),
        [pl.BlockSpec((tile, piece), own)] * len(pieces)
        + [pl.BlockSpec((GAIN_ROWS, piece), lambda t, s: (tokens // GAIN_ROWS, 0))] * len(pieces)
        + [
            pl.BlockSpec((width, columns), whole),
            pl.BlockSpec((tile, HS), own),
            pl.BlockSpec((tile, HS), own),
            pl.BlockSpec((1, turned), whole),
        ],
        [
            pl.BlockSpec((tile, width), own),
            pl.BlockSpec((tile, columns), own),
            pl.BlockSpec((tile, turned), own),
            pl.BlockSpec((tile, 1), own),
        ],
        [
            shape((tokens, width), BF),
            shape((tokens, columns), BF),
            shape((tokens, turned), F32),
            shape((tokens, 1), F32),
        ],
        prefetch=1,
        name="project",
        deps=deps,
    )(starts, *pieces, *pieces, weights, cosine, sine, head_gains)


def mix_back_body(starts, *refs):
    count = starts.shape[0]
    g_refs, (w_ref, out_ref) = refs[:count], refs[count:]
    width = g_refs[0].shape[1]
    total = None
    for index, g_ref in enumerate(g_refs):
        part = dot(g_ref[...], w_ref[pl.ds(pl.multiple_of(starts[index], width), width), :])
        total = part if total is None else total + part
    out_ref[...] = total.astype(BF)


def mix_back(starts, pieces, weights, deps=()):
    tokens, piece = pieces[0].shape
    width, columns = weights.shape
    tile = 256
    return call(
        mix_back_body,
        (tokens // tile,),
        [pl.BlockSpec((tile, piece), lambda t, s: (t, 0))] * len(pieces)
        + [pl.BlockSpec((width, columns), lambda t, s: (0, 0))],
        pl.BlockSpec((tile, columns), lambda t, s: (t, 0)),
        shape((tokens, columns), BF),
        prefetch=1,
        name="mix_back",
        deps=deps,
    )(starts, *pieces, weights)


def projection_grad_body(starts, *refs):
    count = starts.shape[0]
    g_refs, (mixed_ref, out_ref, total_ref) = refs[:count], refs[count:]
    width = g_refs[0].shape[1]

    @pl.when(pl.program_id(0) == 0)
    def _():
        total_ref[...] = jnp.zeros_like(total_ref)

    for index, g_ref in enumerate(g_refs):
        rows = pl.ds(pl.multiple_of(starts[index], width), width)
        total_ref[rows, :] += dot(g_ref[...], mixed_ref[...], 0, 0)

    @pl.when(pl.program_id(0) == pl.num_programs(0) - 1)
    def _():
        out_ref[...] = total_ref[...].astype(BF)


def projection_grad(starts, pieces, mixed, deps=()):
    tokens, piece = pieces[0].shape
    columns = mixed.shape[1]
    width = piece * len(pieces)
    tile = 512
    return call(
        projection_grad_body,
        (tokens // tile,),
        [pl.BlockSpec((tile, piece), lambda t, s: (t, 0))] * len(pieces)
        + [pl.BlockSpec((tile, columns), lambda t, s: (t, 0))],
        pl.BlockSpec((width, columns), lambda t, s: (0, 0)),
        shape((width, columns), BF),
        scratch=[pltpu.VMEM((width, columns), F32)],
        prefetch=1,
        name="projection_grad",
        deps=deps,
    )(starts, *pieces, mixed)


def permute(values, mask):
    return lax.ppermute(values, "row", [(i, i ^ mask) for i in range(4)])


def row_gather(values):
    width = values.shape[1]
    if lax.axis_size("row") != 4:
        return [lax.all_gather(values, "row", axis=1, tiled=True)], jnp.zeros((1,), jnp.int32)
    half = width // 2
    left, right = values[:, :half], values[:, half:]
    left_1, right_2 = permute(left, 1), permute(right, 2)
    left_2, right_1 = permute(left, 2), permute(right, 1)
    left_3, right_3 = permute(left_1, 2), permute(right_2, 1)
    me = lax.axis_index("row")
    starts = jnp.stack(
        [(me ^ mask) * width + side * half for mask in range(4) for side in range(2)]
    ).astype(jnp.int32)
    return [left, right, left_1, right_1, left_2, right_2, left_3, right_3], starts


def small_row_gather(values):
    if lax.axis_size("row") != 4:
        return lax.all_gather(values, "row", axis=0)
    stacked = jnp.stack([values] + [permute(values, mask) for mask in (1, 2, 3)])
    return jnp.take(stacked, lax.axis_index("row") ^ jnp.arange(4), axis=0)


def small_row_swap(blocks):
    if lax.axis_size("row") != 4:
        return lax.all_to_all(blocks, "row", 0, 0, tiled=True)
    me = lax.axis_index("row")
    near = jnp.take(blocks, me ^ jnp.arange(4), axis=0)
    stacked = jnp.stack([near[0]] + [permute(near[mask], mask) for mask in (1, 2, 3)])
    return jnp.take(stacked, me ^ jnp.arange(4), axis=0)


def token_scatter(values):
    z_count, core_count = lax.axis_size("z"), lax.axis_size("core")
    rows, columns = values.shape
    blocks = values.reshape(z_count, core_count, rows // (z_count * core_count), columns)
    core = lax.axis_index("core")
    keep = lax.dynamic_index_in_dim(blocks, core, 1, keepdims=False)
    give = lax.dynamic_index_in_dim(blocks, 1 - core, 1, keepdims=False)
    got = lax.ppermute(give, "core", [(0, 1), (1, 0)])
    summed = (keep.astype(F32) + got.astype(F32)).astype(values.dtype)
    return lax.psum_scatter(summed.reshape(-1, columns), "z", scatter_dimension=0, tiled=True)


def after(value, *others):
    others = [other for other in others if other is not None]
    return pl.pallas_call(
        lambda *refs: None,
        out_shape=shape(value.shape, value.dtype),
        in_specs=[pl.BlockSpec(memory_space=pl.ANY)] * (1 + len(others)),
        out_specs=pl.BlockSpec(memory_space=pl.ANY),
        input_output_aliases={0: 0},
        cost_estimate=pl.CostEstimate(flops=0, bytes_accessed=0, transcendentals=0),
        name="after",
    )(value, *others)


def row_scatter_order(weights):
    if lax.axis_size("row") != 4:
        return weights
    width = weights.shape[0] // 4
    half = width // 2
    me = lax.axis_index("row")
    order = [(1, 0), (3, 0), (2, 1), (3, 1), (2, 0), (1, 1), (0, 0), (0, 1)]
    return jnp.concatenate(
        [
            lax.dynamic_slice_in_dim(weights, (me ^ mask) * width + side * half, half, 0)
            for mask, side in order
        ],
        axis=0,
    )


def row_scatter(left, ordered):
    if lax.axis_size("row") != 4:
        return lax.psum_scatter(
            dot(left, ordered, 1, 1).astype(BF), "row", scatter_dimension=1, tiled=True
        ).astype(F32), ()
    width = ordered.shape[0] // 4
    half = width // 2
    part = lambda index: dot(left, ordered[index * width : (index + 1) * width], 1, 1)
    sent = [part(0).astype(BF), part(1).astype(BF)]
    from_x = permute(sent[0], 1).astype(F32)
    from_y = permute(sent[1], 2).astype(F32)
    onward, own = part(2), part(3)
    last_left = permute((onward[:, :half] + from_x[:, half:]).astype(BF), 2).astype(F32)
    last_right = permute((onward[:, half:] + from_y[:, half:]).astype(BF), 1).astype(F32)
    total = jnp.concatenate(
        [
            own[:, :half] + from_x[:, :half] + last_left,
            own[:, half:] + from_y[:, :half] + last_right,
        ],
        axis=1,
    )
    return total, sent


QUERY_TILE = 256
KEY_TILE = 256
EXP2_SCALE = SCALE * 1.4426950408889634


def key_ranges(segment):
    first = segment[::QUERY_TILE]
    last = segment[QUERY_TILE - 1 :: QUERY_TILE]
    key_first = segment[::KEY_TILE]
    key_last = segment[KEY_TILE - 1 :: KEY_TILE]
    meets = (key_first[None, :] <= last[:, None]) & (key_last[None, :] >= first[:, None])
    order = jnp.arange(meets.shape[1], dtype=jnp.int32)[None, :]
    low = jnp.min(jnp.where(meets, order, meets.shape[1]), axis=1)
    high = jnp.max(jnp.where(meets, order + 1, 0), axis=1)
    return low.astype(jnp.int32), high.astype(jnp.int32)


def key_rows(step):
    return pl.ds(pl.multiple_of(step * KEY_TILE, KEY_TILE), KEY_TILE)


def head(ref, index, rows=slice(None)):
    return ref[rows, index * HS : (index + 1) * HS]


def attend_body(low, high, q_ref, k_ref, v_ref, qs_ref, ks_ref, out_ref, sum_ref):
    block = pl.program_id(0)
    count = q_ref.shape[1] // HS
    query_docs = qs_ref[...]

    def step(index, state):
        rows = key_rows(index)
        allowed = query_docs == ks_ref[:, rows]
        scores = [dot(head(q_ref, h), head(k_ref, h, rows), 1, 1) for h in range(count)]
        raised = [jnp.where(allowed, jnp.exp2(each * EXP2_SCALE), 0.0) for each in scores]
        return tuple(
            (
                total + jnp.sum(each, axis=1, keepdims=True),
                mixed + dot(each.astype(BF), head(v_ref, h, rows)),
            )
            for h, (each, (total, mixed)) in enumerate(zip(raised, state))
        )

    state = lax.fori_loop(
        low[block],
        high[block],
        step,
        ((jnp.zeros((QUERY_TILE, 1), F32), jnp.zeros((QUERY_TILE, HS), F32)),) * count,
    )
    for h, (total, mixed) in enumerate(state):
        out_ref[:, h * HS : (h + 1) * HS] = (mixed / total).astype(BF)
        sum_ref[h] = total


def attend(heads, segment, low, high):
    tokens, columns = heads.shape
    width = columns // 3
    count = width // HS
    return call(
        attend_body,
        (tokens // QUERY_TILE,),
        [
            pl.BlockSpec((QUERY_TILE, width), lambda b, lo, hi: (b, 0)),
            pl.BlockSpec((tokens, width), lambda b, lo, hi: (0, 1)),
            pl.BlockSpec((tokens, width), lambda b, lo, hi: (0, 2)),
            pl.BlockSpec((QUERY_TILE, 1), lambda b, lo, hi: (b, 0)),
            pl.BlockSpec((1, tokens), lambda b, lo, hi: (0, 0)),
        ],
        [
            pl.BlockSpec((QUERY_TILE, width), lambda b, lo, hi: (b, 0)),
            pl.BlockSpec((count, QUERY_TILE, 1), lambda b, lo, hi: (0, b, 0)),
        ],
        [shape((tokens, width), BF), shape((count, tokens, 1), F32)],
        prefetch=2,
        name="attend",
    )(low, high, heads, heads, heads, segment[:, None], segment[None, :])


def head_back(grad, raw, gain, cosine, sine):
    turned = grad * cosine - pltpu.roll(grad, HS // 2, 1) * sine
    factor = lax.rsqrt(jnp.mean(raw * raw, axis=1, keepdims=True) + EPSILON)
    unit = raw * factor
    gain_part = jnp.sum(turned * unit, axis=0, keepdims=True)
    pulled = turned * gain
    inner = jnp.mean(pulled * unit, axis=1, keepdims=True)
    return (pulled - unit * inner) * factor, gain_part


def attend_back_body(
    low, high, q_ref, k_ref, v_ref, g_ref, o_ref, s_ref, qs_ref, ks_ref, qr_ref, kr_ref,
    cos_ref, sin_ref, hg_ref, grad_ref, gain_ref, along_ref, keys_ref, values_ref,
    inner_ref,
):
    block = pl.program_id(0)
    count = q_ref.shape[1] // HS

    @pl.when(block == 0)
    def _():
        keys_ref[...] = jnp.zeros_like(keys_ref)
        values_ref[...] = jnp.zeros_like(values_ref)
        gain_ref[...] = jnp.zeros_like(gain_ref)

    for h in range(count):
        inner_ref[h] = jnp.sum(
            head(g_ref, h).astype(F32) * head(o_ref, h).astype(F32), axis=1, keepdims=True
        )

    def step(index, state):
        rows = key_rows(index)
        allowed = qs_ref[...] == ks_ref[:, rows]
        scores = [dot(head(q_ref, h), head(k_ref, h, rows), 1, 1) for h in range(count)]
        grads = [dot(head(g_ref, h), head(v_ref, h, rows), 1, 1) for h in range(count)]
        new = []
        for h in range(count):
            columns = slice(h * HS, (h + 1) * HS)
            weights = jnp.where(
                allowed, jnp.exp2(scores[h] * EXP2_SCALE) * (1.0 / s_ref[h]), 0.0
            )
            grad_scores = (weights * (grads[h] - inner_ref[h])).astype(BF)
            values_ref[rows, columns] += dot(weights.astype(BF), head(g_ref, h), 0, 0)
            keys_ref[rows, columns] += dot(grad_scores, head(q_ref, h), 0, 0)
            new.append(state[h] + dot(grad_scores, head(k_ref, h, rows)))
        return tuple(new)

    grad_queries = lax.fori_loop(
        low[block], high[block], step, (jnp.zeros((QUERY_TILE, HS), F32),) * count
    )
    rows = pl.ds(pl.multiple_of(block * QUERY_TILE, QUERY_TILE), QUERY_TILE)
    along = jnp.zeros((QUERY_TILE, 1), F32)
    for h, grad_query in enumerate(grad_queries):
        back, part = head_back(
            grad_query * SCALE, head(qr_ref, h), hg_ref[0:1, :], cos_ref[rows, :], sin_ref[rows, :]
        )
        grad_ref[rows, h * HS : (h + 1) * HS] = back.astype(BF)
        gain_ref[0:1, :] += part
        along += jnp.sum(back * head(qr_ref, h), axis=1, keepdims=True)
    along_ref[rows, :] = along

    @pl.when(block == pl.num_programs(0) - 1)
    def _():
        along_ref[...] += jnp.sum(values_ref[...] * v_ref[...].astype(F32), axis=1, keepdims=True)
        for h in range(count):
            back, part = head_back(
                head(keys_ref, h) * SCALE, head(kr_ref, h), hg_ref[1:2, :], cos_ref[...],
                sin_ref[...],
            )
            grad_ref[:, (count + h) * HS : (count + h + 1) * HS] = back.astype(BF)
            gain_ref[1:2, :] += part
            along_ref[...] += jnp.sum(back * head(kr_ref, h), axis=1, keepdims=True)
        grad_ref[:, 2 * count * HS :] = values_ref[...].astype(BF)


def attend_back(
    heads, grad_mixed, mixed, sums, segment, low, high, raw, cosine, sine, gains, deps=()
):
    tokens, columns = heads.shape
    width = columns // 3
    count = width // HS
    whole = lambda b, lo, hi: (0, 0)
    tile = lambda b, lo, hi: (b, 0)
    return call(
        attend_back_body,
        (tokens // QUERY_TILE,),
        [
            pl.BlockSpec((QUERY_TILE, width), tile),
            pl.BlockSpec((tokens, width), lambda b, lo, hi: (0, 1)),
            pl.BlockSpec((tokens, width), lambda b, lo, hi: (0, 2)),
            pl.BlockSpec((QUERY_TILE, width), tile),
            pl.BlockSpec((QUERY_TILE, width), tile),
            pl.BlockSpec((count, QUERY_TILE, 1), lambda b, lo, hi: (0, b, 0)),
            pl.BlockSpec((QUERY_TILE, 1), tile),
            pl.BlockSpec((1, tokens), whole),
            pl.BlockSpec((QUERY_TILE, width), tile),
            pl.BlockSpec((tokens, width), lambda b, lo, hi: (0, 1)),
            pl.BlockSpec((tokens, HS), whole),
            pl.BlockSpec((tokens, HS), whole),
            pl.BlockSpec((2, HS), whole),
        ],
        [
            pl.BlockSpec((tokens, columns), whole),
            pl.BlockSpec((2, HS), whole),
            pl.BlockSpec((tokens, 1), whole),
        ],
        [shape((tokens, columns), BF), shape((2, HS), F32), shape((tokens, 1), F32)],
        scratch=[
            pltpu.VMEM((tokens, width), F32),
            pltpu.VMEM((tokens, width), F32),
            pltpu.VMEM((count, QUERY_TILE, 1), F32),
        ],
        prefetch=2,
        name="attend_back",
        deps=deps,
    )(
        low, high, heads, heads, heads, grad_mixed, mixed, sums, segment[:, None],
        segment[None, :], raw, raw, cosine, sine, gains,
    )


def dispatch_body(slot_ref, x_ref, out_ref):
    local, capacity = out_ref.shape[1], out_ref.shape[3]
    tokens = x_ref.shape[1]
    rows = x_ref[0]
    order = lax.broadcasted_iota(jnp.int32, (capacity, tokens), 0)
    for index in range(local):
        hot = jnp.where(order == slot_ref[0, 0, index : index + 1, :], 1.0, 0.0).astype(BF)
        out_ref[0, index, 0] = dot(hot, rows).astype(BF)


def dispatch(slots, rows, capacity, deps=()):
    groups, targets, local, tokens = slots.shape
    features = rows.shape[2]
    return call(
        dispatch_body,
        (groups, targets),
        [
            pl.BlockSpec((1, 1, local, tokens), lambda g, d: (g, d, 0, 0)),
            pl.BlockSpec((1, tokens, features), lambda g, d: (g, 0, 0)),
        ],
        pl.BlockSpec((1, local, 1, capacity, features), lambda g, d: (d, 0, g, 0, 0)),
        shape((targets, local, groups, capacity, features), BF),
        name="dispatch",
        deps=deps,
    )(slots, rows)


def combine_body(*refs):
    slot_ref, rows_refs, out_ref = refs[0], refs[1:-1], refs[-1]
    targets, local, _, capacity, features = rows_refs[0].shape
    total_local = local * len(rows_refs)
    tile = out_ref.shape[1]
    order = lax.broadcasted_iota(jnp.int32, (tile, capacity), 1)
    slots = slot_ref[0]
    total = jnp.zeros((tile, features), F32)
    for target in range(targets):
        for part, rows_ref in enumerate(rows_refs):
            first = target * total_local + part * local
            hot = jnp.concatenate(
                [
                    jnp.where(order == slots[:, first + i : first + i + 1], 1.0, 0.0).astype(BF)
                    for i in range(local)
                ],
                axis=1,
            )
            total = total + dot(hot, rows_ref[target].reshape(local * capacity, features))
    out_ref[0] = total.astype(BF)


def combine(slots_by_token, parts, chunk, features, deps=()):
    groups, tokens, experts = slots_by_token.shape
    targets, local, _, capacity, _ = parts[0].shape
    tile = 512
    return call(
        combine_body,
        (groups, tokens // tile),
        [pl.BlockSpec((1, tile, experts), lambda g, t: (g, t, 0))]
        + [
            pl.BlockSpec(
                (targets, local, 1, capacity, features), lambda g, t: (0, 0, g, 0, chunk)
            )
        ]
        * len(parts),
        pl.BlockSpec((1, tile, features), lambda g, t: (g, t, 0)),
        shape((groups, tokens, features), BF),
        name="combine",
        flops=2 * groups * experts * capacity * tokens * features,
        deps=deps,
    )(slots_by_token, *parts)


def block_rows(ref, row=0):
    _, cores, _, groups, capacity, features = ref.shape
    return ref[row].reshape(cores * groups * capacity, features)


def expert_body(x_ref, c_ref, gate_w, up_w, down_w, prob_ref, act_ref, gate_out, up_out):
    rows, width = x_ref.shape[0], x_ref.shape[-1]
    prob = prob_ref[0]
    gate = up = grad = None
    for row in range(rows):
        features = pl.ds(row * width, width)
        x = block_rows(x_ref, row)
        c = (block_rows(c_ref, row).astype(F32) * prob).astype(BF)
        gate_part = dot(x, gate_w[0, features, :])
        up_part = dot(x, up_w[0, features, :])
        grad_part = dot(c, down_w[0, features, :])
        gate = gate_part if gate is None else gate + gate_part
        up = up_part if up is None else up + up_part
        grad = grad_part if grad is None else grad + grad_part
    squashed = 1.0 / (1.0 + jnp.exp(-gate))
    act_ref[...] = (gate * squashed * up).astype(BF)
    gate_out[...] = (grad * up * squashed * (1.0 + gate * (1.0 - squashed))).astype(BF)
    up_out[...] = (grad * gate * squashed).astype(BF)


def expert(index, rows, cots, gate_weight, up_weight, down_weight, prob):
    row_count, cores, _, groups, capacity, width = rows.shape
    _, features, hidden = gate_weight.shape
    slots = groups * capacity
    tile = min(512, hidden, 512 * 1024 // slots)
    block = (row_count, 1, 1, groups, capacity, width)
    row_spec = pl.BlockSpec(block, lambda n, k: (0, k, 0, 0, 0, 0))
    w_spec = pl.BlockSpec((1, features, tile), lambda n, k: (index, 0, n))
    out_spec = pl.BlockSpec((slots, tile), lambda n, k: (k, n))
    return call(
        expert_body,
        (hidden // tile, cores),
        [row_spec, row_spec, w_spec, w_spec, w_spec]
        + [pl.BlockSpec((1, slots, 1), lambda n, k: (index, k, 0))],
        [out_spec] * 3,
        [shape((cores * slots, hidden), BF)] * 3,
        name="expert",
    )(rows, cots, gate_weight, up_weight, down_weight, prob)


def produce_body(act_ref, w_ref, prob_ref, c_ref, *refs):
    out_refs, inner_ref = refs[-CHUNKS - 1 : -1], refs[-1]
    width = out_refs[0].shape[-1]

    @pl.when(pl.program_id(1) == 0)
    def _():
        inner_ref[...] = jnp.zeros_like(inner_ref)

    made = dot(act_ref[...], w_ref[0], 1, 1)
    inner_ref[...] += jnp.sum(made * block_rows(c_ref).astype(F32), axis=1, keepdims=True)
    weighted = (made * prob_ref[0]).astype(BF)
    for chunk, out_ref in enumerate(out_refs):
        out_ref[...] = weighted[:, chunk * width : (chunk + 1) * width].reshape(out_ref.shape)


def produce(index, activated, down_weight, prob, cots, dims, buffers):
    rows, cores, local, groups, capacity, width = dims
    hidden = activated.shape[1]
    slots = groups * capacity
    given = () if buffers is None else tuple(buffers)
    outs = pl.pallas_call(
        produce_body,
        out_shape=[shape(dims, BF)] * CHUNKS + [shape((cores * slots, 1), F32)],
        grid=(cores, rows),
        in_specs=[
            pl.BlockSpec((slots, hidden), lambda k, r: (k, 0)),
            pl.BlockSpec((1, width * CHUNKS, hidden), lambda k, r: (index, r, 0)),
            pl.BlockSpec((1, slots, 1), lambda k, r: (index, k, 0)),
            pl.BlockSpec(
                (1, 1, 1, groups, capacity, width * CHUNKS), lambda k, r: (r, k, 0, 0, 0, 0)
            ),
        ]
        + [pl.BlockSpec(memory_space=pl.ANY)] * len(given),
        out_specs=[
            pl.BlockSpec(
                (1, 1, 1, groups, capacity, width), lambda k, r: (r, k, index, 0, 0, 0)
            )
        ]
        * CHUNKS
        + [pl.BlockSpec((slots, 1), lambda k, r: (k, 0))],
        input_output_aliases={4 + chunk: chunk for chunk in range(len(given))},
        compiler_params=pltpu.CompilerParams(
            dimension_semantics=("arbitrary",) * 2, vmem_limit_bytes=VMEM_BYTES
        ),
        cost_estimate=pl.CostEstimate(
            flops=2 * cores * slots * D * hidden,
            bytes_accessed=2 * D * hidden + 8 * cores * slots * D,
            transcendentals=0,
        ),
        name="produce",
    )(activated, down_weight, prob, cots, *given)
    return outs[:CHUNKS], outs[CHUNKS]


def held_while(expert_index, last):
    return lambda i, r: jnp.where(i == expert_index, r, jnp.where(i < expert_index, 0, last))


def down_grad_body(*refs):
    prob_ref, refs = refs[0], refs[1:]
    local = len(refs) // 2
    c_refs, act_refs, out_ref = refs[:local], refs[local:-1], refs[-1]
    for index in range(local):

        @pl.when(pl.program_id(0) == index)
        def _():
            c = (block_rows(c_refs[index]).astype(F32) * prob_ref[0]).astype(BF)
            out_ref[0] = dot(c, act_refs[index][...], 0, 0)


def row_specs(local, shape_of):
    rows, cores, _, groups, capacity, width = shape_of

    def spec(index):
        where = held_while(index, rows - 1)
        return pl.BlockSpec(
            (1, cores, 1, groups, capacity, width), lambda i, r: (where(i, r), 0, 0, 0, 0, 0)
        )

    return [spec(index) for index in range(local)]


def down_grad(cots, prob, activated, deps=()):
    rows, cores, _, groups, capacity, width = cots[0].shape
    slots, hidden = activated[0].shape
    local = len(cots)
    return call(
        down_grad_body,
        (local, rows),
        [pl.BlockSpec((1, slots, 1), lambda i, r: (i, 0, 0))]
        + row_specs(local, cots[0].shape)
        + [pl.BlockSpec((slots, hidden), lambda i, r: (0, 0))] * local,
        pl.BlockSpec((1, width, hidden), lambda i, r: (i, r, 0)),
        shape((local, rows * width, hidden), F32),
        name="down_grad",
        flops=2 * local * slots * D * hidden,
        deps=deps,
    )(prob, *cots, *activated)


def gate_grad_body(*refs):
    local = (len(refs) - 2) // 3
    x_refs, gate_refs, up_refs = refs[:local], refs[local : 2 * local], refs[2 * local : -2]
    gate_out, up_out = refs[-2:]
    for index in range(local):

        @pl.when(pl.program_id(0) == index)
        def _():
            x = block_rows(x_refs[index])
            gate_out[0] = dot(x, gate_refs[index][...], 0, 0)
            up_out[0] = dot(x, up_refs[index][...], 0, 0)


def gate_grad(parts, grad_gate_pre, grad_up_pre, deps=()):
    rows, cores, _, groups, capacity, width = parts[0].shape
    slots, hidden = grad_gate_pre[0].shape
    local = len(parts)
    wide = pl.BlockSpec((slots, hidden), lambda i, r: (0, 0))
    out = pl.BlockSpec((1, width, hidden), lambda i, r: (i, r, 0))
    return call(
        gate_grad_body,
        (local, rows),
        row_specs(local, parts[0].shape) + [wide] * (2 * local),
        [out, out],
        [shape((local, rows * width, hidden), F32)] * 2,
        name="gate_grad",
        deps=deps,
    )(*parts, *grad_gate_pre, *grad_up_pre)


def rows_back_body(gate_ref, up_ref, gate_w, up_w, *refs):
    out_ref = refs[-1]
    made = dot(gate_ref[...], gate_w[0], 1, 1) + dot(up_ref[...], up_w[0], 1, 1)
    out_ref[...] = made.astype(BF).reshape(out_ref.shape)


def rows_back(
    index, grad_gate_pre, grad_up_pre, gate_weight, up_weight, chunk, dims, buffer, deps=()
):
    rows, cores, local, groups, capacity, width = dims
    hidden = gate_weight.shape[2]
    slots = groups * capacity
    pre = pl.BlockSpec((slots, hidden), lambda k, r: (k, 0))
    weight = pl.BlockSpec((1, width, hidden), lambda k, r: (index, r * CHUNKS + chunk, 0))
    given = () if buffer is None else (buffer,)
    return pl.pallas_call(
        rows_back_body,
        out_shape=shape(dims, BF),
        grid=(cores, rows),
        in_specs=[pre, pre, weight, weight]
        + [pl.BlockSpec(memory_space=pl.ANY)] * len(given + tuple(deps)),
        out_specs=pl.BlockSpec(
            (1, 1, 1, groups, capacity, width), lambda k, r: (r, k, index, 0, 0, 0)
        ),
        input_output_aliases={4: 0} if given else {},
        compiler_params=pltpu.CompilerParams(
            dimension_semantics=("arbitrary",) * 2, vmem_limit_bytes=VMEM_BYTES
        ),
        cost_estimate=pl.CostEstimate(
            flops=4 * cores * slots * width * rows * hidden,
            bytes_accessed=4 * rows * width * hidden + 6 * cores * slots * width * rows,
            transcendentals=0,
        ),
        name="rows_back",
    )(grad_gate_pre, grad_up_pre, gate_weight, up_weight, *given, *deps)


def swap(rows):
    return lax.all_to_all(rows, SWAP_AXES, split_axis=0, concat_axis=0, tiled=True)


def slot_positions(routes, ranks, capacity):
    experts = jnp.arange(E, dtype=jnp.int32)
    member = jnp.any(routes.T[:, None, :] == experts[None, :, None], axis=0)
    earlier = (ranks[:, None] < ranks[None, :]).astype(BF)
    position = jnp.dot(member.astype(BF), earlier, preferred_element_type=F32)
    return jnp.where(member & (position < capacity), position, -1.0)


def per_device(
    hidden_in,
    attention_gain,
    query_weight,
    key_weight,
    value_weight,
    projection,
    query_gain,
    key_gain,
    feedforward_gain,
    router_weight,
    gate_weight,
    up_weight,
    down_weight,
    segments,
    routes,
    priority,
    cotangent,
):
    tokens, width_here = hidden_in.shape
    row_count = lax.axis_size("row")
    z_count = lax.axis_size("z")
    core_count = lax.axis_size("core")
    local = gate_weight.shape[0]
    piece_count = row_count * z_count * core_count * local
    pieces = max(1, piece_count // E)
    capacity = tokens * TOPK // E
    width = width_here // CHUNKS
    row_index = lax.axis_index("row")
    z_index = lax.axis_index("z")
    core_index = lax.axis_index("core")
    head_columns = query_weight.shape[1]
    experts_here = E // row_count
    head_count = head_columns // HS

    hidden_pieces, hidden_starts = row_gather(
        jnp.concatenate(
            [hidden_in, jnp.broadcast_to(attention_gain[None, :], (GAIN_ROWS, width_here))], axis=0
        )
    )
    qkv_full = lax.all_gather(
        jnp.concatenate([query_weight, key_weight, value_weight], axis=1),
        TOKENS_AXES,
        axis=0,
        tiled=True,
    )
    with_router = lax.all_gather(
        jnp.concatenate([projection, router_weight], axis=1),
        TOKENS_AXES,
        axis=0,
        tiled=True,
    )
    projection_full = with_router[:, :head_columns]
    router_rows = with_router[:, head_columns:].reshape(row_count, width_here, -1)
    router_here = jnp.swapaxes(small_row_swap(router_rows), 1, 2).reshape(E, width_here)

    position = slot_positions(routes, priority[0], capacity)
    by_piece = jnp.repeat(position.astype(BF), pieces, axis=0).reshape(
        row_count, z_count, core_count * local, tokens
    )
    mine = lax.all_to_all(jnp.swapaxes(by_piece, 0, 1), "z", 0, 0, tiled=True).astype(jnp.int32)
    slots = mine.reshape(z_count, row_count * core_count, local, tokens)
    slots_by_token = jnp.swapaxes(
        mine.reshape(z_count, row_count * core_count * local, tokens), 1, 2
    )
    dims = (row_count, core_count, local, z_count, capacity, width)

    expert_dims = (row_count, core_count, 1, z_count, capacity, width_here)
    def scatter_back(summed):
        return lax.psum_scatter(summed, "z", scatter_dimension=0, tiled=True).reshape(
            tokens, width
        )

    spread_cots = lax.all_gather(after(cotangent, *hidden_pieces[2:6]), "z", axis=0)

    cosine, sine = rotary_tables()
    first_gain = attention_gain.astype(F32)
    second_gain = feedforward_gain.astype(F32)
    head_gains = jnp.stack([query_gain, key_gain]).astype(F32)
    residual = hidden_in.astype(F32)
    normed_one, heads, raw, first_factor = project(
        hidden_starts,
        hidden_pieces,
        qkv_full,
        cosine,
        sine,
        jnp.repeat(head_gains, head_count, axis=0).reshape(1, -1),
        (mine, router_here),
    )
    segment = segments[0]
    low, high = key_ranges(segment)
    mixed, sums = attend(heads, segment, low, high)
    middle = residual + row_scatter(mixed, row_scatter_order(projection_full))[0]
    second_factor = lax.rsqrt(lax.psum(jnp.sum(middle * middle, axis=1), "row") / D + EPSILON)[
        :, None
    ]
    normed_two = (middle * second_factor * second_gain).astype(BF)

    logits = jnp.sum(small_row_gather(dot(router_here, normed_two, 1, 1)), axis=0)
    raised = jnp.exp(logits)
    router_probs = raised / jnp.sum(raised, axis=0, keepdims=True)

    def send(spread, index, earlier, *before):
        picked = dispatch(slots[:, :, index : index + 1], spread, capacity, before)
        return swap(after(picked, *earlier) if earlier else picked).reshape(expert_dims)

    cots, rows = [], []
    for index in range(local):
        cots.append(send(spread_cots, index, cots[-1:] or [logits], normed_two))
    spread_rows = lax.all_gather(normed_two, "z", axis=0)
    for index in range(local):
        rows.append(send(spread_rows, index, [cots[-1]] + rows[-1:], cots[0]))
    own_slots = lax.dynamic_slice_in_dim(position, row_index * experts_here, experts_here, 0)
    own_probs = lax.dynamic_slice_in_dim(router_probs, row_index * experts_here, experts_here, 0)
    order = jnp.arange(capacity, dtype=jnp.int32).astype(F32)
    slot_prob = jnp.sum(
        jnp.where(own_slots[:, None, :] == order[None, :, None], own_probs[:, None, :], 0.0), axis=2
    )
    prob_groups = jnp.repeat(
        lax.all_gather(slot_prob, TOKENS_AXES, axis=0), pieces, axis=1
    ).reshape(z_count, core_count, z_count, core_count, local, capacity)
    prob_here = lax.dynamic_index_in_dim(
        lax.dynamic_index_in_dim(prob_groups, z_index, 2, keepdims=False),
        core_index,
        2,
        keepdims=False,
    )
    prob = jnp.transpose(prob_here, (2, 1, 0, 3)).reshape(
        local, core_count * z_count * capacity, 1
    )
    swapped_dims = (row_count * core_count,) + dims[2:]
    activated, grad_gate_pre, grad_up_pre = [], [], []
    buffers = [None] * CHUNKS
    for index in range(local):
        rows_here = rows[index]
        act, gate_pre, up_pre = expert(
            index, rows_here, cots[index], gate_weight, up_weight, down_weight, prob
        )
        activated.append(act)
        grad_gate_pre.append(gate_pre)
        grad_up_pre.append(up_pre)
        for chunk in range(CHUNKS):
            buffers[chunk] = rows_back(
                index, gate_pre, up_pre, gate_weight, up_weight, chunk, dims, buffers[chunk],
                buffers[:chunk] if index == local - 1 else (),
            )
    inners, made_buffers = [], None
    for index in range(local):
        made_buffers, inner = produce(
            index, activated[index], down_weight, prob, cots[index], dims, made_buffers
        )
        inners.append(inner)

    inner = jnp.stack(inners).reshape(local, core_count, z_count, capacity)
    to_groups = jnp.transpose(inner, (2, 1, 0, 3)).reshape(
        z_count * core_count, local * capacity
    )
    back_rows = [swap(buffers[0].reshape(swapped_dims))]
    of_group = lax.all_to_all(
        after(to_groups, back_rows[0]), TOKENS_AXES, 0, 0, tiled=True
    ).reshape(-1, capacity)
    slot_grads = jnp.sum(small_row_gather(of_group).reshape(E, pieces, capacity), axis=1)
    grad_down = down_grad(cots, prob, activated, inners)
    ready = after(buffers[1], grad_down)
    back_rows.append(swap(ready.reshape(swapped_dims)))
    grad_prob = jnp.sum(
        jnp.where(position[:, None, :] == order[None, :, None], slot_grads[:, :, None], 0.0), axis=1
    )
    grad_logits = (
        router_probs * (grad_prob - jnp.sum(router_probs * grad_prob, axis=0, keepdims=True))
    ).astype(BF)
    from_router = dot(grad_logits, router_here, 0, 0)
    first_sum = combine(slots_by_token, [back_rows[0]], 0, width, [ready])
    grad_gate, grad_up = gate_grad(rows, grad_gate_pre, grad_up_pre, [first_sum])
    first_sum = scatter_back(first_sum)
    second_sum = scatter_back(
        combine(slots_by_token, [back_rows[1]], 0, width, [grad_gate, first_sum])
    )
    grad_normed_two = from_router + jnp.concatenate(
        [first_sum, second_sum], axis=1
    ).astype(F32)
    router_part = dot(grad_logits, normed_two)
    router_swapped = lax.all_to_all(
        router_part.reshape(row_count, experts_here, width_here), "row", 0, 0, tiled=True
    )
    grad_router = lax.psum_scatter(
        jnp.swapaxes(router_swapped, 0, 1).reshape(experts_here, D),
        TOKENS_AXES,
        scatter_dimension=1,
        tiled=True,
    ).T

    scaled_two = grad_normed_two * second_gain
    second_inner = lax.psum(jnp.sum(scaled_two * middle, axis=1), "row")[:, None]
    grad_middle = (
        cotangent.astype(F32)
        + scaled_two * second_factor
        - middle * second_factor**3 * second_inner / D
    )
    grad_feedforward_gain = jnp.sum(grad_normed_two * middle * second_factor, axis=0)

    grad_branch = grad_middle.astype(BF)
    made_rows = [swap(after(made_buffers[0], back_rows[1], slot_grads).reshape(swapped_dims))]
    branch_pieces, branch_starts = row_gather(after(grad_branch, made_rows[0]))
    made_rows.append(swap(after(made_buffers[1], *branch_pieces).reshape(swapped_dims)))
    made_sums = [combine(slots_by_token, [made_rows[0]], 0, width, [grad_branch])]
    grad_mixed = mix_back(
        branch_starts, branch_pieces, projection_full, made_sums + [router_swapped]
    )
    grad_projection = projection_grad(branch_starts, branch_pieces, mixed, [grad_mixed])
    grad_raw, head_gain_grads, along = attend_back(
        heads, grad_mixed, mixed, sums, segment, low, high, raw, cosine, sine, head_gains,
        [grad_projection],
    )
    from_experts = [scatter_back(made_sums[0])]
    grad_raw = after(grad_raw, made_rows[1], from_experts[0])
    grad_first, sent = row_scatter(grad_raw, row_scatter_order(qkv_full))
    from_experts.append(
        scatter_back(combine(slots_by_token, [made_rows[1]], 0, width, sent))
    )
    small = jnp.concatenate([along.reshape(-1, HS), head_gain_grads], axis=0)
    small = jnp.sum(small_row_gather(small), axis=0)
    first_inner = small[:-2].reshape(-1, 1) / first_factor
    head_gain_grads = small[-2:]
    grad_qkv = dot(after(normed_one, *sent), grad_raw, 0, 0).astype(BF)
    scaled_one = grad_first * first_gain
    grad_input = (
        grad_middle + scaled_one * first_factor - residual * first_factor**3 * first_inner / D
    )
    grad_attention_gain = jnp.sum(grad_first * residual * first_factor, axis=0)

    grad_attention_gain, grad_feedforward_gain, head_gain_grads = lax.psum(
        (grad_attention_gain, grad_feedforward_gain, head_gain_grads), TOKENS_AXES
    )
    grad_projection = token_scatter(grad_projection).astype(F32)
    grad_qkv = token_scatter(grad_qkv).astype(F32)
    from_experts = jnp.concatenate(from_experts, axis=1).astype(F32)
    output = (after(middle, grad_first) + from_experts).astype(BF)
    return (
        output,
        grad_input,
        grad_attention_gain,
        grad_qkv[:, :head_columns],
        grad_qkv[:, head_columns : 2 * head_columns],
        grad_qkv[:, 2 * head_columns :],
        grad_projection,
        head_gain_grads[0],
        head_gain_grads[1],
        grad_feedforward_gain,
        grad_router,
        grad_gate,
        grad_up,
        grad_down,
    )


def solution(mesh):
    rows, columns = mesh.shape["row"], mesh.shape["col"]
    split_mesh = Mesh(
        mesh.devices.reshape(rows, columns // 2, 2), ("row", "z", "core")
    )
    both = P(TOKENS_AXES, "row")
    expert = P(ALL_AXES, None, None)
    grouped = P(TOKENS_AXES, None)
    return jax.shard_map(
        per_device,
        mesh=split_mesh,
        in_specs=(
            both, P("row"), both, both, both, both, P(), P(), P("row"), both,
            expert, expert, expert, grouped, grouped, grouped, both,
        ),
        out_specs=(
            both, both, P("row"), both, both, both, both, P(), P(), P("row"), both,
            expert, expert, expert,
        ),
        check_vma=False,
    )
```

time: 1680 us -> 1600 us (0.952)
  blocking collectives: 267 us -> 90.3 us
  waiting for transfers between devices: 525 us -> 571 us
    all_gather x4 -> x0, blocking collectives: 187 us -> none  [the longest x1 83.3 us: per_device(): lax.all_gather(lax.all_gather(router_weight.T, TOKENS_AXES, axis=1, tiled...]
    ppermute x20 -> x32, waiting for transfers between devices: 134 us -> 239 us  [permute(): return lax.ppermute(values, 'row', [(i, i ^ mask) for i in range(4)])]
    all_to_all x8, waiting for transfers between devices: 303 us -> 215 us  [swap(): lax.all_to_all(rows, SWAP_AXES, split_axis=0, concat_axis=0, tiled=True)]
    psum x1, blocking collectives: 8.41 us -> 41.2 us  [per_device(): lax.psum(jnp.sum(scaled_two * middle, axis=1), 'row')[:, None]]
    psum x2 -> x1, blocking collectives: 47.1 us -> 16.7 us  [per_device(): lax.psum((grad_attention_gain, grad_feedforward_gain, head_gain_grads), T...]
    reduce_scatter x6, waiting for transfers between devices: 0.08 us -> 29.3 us  [the longest x4 29.3 us: scatter_back(): lax.psum_scatter(summed, 'z', scatter_dimension=0, tiled=True)]
    reduce_scatter x1, waiting for transfers between devices: 0.01 us -> 26.1 us  [per_device(): lax.psum_scatter(jnp.swapaxes(router_swapped, 0, 1).reshape(experts_here,...]
    all_gather x7 -> x3, waiting for transfers between devices: 69.9 us -> 51.2 us  [the longest x1 51.2 us: per_device(): spread_rows = lax.all_gather(normed_two, 'z', axis=0)]
  transfers between devices with their start and end apart: 44 -> 55, of which waited for: 21 -> 34; matrix products, arithmetic and copies ran while one was open for 10% -> 11% of each run, Pallas kernels for 32% -> 30%
where the time goes in v3:
time: 1600 us; the launch traced here: 1580 us
  Pallas kernels  622 us (39%)
  waiting for transfers between devices  571 us (36%)
  blocking collectives  90.3 us (6%)
  other arithmetic  88.5 us (6%)
  starting transfers between devices  84.3 us (5%)
  matrix products  62.5 us (4%)
  local copies, waits for them, and re-layouts  49.7 us (3%)
    pallas_call x17, Pallas kernels, call(): return lambda *args: kernel(*args[:prefetch], *deps, *args[prefetch:])  524 us
    ppermute x32, waiting for transfers between devices, permute(): return lax.ppermute(values, 'row', [(i, i ^ mask) for i in range(4)])  239 us
    all_to_all x8, waiting for transfers between devices, swap(): lax.all_to_all(rows, SWAP_AXES, split_axis=0, concat_axis=0, tiled=True)  215 us
    pallas_call x4, Pallas kernels, rows_back(): pl.pallas_call(rows_back_body, out_shape=shape(dims, BF), grid=(cores, ro...  61.7 us
    dot_general x12, matrix products, dot(): lax.dot_general(left, right, (((left_dim,), (right_dim,)), ((), ())), pre...  58.7 us
    all_gather x1, waiting for transfers between devices, per_device(): spread_rows = lax.all_gather(normed_two, 'z', axis=0)  51.2 us
    psum x1, blocking collectives, per_device(): lax.psum(jnp.sum(scaled_two * middle, axis=1), 'row')[:, None]  41.2 us
    all_to_all x8, starting transfers between devices, swap(): lax.all_to_all(rows, SWAP_AXES, split_axis=0, concat_axis=0, tiled=True)  40.1 us
  transfers between devices with their start and end apart: 55, of which 34 were waited for; matrix products, arithmetic and copies ran while one was open for 11% of the time, Pallas kernels for 30%

profile of v3, /device:TPU:0, one launch (start us, length us, event | category | flops | bytes accessed | tf_op | source)
XLA Modules:
  0.0 1583.3 jit_solution(18159068414374318282)
XLA Ops:
  19.6 20.8 %collective-permute-done.3.refs_5_.refs_13_.refs_1_ = bf16[2064,256]{1,0:T(8,128)(2,1)S(1)} collective-permute-done((bf16[2064,256]{1,0:T(8,128)(2,1)S(1)}, bf16[2064,256]{1,0:T(8,128)(2,1)S(1)}, u32[]{:S(2)}, u32[]{:S(2)}) %collective-permute-start.3) | collective-permute-done | bytes 1056800 | tf_op jit(solution)/shard_map/ppermute | solution.py:206
  42.5 19.8 %collective-permute-done.4.refs_6_.refs_14_.refs_2_ = bf16[2064,256]{1,0:T(8,128)(2,1)} collective-permute-done((bf16[2064,256]{1,0:T(8,128)(2,1)S(1)}, bf16[2064,256]{1,0:T(8,128)(2,1)}, u32[]{:S(2)}, u32[]{:S(2)}) %collective-permute-start.4) | collective-permute-done | bytes 1056800 | tf_op jit(solution)/shard_map/ppermute | solution.py:206
  118.3 31.1 %project.1 = (bf16[2048,2048]{1,0:T(8,128)(2,1)}, bf16[2048,1536]{1,0:T(8,128)(2,1)}, f32[2048,1024]{1,0:T(8,128)}, f32[2048,1]{1,0:T(8,128)}) custom-call(s32[8]{0:T(128)} %stack.116.refs_0_, s32[4,4,4,2048]{3,2,1,0:T(4,128)} %convert_element_type.133.refs_1_, bf16[64,512]{1,0:T(8,128)(2,1)} %bitcast.138, bf16[2064,256]{1,0:T(8,128)(2,1)} %copy-done.18, ...), custom_call_target="tpu_custom_call" | custom-call | tf_op jit(solution)/shard_map/project/pallas_call | solution.py:49
  149.5 25.9 %attend.1 = (bf16[2048,512]{1,0:T(8,128)(2,1)}, f32[4,2048,1]{2,1,0:T(8,128)}) custom-call(s32[8]{0:T(128)} %get-tuple-element.67.refs_0_, s32[8]{0:T(128)} %get-tuple-element.66.refs_1_, bf16[2048,1536]{1,0:T(8,128)(2,1)} %get-tuple-element.38.refs_2_.refs_3_.refs_4_.refs_5_, bf16[2048,1536]{1,0:T(8,128)(2,1)} %get-tuple-element.38.refs_2_.refs_3_.refs_4_.refs_5_, ...), custom_call_target="tpu_custom_call" | custom-call | tf_op jit(solution)/shard_map/attend/pallas_call | solution.py:49
  184.1 42.1 %collective-permute-done.11 = bf16[2048,512]{1,0:T(8,128)(2,1)S(1)} collective-permute-done((bf16[2048,512]{1,0:T(8,128)(2,1)S(1)}, bf16[2048,512]{1,0:T(8,128)(2,1)S(1)}, u32[]{:S(2)}, u32[]{:S(2)}) %collective-permute-start.11) | collective-permute-done | bytes 2097184 | tf_op jit(solution)/shard_map/ppermute | solution.py:206
  233.8 20.8 %collective-permute-done.10 = bf16[2048,256]{1,0:T(8,128)(2,1)S(1)} collective-permute-done((bf16[2048,256]{1,0:T(8,128)(2,1)S(1)}, bf16[2048,256]{1,0:T(8,128)(2,1)S(1)}, u32[]{:S(2)}, u32[]{:S(2)}) %collective-permute-start.10) | collective-permute-done | bytes 1048608 | tf_op jit(solution)/shard_map/ppermute | solution.py:206
  279.1 28.7 %dispatch.4.refs_0_ = bf16[8,1,4,256,512]{4,3,2,1,0:T(8,128)(2,1)} custom-call(bf16[2048,512]{1,0:T(8,128)(2,1)} %copy-done, s32[4,8,1,2048]{3,2,1,0:T(1,128)} %get-tuple-element.110.refs_1_, bf16[4,2048,512]{2,1,0:T(8,128)(2,1)} %bitcast.121), custom_call_target="tpu_custom_call" | custom-call | tf_op jit(solution)/shard_map/dispatch/pallas_call | solution.py:49
  319.8 29.2 %dispatch.6.refs_0_ = bf16[8,1,4,256,512]{4,3,2,1,0:T(8,128)(2,1)} custom-call(bf16[2048,512]{1,0:T(8,128)(2,1)} %copy-done, s32[4,8,1,2048]{3,2,1,0:T(1,128)} %get-tuple-element.109.refs_1_, bf16[4,2048,512]{2,1,0:T(8,128)(2,1)} %bitcast.122), custom_call_target="tpu_custom_call" | custom-call | tf_op jit(solution)/shard_map/dispatch/pallas_call | solution.py:49
  349.0 64.3 %all-to-all-done.1 = bf16[8,1,4,256,512]{4,3,2,1,0:T(8,128)(2,1)} async-done(((bf16[8,1,4,256,512]{4,3,2,1,0:T(8,128)(2,1)}), bf16[8,1,4,256,512]{4,3,2,1,0:T(8,128)(2,1)}, u32[]{:S(2)}, u32[]{:S(2)}) %all-to-all-start.1) | async-done | bytes 8388640 | tf_op jit(solution)/shard_map/all_to_all | solution.py:788
  418.4 51.2 %all-gather.14.cloned.1.call-done = bf16[8192,512]{1,0:T(8,128)(2,1)} async-done(((bf16[2048,512]{1,0:T(8,128)(2,1)}), bf16[8192,512]{1,0:T(8,128)(2,1)}) %all-gather.14.cloned.1.call-update) | async-done | bytes 8388624 | tf_op jit(solution)/shard_map/all_gather | solution.py:908
  469.6 28.7 %dispatch.5.refs_0_ = bf16[8,1,4,256,512]{4,3,2,1,0:T(8,128)(2,1)} custom-call(bf16[4,2,1,4,256,512]{5,4,3,2,1,0:T(8,128)(2,1)} %bitcast.32.refs_0_.refs_1_.c_ref.refs_3_, s32[4,8,1,2048]{3,2,1,0:T(1,128)} %get-tuple-element.110.refs_1_, bf16[4,2048,512]{2,1,0:T(8,128)(2,1)} %bitcast.119), custom_call_target="tpu_custom_call" | custom-call | tf_op jit(solution)/shard_map/dispatch/pallas_call | solution.py:49
  517.4 28.8 %dispatch.7.refs_0_ = bf16[8,1,4,256,512]{4,3,2,1,0:T(8,128)(2,1)} custom-call(bf16[4,2,1,4,256,512]{5,4,3,2,1,0:T(8,128)(2,1)} %bitcast.32.refs_0_.refs_1_.c_ref.refs_3_, s32[4,8,1,2048]{3,2,1,0:T(1,128)} %get-tuple-element.109.refs_1_, bf16[4,2048,512]{2,1,0:T(8,128)(2,1)} %bitcast.120), custom_call_target="tpu_custom_call" | custom-call | tf_op jit(solution)/shard_map/dispatch/pallas_call | solution.py:49
  546.2 65.3 %all-to-all-done.3 = bf16[8,1,4,256,512]{4,3,2,1,0:T(8,128)(2,1)} async-done(((bf16[8,1,4,256,512]{4,3,2,1,0:T(8,128)(2,1)}), bf16[8,1,4,256,512]{4,3,2,1,0:T(8,128)(2,1)}, u32[]{:S(2)}, u32[]{:S(2)}) %all-to-all-start.3) | async-done | bytes 8388640 | tf_op jit(solution)/shard_map/all_to_all | solution.py:788
  639.1 37.0 %expert.2 = (bf16[2048,1024]{1,0:T(8,128)(2,1)}, bf16[2048,1024]{1,0:T(8,128)(2,1)}, bf16[2048,1024]{1,0:T(8,128)(2,1)}) custom-call(bf16[4,2,1,4,256,512]{5,4,3,2,1,0:T(8,128)(2,1)} %bitcast.35.refs_0_.refs_2_.refs_1_, bf16[4,2,1,4,256,512]{5,4,3,2,1,0:T(8,128)(2,1)} %bitcast.32.refs_0_.refs_1_.c_ref.refs_3_, bf16[2,2048,1024]{2,1,0:T(8,128)(2,1)} %gate_w.7, ...), custom_call_target="tpu_custom_call" | custom-call | tf_op jit(solution)/shard_map/expert/pallas_call | solution.py:49
  691.6 19.0 %all-to-all-done.4 = bf16[8,1,4,256,512]{4,3,2,1,0:T(8,128)(2,1)} async-done(((bf16[8,1,4,256,512]{4,3,2,1,0:T(8,128)(2,1)}), bf16[8,1,4,256,512]{4,3,2,1,0:T(8,128)(2,1)}, u32[]{:S(2)}, u32[]{:S(2)}) %all-to-all-start.4) | async-done | bytes 8388640 | tf_op jit(solution)/shard_map/all_to_all | solution.py:788
  710.6 37.2 %expert.3 = (bf16[2048,1024]{1,0:T(8,128)(2,1)}, bf16[2048,1024]{1,0:T(8,128)(2,1)}, bf16[2048,1024]{1,0:T(8,128)(2,1)}) custom-call(bf16[4,2,1,4,256,512]{5,4,3,2,1,0:T(8,128)(2,1)} %bitcast.38.refs_0_.refs_2_, bf16[4,2,1,4,256,512]{5,4,3,2,1,0:T(8,128)(2,1)} %bitcast.34.refs_1_.c_ref.refs_4_, bf16[2,2048,1024]{2,1,0:T(8,128)(2,1)} %gate_w.7, ...), custom_call_target="tpu_custom_call" | custom-call | tf_op jit(solution)/shard_map/expert/pallas_call | solution.py:49
  787.1 18.0 %produce.2 = (bf16[4,2,2,4,256,256]{5,4,3,2,1,0:T(8,128)(2,1)}, bf16[4,2,2,4,256,256]{5,4,3,2,1,0:T(8,128)(2,1)}, f32[2048,1]{1,0:T(8,128)}) custom-call(bf16[2048,1024]{1,0:T(8,128)(2,1)} %get-tuple-element.40.act_ref.refs_5_, bf16[2,2048,1024]{2,1,0:T(8,128)(2,1)} %w_ref.3, f32[2,2048,1]{2,1,0:T(8,128)} %reshape.288.refs_5_.prob_ref.refs_2_, ...), custom_call_target="tpu_custom_call" | custom-call | flops 8589934592 | bytes 37748736 | tf_op jit(solution)/shard_map/produce/pallas_call | solution.py:640
  838.5 27.2 %down_grad.1.refs_1_ = f32[2,2048,1024]{2,1,0:T(8,128)} custom-call(f32[2048,1]{1,0:T(8,128)} %get-tuple-element.41.refs_0_, f32[2048,1]{1,0:T(8,128)} %get-tuple-element.45.refs_1_, f32[2,2048,1]{2,1,0:T(8,128)} %reshape.288.refs_5_.prob_ref.refs_2_, bf16[4,2,1,4,256,512]{5,4,3,2,1,0:T(8,128)(2,1)} %bitcast.32.refs_0_.refs_1_.c_ref.refs_3_, ...), custom_call_target="tpu_custom_call" | custom-call | flops 17179869184 | tf_op jit(solution)/shard_map/down_grad/pallas_call | solution.py:49
  865.7 30.9 %combine.4.refs_0_ = bf16[4,2048,256]{2,1,0:T(8,128)(2,1)} custom-call(bf16[4,2,2,4,256,256]{5,4,3,2,1,0:T(8,128)(2,1)} %after.19.refs_0_, s32[4,2048,16]{2,1,0:T(8,128)} %bitcast.128, bf16[8,2,4,256,256]{4,3,2,1,0:T(8,128)(2,1)} %all-to-all-done.5.refs_1_.refs_2_), custom_call_target="tpu_custom_call" | custom-call | flops 17179869184 | tf_op jit(solution)/shard_map/combine/pallas_call | solution.py:49
  901.6 45.9 %gate_grad.1 = (f32[2,2048,1024]{2,1,0:T(8,128)}, f32[2,2048,1024]{2,1,0:T(8,128)}) custom-call(bf16[4,2048,256]{2,1,0:T(8,128)(2,1)} %combine.4.refs_0_, bf16[4,2,1,4,256,512]{5,4,3,2,1,0:T(8,128)(2,1)} %bitcast.35.refs_0_.refs_2_.refs_1_, bf16[4,2,1,4,256,512]{5,4,3,2,1,0:T(8,128)(2,1)} %bitcast.38.refs_0_.refs_2_, ...), custom_call_target="tpu_custom_call" | custom-call | tf_op jit(solution)/shard_map/gate_grad/pallas_call | solution.py:49
  947.5 48.1 %all-to-all-done.7.refs_3_.refs_1_ = bf16[8,2,4,256,256]{4,3,2,1,0:T(8,128)(2,1)} async-done(((bf16[8,2,4,256,256]{4,3,2,1,0:T(8,128)(2,1)}), bf16[8,2,4,256,256]{4,3,2,1,0:T(8,128)(2,1)}, u32[]{:S(2)}, u32[]{:S(2)}) %all-to-all-start.7) | async-done | bytes 8388640 | tf_op jit(solution)/shard_map/all_to_all | solution.py:788
  995.6 30.9 %combine.5 = bf16[4,2048,256]{2,1,0:T(8,128)(2,1)} custom-call(f32[2,2048,1024]{2,1,0:T(8,128)} %get-tuple-element.35.refs_0_, bf16[2048,256]{1,0:T(8,128)(2,1)} %bitcast.141, s32[4,2048,16]{2,1,0:T(8,128)} %bitcast.129, bf16[8,2,4,256,256]{4,3,2,1,0:T(8,128)(2,1)} %all-to-all-done.7.refs_3_.refs_1_), custom_call_target="tpu_custom_call" | custom-call | flops 17179869184 | tf_op jit(solution)/shard_map/combine/pallas_call | solution.py:49
  1050.7 19.9 %select_reduce_fusion = f32[64,2048]{1,0:T(8,128)S(1)} fusion(f32[64,256]{1,0:T(8,128)S(1)} %copy-done.39, f32[64,2048]{1,0:T(8,128)S(1)} %copy-done.35, f32[256]{0:T(256)S(1)} %copy-done.62), kind=kLoop, calls=%fused_computation.5 | loop fusion | flops 100532224 | bytes 1115136 | tf_op jit(solution)/shard_map/reduce_sum | solution.py:964
  1070.9 29.3 %reduce-scatter.10.cloned.1.call-done = bf16[1,2048,256]{2,1,0:T(8,128)(2,1)} async-done(((bf16[4,2048,256]{2,1,0:T(8,128)(2,1)}), bf16[1,2048,256]{2,1,0:T(8,128)(2,1)}) %reduce-scatter.10.cloned.1.call-update) | async-done | bytes 1048592 | tf_op jit(solution)/shard_map/reduce_scatter | solution.py:868
  1105.9 41.2 %psum.36 = f32[2048]{0:T(1024)S(1)} all-reduce(f32[2048]{0:T(1024)S(1)} %get-tuple-element.62), channel_id=1, replica_groups=mesh['row'=4,'z'=4,'core'=2] {'row'}, use_global_device_ids=true, to_apply=%region_13.15 | all-reduce | flops 2048 | bytes 16384 | tf_op jit(solution)/shard_map/psum | solution.py:992
  1153.0 30.9 %combine.6.refs_1_ = bf16[4,2048,256]{2,1,0:T(8,128)(2,1)} custom-call(bf16[2048,512]{1,0:T(8,128)(2,1)} %get-tuple-element.71.refs_0_, s32[4,2048,16]{2,1,0:T(8,128)} %bitcast.130, bf16[8,2,4,256,256]{4,3,2,1,0:T(8,128)(2,1)} %all-to-all-done.8.refs_2_.refs_1_), custom_call_target="tpu_custom_call" | custom-call | flops 17179869184 | tf_op jit(solution)/shard_map/combine/pallas_call | solution.py:49
  1190.7 22.3 %collective-permute-done.19.refs_5_.refs_4_.refs_3_ = bf16[2048,256]{1,0:T(8,128)(2,1)} collective-permute-done((bf16[2048,256]{1,0:T(8,128)(2,1)}, bf16[2048,256]{1,0:T(8,128)(2,1)}, u32[]{:S(2)}, u32[]{:S(2)}) %collective-permute-start.19) | collective-permute-done | bytes 1048608 | tf_op jit(solution)/shard_map/ppermute | solution.py:206
  1236.7 21.0 %collective-permute-done.23.refs_9_.refs_8_.refs_7_ = bf16[2048,256]{1,0:T(8,128)(2,1)} collective-permute-done((bf16[2048,256]{1,0:T(8,128)(2,1)}, bf16[2048,256]{1,0:T(8,128)(2,1)}, u32[]{:S(2)}, u32[]{:S(2)}) %collective-permute-start.23) | collective-permute-done | bytes 1048608 | tf_op jit(solution)/shard_map/ppermute | solution.py:206
  1291.9 59.3 %attend_back.1 = (bf16[2048,1536]{1,0:T(8,128)(2,1)}, f32[2,128]{1,0:T(2,128)}, f32[2048,1]{1,0:T(8,128)}) custom-call(s32[8]{0:T(128)} %get-tuple-element.67.refs_0_, s32[8]{0:T(128)} %get-tuple-element.66.refs_1_, bf16[2048,512]{1,0:T(8,128)(2,1)} %projection_grad.1.refs_2_, bf16[2048,1536]{1,0:T(8,128)(2,1)} %get-tuple-element.38.refs_2_.refs_3_.refs_4_.refs_5_, ...), custom_call_target="tpu_custom_call" | custom-call | tf_op jit(solution)/shard_map/attend_back/pallas_call | solution.py:49
  1372.6 30.9 %combine.7 = bf16[4,2048,256]{2,1,0:T(8,128)(2,1)} custom-call(bf16[2048,512]{1,0:T(8,128)(2,1)} %convolution_convert_fusion.2.refs_0_.refs_1_, bf16[2048,512]{1,0:T(8,128)(2,1)} %convolution_convert_fusion.1.refs_1_.refs_2_, s32[4,2048,16]{2,1,0:T(8,128)} %bitcast.131, bf16[8,2,4,256,256]{4,3,2,1,0:T(8,128)(2,1)} %all-to-all-done.10.refs_1_.refs_3_), custom_call_target="tpu_custom_call" | custom-call | flops 17179869184 | tf_op jit(solution)/shard_map/combine/pallas_call | solution.py:49
  1436.7 41.3 %collective-permute-done.29 = f32[18,128]{1,0:T(8,128)S(1)} collective-permute-done((f32[18,128]{1,0:T(8,128)S(1)}, f32[18,128]{1,0:T(8,128)S(1)}, u32[]{:S(2)}, u32[]{:S(2)}) %collective-permute-start.29) | collective-permute-done | bytes 9248 | tf_op jit(solution)/shard_map/ppermute | solution.py:206
  1550.5 26.1 %reduce-scatter.20.cloned.1.call-done = f32[16,256]{1,0:T(8,128)} async-done(((f32[16,2048]{1,0:T(8,128)}), f32[16,256]{1,0:T(8,128)}) %reduce-scatter.20.cloned.1.call-update) | async-done | bytes 16400 | tf_op jit(solution)/shard_map/reduce_scatter | solution.py:984
  (389 shorter events, 495.2 us)
Async XLA Ops:
  7.2 83.5 %all-gather.8.cloned.1.call-start = ((), (), s32[]{:S(2)}) async-start(), calls=%async_computation.18 | async-start | bytes 2949120 | tf_op jit(solution)/shard_map/all_gather | solution.py:845
  9.9 107.8 %all-gather.10.cloned.1.call-start = ((), (), s32[]{:S(2)}) async-start(), calls=%async_computation.19 | async-start | bytes 7077888 | tf_op jit(solution)/shard_map/all_gather | solution.py:839
  12.1 267.1 %all-gather.12.cloned.1.call-start = ((), (), s32[]{:S(2)}) async-start(), calls=%async_computation.27 | async-start | bytes 10485760 | tf_op jit(solution)/shard_map/all_gather | solution.py:872
  17.7 44.6 %collective-permute-start.4 = (bf16[2064,256]{1,0:T(8,128)(2,1)S(1)}, bf16[2064,256]{1,0:T(8,128)(2,1)}, u32[]{:S(2)}, u32[]{:S(2)}) collective-permute-start(bf16[2064,256]{1,0:T(8,128)(2,1)S(1)} %get-tuple-element.94.refs_4_.refs_12_), channel_id=1, source_target_pairs={{0,8},{8,0},{16,24},{24,16},{1,9},{9,1},{17,25},{25,17},{2,10},{10... | collective-permute-start | bytes 3170312 | tf_op jit(solution)/shard_map/ppermute | solution.py:206
  18.2 45.5 %collective-permute-start.5 = (bf16[2064,256]{1,0:T(8,128)(2,1)S(1)}, bf16[2064,256]{1,0:T(8,128)(2,1)}, u32[]{:S(2)}, u32[]{:S(2)}) collective-permute-start(bf16[2064,256]{1,0:T(8,128)(2,1)S(1)} %get-tuple-element.95.refs_3_.refs_11_), channel_id=1, source_target_pairs={{0,16},{8,24},{16,0},{24,8},{1,17},{9,25},{17,1},{25,9},{2,18},{10... | collective-permute-start | bytes 3170312 | tf_op jit(solution)/shard_map/ppermute | solution.py:206
  178.4 47.8 %collective-permute-start.11 = (bf16[2048,512]{1,0:T(8,128)(2,1)S(1)}, bf16[2048,512]{1,0:T(8,128)(2,1)S(1)}, u32[]{:S(2)}, u32[]{:S(2)}) collective-permute-start(bf16[2048,512]{1,0:T(8,128)(2,1)S(1)} %convolution_convert_fusion.3), channel_id=1, source_target_pairs={{0,16},{8,24},{16,0},{24,8},{1,17},{9,25},{17,1},{25,9},{2,18},{10... | collective-permute-start | bytes 6291464 | tf_op jit(solution)/shard_map/ppermute | solution.py:206
  181.2 47.5 %collective-permute-start.9 = (bf16[2048,512]{1,0:T(8,128)(2,1)S(1)}, bf16[2048,512]{1,0:T(8,128)(2,1)S(1)}, u32[]{:S(2)}, u32[]{:S(2)}) collective-permute-start(bf16[2048,512]{1,0:T(8,128)(2,1)S(1)} %convolution_convert_fusion.4), channel_id=1, source_target_pairs={{0,8},{8,0},{16,24},{24,16},{1,9},{9,1},{17,25},{25,17},{2,10},{10... | collective-permute-start | bytes 6291464 | tf_op jit(solution)/shard_map/ppermute | solution.py:206
  314.3 99.0 %all-to-all-start.1 = ((bf16[8,1,4,256,512]{4,3,2,1,0:T(8,128)(2,1)}), bf16[8,1,4,256,512]{4,3,2,1,0:T(8,128)(2,1)}, u32[]{:S(2)}, u32[]{:S(2)}) async-start(bf16[8,1,4,256,512]{4,3,2,1,0:T(8,128)(2,1)} %after.14), calls=%async_computation.1 | async-start | bytes 16777216 | tf_op jit(solution)/shard_map/all_to_all | solution.py:788
  319.2 150.4 %all-gather.14.cloned.1.call-start = ((), (), s32[]{:S(2)}) async-start(), calls=%async_computation.28 | async-start | bytes 10485760 | tf_op jit(solution)/shard_map/all_gather | solution.py:908
  413.3 99.2 %all-to-all-start.2 = ((bf16[8,1,4,256,512]{4,3,2,1,0:T(8,128)(2,1)}), bf16[8,1,4,256,512]{4,3,2,1,0:T(8,128)(2,1)}, u32[]{:S(2)}, u32[]{:S(2)}) async-start(bf16[8,1,4,256,512]{4,3,2,1,0:T(8,128)(2,1)} %after.15), calls=%async_computation.2 | async-start | bytes 16777216 | tf_op jit(solution)/shard_map/all_to_all | solution.py:788
  512.4 99.0 %all-to-all-start.3 = ((bf16[8,1,4,256,512]{4,3,2,1,0:T(8,128)(2,1)}), bf16[8,1,4,256,512]{4,3,2,1,0:T(8,128)(2,1)}, u32[]{:S(2)}, u32[]{:S(2)}) async-start(bf16[8,1,4,256,512]{4,3,2,1,0:T(8,128)(2,1)} %after.16), calls=%async_computation.3 | async-start | bytes 16777216 | tf_op jit(solution)/shard_map/all_to_all | solution.py:788
  611.5 99.1 %all-to-all-start.4 = ((bf16[8,1,4,256,512]{4,3,2,1,0:T(8,128)(2,1)}), bf16[8,1,4,256,512]{4,3,2,1,0:T(8,128)(2,1)}, u32[]{:S(2)}, u32[]{:S(2)}) async-start(bf16[8,1,4,256,512]{4,3,2,1,0:T(8,128)(2,1)} %after.17), calls=%async_computation.4 | async-start | bytes 16777216 | tf_op jit(solution)/shard_map/all_to_all | solution.py:788
  763.2 102.5 %all-to-all-start.5 = ((bf16[8,2,4,256,256]{4,3,2,1,0:T(8,128)(2,1)}), bf16[8,2,4,256,256]{4,3,2,1,0:T(8,128)(2,1)}, u32[]{:S(2)}, u32[]{:S(2)}) async-start(bf16[8,2,4,256,256]{4,3,2,1,0:T(8,128)(2,1)} %bitcast.115), calls=%async_computation.5 | async-start | bytes 16777216 | tf_op jit(solution)/shard_map/all_to_all | solution.py:788
  768.1 227.5 %reduce-scatter.8.cloned.1.call-start = ((), (), s32[]{:S(2)}) async-start(), calls=%async_computation.20 | async-start | bytes 5242880 | tf_op jit(solution)/shard_map/reduce_scatter | solution.py:868
  896.6 99.0 %all-to-all-start.7 = ((bf16[8,2,4,256,256]{4,3,2,1,0:T(8,128)(2,1)}), bf16[8,2,4,256,256]{4,3,2,1,0:T(8,128)(2,1)}, u32[]{:S(2)}, u32[]{:S(2)}) async-start(bf16[8,2,4,256,256]{4,3,2,1,0:T(8,128)(2,1)} %bitcast.116), calls=%async_computation.8 | async-start | bytes 16777216 | tf_op jit(solution)/shard_map/all_to_all | solution.py:788
  901.6 198.6 %reduce-scatter.10.cloned.1.call-start = ((), (), s32[]{:S(2)}) async-start(), calls=%async_computation.21 | async-start | bytes 5242880 | tf_op jit(solution)/shard_map/reduce_scatter | solution.py:868
  1045.5 107.4 %all-to-all-start.8 = ((bf16[8,2,4,256,256]{4,3,2,1,0:T(8,128)(2,1)}), bf16[8,2,4,256,256]{4,3,2,1,0:T(8,128)(2,1)}, u32[]{:S(2)}, u32[]{:S(2)}) async-start(bf16[8,2,4,256,256]{4,3,2,1,0:T(8,128)(2,1)} %bitcast.117), calls=%async_computation.10 | async-start | bytes 16777216 | tf_op jit(solution)/shard_map/all_to_all | solution.py:788
  1050.6 303.1 %reduce-scatter.12.cloned.1.call-start = ((), (), s32[]{:S(2)}) async-start(), calls=%async_computation.22 | async-start | bytes 5242880 | tf_op jit(solution)/shard_map/reduce_scatter | solution.py:868
  1188.7 46.7 %collective-permute-start.20 = (bf16[2048,256]{1,0:T(8,128)(2,1)S(1)}, bf16[2048,256]{1,0:T(8,128)(2,1)}, u32[]{:S(2)}, u32[]{:S(2)}) collective-permute-start(bf16[2048,256]{1,0:T(8,128)(2,1)S(1)} %get-tuple-element.96.refs_4_.refs_3_.refs_2_), channel_id=1, source_target_pairs={{0,8},{8,0},{16,24},{24,16},{1,9},{9,1},{17,25},{25,17},{2,10},{10... | collective-permute-start | bytes 3145736 | tf_op jit(solution)/shard_map/ppermute | solution.py:206
  1190.2 46.5 %collective-permute-start.21 = (bf16[2048,256]{1,0:T(8,128)(2,1)}, bf16[2048,256]{1,0:T(8,128)(2,1)}, u32[]{:S(2)}, u32[]{:S(2)}) collective-permute-start(bf16[2048,256]{1,0:T(8,128)(2,1)} %get-tuple-element.97.refs_3_.refs_2_.refs_1_), channel_id=1, source_target_pairs={{0,16},{8,24},{16,0},{24,8},{1,17},{9,25},{17,1},{25,9},{2,18},{10... | collective-permute-start | bytes 3145736 | tf_op jit(solution)/shard_map/ppermute | solution.py:206
  1213.0 44.6 %collective-permute-start.23 = (bf16[2048,256]{1,0:T(8,128)(2,1)}, bf16[2048,256]{1,0:T(8,128)(2,1)}, u32[]{:S(2)}, u32[]{:S(2)}) collective-permute-start(bf16[2048,256]{1,0:T(8,128)(2,1)} %collective-permute-done.19.refs_5_.refs_4_.refs_3_), channel_id=1, source_target_pairs={{0,16},{8,24},{16,0},{24,8},{1,17},{9,25},{17,1},{25,9},{2,18},{10... | collective-permute-start | bytes 3145736 | tf_op jit(solution)/shard_map/ppermute | solution.py:206
  1258.5 99.0 %all-to-all-start.10 = ((bf16[8,2,4,256,256]{4,3,2,1,0:T(8,128)(2,1)}), bf16[8,2,4,256,256]{4,3,2,1,0:T(8,128)(2,1)}, u32[]{:S(2)}, u32[]{:S(2)}) async-start(bf16[8,2,4,256,256]{4,3,2,1,0:T(8,128)(2,1)} %bitcast.118), calls=%async_computation.12 | async-start | bytes 16777216 | tf_op jit(solution)/shard_map/all_to_all | solution.py:788
  1263.5 233.7 %reduce-scatter.18.cloned.1.call-start = ((), (), s32[]{:S(2)}) async-start(), calls=%async_computation.25 | async-start | bytes 1310720 | tf_op jit(solution)/shard_map/reduce_scatter | solution.py:250
  1286.2 64.9 %collective-permute-start.33 = (bf16[4,256,512]{2,1,0:T(8,128)(2,1)S(1)}, bf16[4,256,512]{2,1,0:T(8,128)(2,1)}, u32[]{:S(2)}, u32[]{:S(2)}) collective-permute-start(bf16[4,256,512]{2,1,0:T(8,128)(2,1)S(1)} %dynamic-slice_bitcast_fusion.1), channel_id=1, source_target_pairs={{0,1},{1,0},{2,3},{3,2},{4,5},{5,4},{6,7},{7,6},{8,9},{9,8},{10,11... | collective-permute-start | bytes 3145736 | tf_op jit(solution)/shard_map/ppermute | solution.py:248
  1353.7 188.7 %reduce-scatter.14.cloned.1.call-start = ((), (), s32[]{:S(2)}) async-start(), calls=%async_computation.23 | async-start | bytes 5242880 | tf_op jit(solution)/shard_map/reduce_scatter | solution.py:868
  1403.5 144.6 %reduce-scatter.16.cloned.1.call-start = ((), (), s32[]{:S(2)}) async-start(), calls=%async_computation.24 | async-start | bytes 3932160 | tf_op jit(solution)/shard_map/reduce_scatter | solution.py:250
  1429.5 147.1 %reduce-scatter.20.cloned.1.call-start = ((), (), s32[]{:S(2)}) async-start(), calls=%async_computation.26 | async-start | bytes 147456 | tf_op jit(solution)/shard_map/reduce_scatter | solution.py:984
  1429.6 56.8 %collective-permute-start.27 = (bf16[2048,512]{1,0:T(8,128)(2,1)}, bf16[2048,512]{1,0:T(8,128)(2,1)}, u32[]{:S(2)}, u32[]{:S(2)}) collective-permute-start(bf16[2048,512]{1,0:T(8,128)(2,1)} %convolution_convert_fusion.1.refs_1_.refs_2_), channel_id=1, source_target_pairs={{0,16},{8,24},{16,0},{24,8},{1,17},{9,25},{17,1},{25,9},{2,18},{10... | collective-permute-start | bytes 6291464 | tf_op jit(solution)/shard_map/ppermute | solution.py:206
  1430.2 58.4 %collective-permute-start.25 = (bf16[2048,512]{1,0:T(8,128)(2,1)S(1)}, bf16[2048,512]{1,0:T(8,128)(2,1)}, u32[]{:S(2)}, u32[]{:S(2)}) collective-permute-start(bf16[2048,512]{1,0:T(8,128)(2,1)S(1)} %copy-done.24), channel_id=1, source_target_pairs={{0,8},{8,0},{16,24},{24,16},{1,9},{9,1},{17,25},{25,17},{2,10},{10... | collective-permute-start | bytes 6291464 | tf_op jit(solution)/shard_map/ppermute | solution.py:206
  1432.4 45.6 %collective-permute-start.29 = (f32[18,128]{1,0:T(8,128)S(1)}, f32[18,128]{1,0:T(8,128)S(1)}, u32[]{:S(2)}, u32[]{:S(2)}) collective-permute-start(f32[18,128]{1,0:T(8,128)S(1)} %get-tuple-element.116), channel_id=1, source_target_pairs={{0,8},{8,0},{16,24},{24,16},{1,9},{9,1},{17,25},{25,17},{2,10},{10... | collective-permute-start | bytes 27656 | tf_op jit(solution)/shard_map/ppermute | solution.py:206
  1433.9 44.1 %collective-permute-start.30 = (f32[18,128]{1,0:T(8,128)S(1)}, f32[18,128]{1,0:T(8,128)S(1)}, u32[]{:S(2)}, u32[]{:S(2)}) collective-permute-start(f32[18,128]{1,0:T(8,128)S(1)} %get-tuple-element.116), channel_id=1, source_target_pairs={{0,16},{8,24},{16,0},{24,8},{1,17},{9,25},{17,1},{25,9},{2,18},{10... | collective-permute-start | bytes 27656 | tf_op jit(solution)/shard_map/ppermute | solution.py:206
  1435.4 43.7 %collective-permute-start.31 = (f32[18,128]{1,0:T(8,128)S(1)}, f32[18,128]{1,0:T(8,128)S(1)}, u32[]{:S(2)}, u32[]{:S(2)}) collective-permute-start(f32[18,128]{1,0:T(8,128)S(1)} %get-tuple-element.116), channel_id=1, source_target_pairs={{0,24},{8,16},{16,8},{24,0},{1,25},{9,17},{17,9},{25,1},{2,26},{10... | collective-permute-start | bytes 27656 | tf_op jit(solution)/shard_map/ppermute | solution.py:206
  (93 other events, 1987.6 us)
Sparse Core Ops, SparseCore 0:
  10.2 36.4 all-gather.7
  48.3 69.3 all-gather.9
  119.8 148.1 all-gather.11
  321.3 148.2 all-gather.13
  896.7 75.3 reduce-scatter.7
  1026.6 73.4 reduce-scatter.9
  1215.2 76.3 reduce-scatter.11
  1353.8 30.1 reduce-scatter.17
  1403.6 75.9 reduce-scatter.13
  1481.7 61.4 reduce-scatter.15
  1546.1 30.4 reduce-scatter.19

commit v4 on v3

--- a/solution.py
+++ b/solution.py
@@ -238,7 +238,7 @@
     return jnp.take(stacked, me ^ jnp.arange(4), axis=0)
 
 
-def token_scatter(values):
+def core_sum(values):
     z_count, core_count = lax.axis_size("z"), lax.axis_size("core")
     rows, columns = values.shape
     blocks = values.reshape(z_count, core_count, rows // (z_count * core_count), columns)
@@ -246,8 +246,20 @@
     keep = lax.dynamic_index_in_dim(blocks, core, 1, keepdims=False)
     give = lax.dynamic_index_in_dim(blocks, 1 - core, 1, keepdims=False)
     got = lax.ppermute(give, "core", [(0, 1), (1, 0)])
-    summed = (keep.astype(F32) + got.astype(F32)).astype(values.dtype)
-    return lax.psum_scatter(summed.reshape(-1, columns), "z", scatter_dimension=0, tiled=True)
+    return (keep.astype(F32) + got.astype(F32)).astype(values.dtype).reshape(-1, columns)
+
+
+def z_scatter(values):
+    return lax.psum_scatter(values, "z", scatter_dimension=0, tiled=True)
+
+
+def row_sum(values):
+    if lax.axis_size("row") != 4:
+        return jnp.sum(lax.all_gather(values, "row", axis=0), axis=0)
+    half = values.shape[1] // 2
+    left, right = values[:, :half], values[:, half:]
+    left, right = left + permute(left, 1), right + permute(right, 2)
+    return jnp.concatenate([left + permute(left, 2), right + permute(right, 1)], axis=1)
 
 
 def after(value, *others):
@@ -279,20 +291,25 @@
     )
 
 
-def row_scatter(left, ordered):
+def row_scatter(left, ordered, *meanwhile):
     if lax.axis_size("row") != 4:
         return lax.psum_scatter(
             dot(left, ordered, 1, 1).astype(BF), "row", scatter_dimension=1, tiled=True
-        ).astype(F32), ()
+        ).astype(F32), (), ()
     width = ordered.shape[0] // 4
     half = width // 2
     part = lambda index: dot(left, ordered[index * width : (index + 1) * width], 1, 1)
     sent = [part(0).astype(BF), part(1).astype(BF)]
-    from_x = permute(sent[0], 1).astype(F32)
-    from_y = permute(sent[1], 2).astype(F32)
+    received = [permute(sent[0], 1), permute(sent[1], 2)]
+    from_x, from_y = received[0].astype(F32), received[1].astype(F32)
     onward, own = part(2), part(3)
-    last_left = permute((onward[:, :half] + from_x[:, half:]).astype(BF), 2).astype(F32)
-    last_right = permute((onward[:, half:] + from_y[:, half:]).astype(BF), 1).astype(F32)
+    onward_left = (onward[:, :half] + from_x[:, half:]).astype(BF)
+    onward_right = (onward[:, half:] + from_y[:, half:]).astype(BF)
+    if meanwhile:
+        onward_left = after(onward_left, *meanwhile)
+        onward_right = after(onward_right, *meanwhile)
+    last_left = permute(onward_left, 2).astype(F32)
+    last_right = permute(onward_right, 1).astype(F32)
     total = jnp.concatenate(
         [
             own[:, :half] + from_x[:, :half] + last_left,
@@ -300,7 +317,7 @@
         ],
         axis=1,
     )
-    return total, sent
+    return total, sent, received
 
 
 QUERY_TILE = 256
@@ -577,17 +594,23 @@
     return ref[row].reshape(cores * groups * capacity, features)
 
 
-def expert_body(x_ref, c_ref, gate_w, up_w, down_w, prob_ref, act_ref, gate_out, up_out):
+def expert_body(*refs):
+    x_ref, c_refs = refs[0], refs[1 : 1 + CHUNKS]
+    gate_w, up_w, down_w, prob_ref, act_ref, gate_out, up_out = refs[1 + CHUNKS :]
     rows, width = x_ref.shape[0], x_ref.shape[-1]
     prob = prob_ref[0]
     gate = up = grad = None
     for row in range(rows):
         features = pl.ds(row * width, width)
         x = block_rows(x_ref, row)
-        c = (block_rows(c_ref, row).astype(F32) * prob).astype(BF)
         gate_part = dot(x, gate_w[0, features, :])
         up_part = dot(x, up_w[0, features, :])
-        grad_part = dot(c, down_w[0, features, :])
+        grad_part = None
+        for chunk, c_ref in enumerate(c_refs):
+            c = (block_rows(c_ref, row).astype(F32) * prob).astype(BF)
+            part_width = width // CHUNKS
+            part = dot(c, down_w[0, pl.ds(row * width + chunk * part_width, part_width), :])
+            grad_part = part if grad_part is None else grad_part + part
         gate = gate_part if gate is None else gate + gate_part
         up = up_part if up is None else up + up_part
         grad = grad_part if grad is None else grad + grad_part
@@ -602,23 +625,27 @@
     _, features, hidden = gate_weight.shape
     slots = groups * capacity
     tile = min(512, hidden, 512 * 1024 // slots)
-    block = (row_count, 1, 1, groups, capacity, width)
-    row_spec = pl.BlockSpec(block, lambda n, k: (0, k, 0, 0, 0, 0))
+    row_spec = pl.BlockSpec(
+        (row_count, 1, 1, groups, capacity, width), lambda n, k: (0, k, 0, 0, 0, 0)
+    )
+    cot_spec = pl.BlockSpec(
+        (row_count, 1, 1, groups, capacity, width // CHUNKS), lambda n, k: (0, k, index, 0, 0, 0)
+    )
     w_spec = pl.BlockSpec((1, features, tile), lambda n, k: (index, 0, n))
     out_spec = pl.BlockSpec((slots, tile), lambda n, k: (k, n))
     return call(
         expert_body,
         (hidden // tile, cores),
-        [row_spec, row_spec, w_spec, w_spec, w_spec]
+        [row_spec] + [cot_spec] * CHUNKS + [w_spec, w_spec, w_spec]
         + [pl.BlockSpec((1, slots, 1), lambda n, k: (index, k, 0))],
         [out_spec] * 3,
         [shape((cores * slots, hidden), BF)] * 3,
         name="expert",
-    )(rows, cots, gate_weight, up_weight, down_weight, prob)
-
-
-def produce_body(act_ref, w_ref, prob_ref, c_ref, *refs):
-    out_refs, inner_ref = refs[-CHUNKS - 1 : -1], refs[-1]
+    )(rows, *cots, gate_weight, up_weight, down_weight, prob)
+
+
+def produce_body(act_ref, w_ref, prob_ref, *refs):
+    c_refs, out_refs, inner_ref = refs[:CHUNKS], refs[-CHUNKS - 1 : -1], refs[-1]
     width = out_refs[0].shape[-1]
 
     @pl.when(pl.program_id(1) == 0)
@@ -626,10 +653,13 @@
         inner_ref[...] = jnp.zeros_like(inner_ref)
 
     made = dot(act_ref[...], w_ref[0], 1, 1)
-    inner_ref[...] += jnp.sum(made * block_rows(c_ref).astype(F32), axis=1, keepdims=True)
     weighted = (made * prob_ref[0]).astype(BF)
     for chunk, out_ref in enumerate(out_refs):
-        out_ref[...] = weighted[:, chunk * width : (chunk + 1) * width].reshape(out_ref.shape)
+        columns = slice(chunk * width, (chunk + 1) * width)
+        inner_ref[...] += jnp.sum(
+            made[:, columns] * block_rows(c_refs[chunk]).astype(F32), axis=1, keepdims=True
+        )
+        out_ref[...] = weighted[:, columns].reshape(out_ref.shape)
 
 
 def produce(index, activated, down_weight, prob, cots, dims, buffers):
@@ -645,10 +675,11 @@
             pl.BlockSpec((slots, hidden), lambda k, r: (k, 0)),
             pl.BlockSpec((1, width * CHUNKS, hidden), lambda k, r: (index, r, 0)),
             pl.BlockSpec((1, slots, 1), lambda k, r: (index, k, 0)),
-            pl.BlockSpec(
-                (1, 1, 1, groups, capacity, width * CHUNKS), lambda k, r: (r, k, 0, 0, 0, 0)
-            ),
         ]
+        + [
+            pl.BlockSpec((1, 1, 1, groups, capacity, width), lambda k, r: (r, k, index, 0, 0, 0))
+        ]
+        * CHUNKS
         + [pl.BlockSpec(memory_space=pl.ANY)] * len(given),
         out_specs=[
             pl.BlockSpec(
@@ -657,7 +688,7 @@
         ]
         * CHUNKS
         + [pl.BlockSpec((slots, 1), lambda k, r: (k, 0))],
-        input_output_aliases={4 + chunk: chunk for chunk in range(len(given))},
+        input_output_aliases={3 + CHUNKS + chunk: chunk for chunk in range(len(given))},
         compiler_params=pltpu.CompilerParams(
             dimension_semantics=("arbitrary",) * 2, vmem_limit_bytes=VMEM_BYTES
         ),
@@ -667,7 +698,7 @@
             transcendentals=0,
         ),
         name="produce",
-    )(activated, down_weight, prob, cots, *given)
+    )(activated, down_weight, prob, *cots, *given)
     return outs[:CHUNKS], outs[CHUNKS]
 
 
@@ -676,15 +707,17 @@
 
 
 def down_grad_body(*refs):
-    prob_ref, refs = refs[0], refs[1:]
-    local = len(refs) // 2
-    c_refs, act_refs, out_ref = refs[:local], refs[local:-1], refs[-1]
-    for index in range(local):
+    prob_ref, c_refs, act_refs, out_ref = (
+        refs[0], refs[1 : 1 + CHUNKS], refs[1 + CHUNKS : -1], refs[-1]
+    )
+    width = c_refs[0].shape[-1]
+    for index, act_ref in enumerate(act_refs):
 
         @pl.when(pl.program_id(0) == index)
         def _():
-            c = (block_rows(c_refs[index]).astype(F32) * prob_ref[0]).astype(BF)
-            out_ref[0] = dot(c, act_refs[index][...], 0, 0)
+            for chunk, c_ref in enumerate(c_refs):
+                c = (block_rows(c_ref).astype(F32) * prob_ref[0]).astype(BF)
+                out_ref[0, pl.ds(chunk * width, width), :] = dot(c, act_ref[...], 0, 0)
 
 
 def row_specs(local, shape_of):
@@ -700,17 +733,17 @@
 
 
 def down_grad(cots, prob, activated, deps=()):
-    rows, cores, _, groups, capacity, width = cots[0].shape
+    rows, cores, local, groups, capacity, width = cots[0].shape
     slots, hidden = activated[0].shape
-    local = len(cots)
     return call(
         down_grad_body,
         (local, rows),
         [pl.BlockSpec((1, slots, 1), lambda i, r: (i, 0, 0))]
-        + row_specs(local, cots[0].shape)
+        + [pl.BlockSpec((1, cores, 1, groups, capacity, width), lambda i, r: (r, 0, i, 0, 0, 0))]
+        * CHUNKS
         + [pl.BlockSpec((slots, hidden), lambda i, r: (0, 0))] * local,
-        pl.BlockSpec((1, width, hidden), lambda i, r: (i, r, 0)),
-        shape((local, rows * width, hidden), F32),
+        pl.BlockSpec((1, width * CHUNKS, hidden), lambda i, r: (i, r, 0)),
+        shape((local, rows * width * CHUNKS, hidden), F32),
         name="down_grad",
         flops=2 * local * slots * D * hidden,
         deps=deps,
@@ -869,7 +902,15 @@
             tokens, width
         )
 
-    spread_cots = lax.all_gather(after(cotangent, *hidden_pieces[2:6]), "z", axis=0)
+    spread_cots = [
+        lax.all_gather(
+            after(cotangent[:, chunk * width : (chunk + 1) * width], *hidden_pieces[2:6]),
+            "z",
+            axis=0,
+        )
+        for chunk in range(CHUNKS)
+    ]
+    first_picked = dispatch(slots, spread_cots[0], capacity)
 
     cosine, sine = rotary_tables()
     first_gain = attention_gain.astype(F32)
@@ -888,26 +929,27 @@
     segment = segments[0]
     low, high = key_ranges(segment)
     mixed, sums = attend(heads, segment, low, high)
-    middle = residual + row_scatter(mixed, row_scatter_order(projection_full))[0]
+    middle = residual + row_scatter(
+        mixed, row_scatter_order(projection_full), first_picked
+    )[0]
     second_factor = lax.rsqrt(lax.psum(jnp.sum(middle * middle, axis=1), "row") / D + EPSILON)[
         :, None
     ]
     normed_two = (middle * second_factor * second_gain).astype(BF)
 
-    logits = jnp.sum(small_row_gather(dot(router_here, normed_two, 1, 1)), axis=0)
+    logits = row_sum(dot(router_here, normed_two, 1, 1))
     raised = jnp.exp(logits)
     router_probs = raised / jnp.sum(raised, axis=0, keepdims=True)
 
-    def send(spread, index, earlier, *before):
-        picked = dispatch(slots[:, :, index : index + 1], spread, capacity, before)
-        return swap(after(picked, *earlier) if earlier else picked).reshape(expert_dims)
-
-    cots, rows = [], []
+    cots = [swap(after(first_picked, normed_two)).reshape(dims)]
+    for spread in spread_cots[1:]:
+        picked = dispatch(slots, spread, capacity, [normed_two])
+        cots.append(swap(after(picked, cots[-1])).reshape(dims))
+    spread_rows = lax.all_gather(normed_two, "z", axis=0)
+    rows = []
     for index in range(local):
-        cots.append(send(spread_cots, index, cots[-1:] or [logits], normed_two))
-    spread_rows = lax.all_gather(normed_two, "z", axis=0)
-    for index in range(local):
-        rows.append(send(spread_rows, index, [cots[-1]] + rows[-1:], cots[0]))
+        picked = dispatch(slots[:, :, index : index + 1], spread_rows, capacity, cots[:1])
+        rows.append(swap(after(picked, logits, cots[-1], *rows[-1:])).reshape(expert_dims))
     own_slots = lax.dynamic_slice_in_dim(position, row_index * experts_here, experts_here, 0)
     own_probs = lax.dynamic_slice_in_dim(router_probs, row_index * experts_here, experts_here, 0)
     order = jnp.arange(capacity, dtype=jnp.int32).astype(F32)
@@ -932,7 +974,7 @@
     for index in range(local):
         rows_here = rows[index]
         act, gate_pre, up_pre = expert(
-            index, rows_here, cots[index], gate_weight, up_weight, down_weight, prob
+            index, rows_here, cots, gate_weight, up_weight, down_weight, prob
         )
         activated.append(act)
         grad_gate_pre.append(gate_pre)
@@ -945,7 +987,7 @@
     inners, made_buffers = [], None
     for index in range(local):
         made_buffers, inner = produce(
-            index, activated[index], down_weight, prob, cots[index], dims, made_buffers
+            index, activated[index], down_weight, prob, cots, dims, made_buffers
         )
         inners.append(inner)
 
@@ -954,12 +996,11 @@
         z_count * core_count, local * capacity
     )
     back_rows = [swap(buffers[0].reshape(swapped_dims))]
-    of_group = lax.all_to_all(
-        after(to_groups, back_rows[0]), TOKENS_AXES, 0, 0, tiled=True
-    ).reshape(-1, capacity)
+    to_groups = after(to_groups, back_rows[0], buffers[1])
+    of_group = lax.all_to_all(to_groups, TOKENS_AXES, 0, 0, tiled=True).reshape(-1, capacity)
     slot_grads = jnp.sum(small_row_gather(of_group).reshape(E, pieces, capacity), axis=1)
     grad_down = down_grad(cots, prob, activated, inners)
-    ready = after(buffers[1], grad_down)
+    ready = after(buffers[1], grad_down, slot_grads)
     back_rows.append(swap(ready.reshape(swapped_dims)))
     grad_prob = jnp.sum(
         jnp.where(position[:, None, :] == order[None, :, None], slot_grads[:, :, None], 0.0), axis=1
@@ -968,11 +1009,11 @@
         router_probs * (grad_prob - jnp.sum(router_probs * grad_prob, axis=0, keepdims=True))
     ).astype(BF)
     from_router = dot(grad_logits, router_here, 0, 0)
-    first_sum = combine(slots_by_token, [back_rows[0]], 0, width, [ready])
+    first_sum = combine(slots_by_token, [back_rows[0]], 0, width, [grad_down, to_groups])
     grad_gate, grad_up = gate_grad(rows, grad_gate_pre, grad_up_pre, [first_sum])
     first_sum = scatter_back(first_sum)
     second_sum = scatter_back(
-        combine(slots_by_token, [back_rows[1]], 0, width, [grad_gate, first_sum])
+        combine(slots_by_token, [back_rows[1]], 0, width, [grad_gate, first_sum, from_router])
     )
     grad_normed_two = from_router + jnp.concatenate(
         [first_sum, second_sum], axis=1
@@ -986,7 +1027,7 @@
         TOKENS_AXES,
         scatter_dimension=1,
         tiled=True,
-    ).T
+    )
 
     scaled_two = grad_normed_two * second_gain
     second_inner = lax.psum(jnp.sum(scaled_two * middle, axis=1), "row")[:, None]
@@ -998,21 +1039,22 @@
     grad_feedforward_gain = jnp.sum(grad_normed_two * middle * second_factor, axis=0)
 
     grad_branch = grad_middle.astype(BF)
-    made_rows = [swap(after(made_buffers[0], back_rows[1], slot_grads).reshape(swapped_dims))]
+    made_rows = [swap(after(made_buffers[0], back_rows[1], router_swapped).reshape(swapped_dims))]
     branch_pieces, branch_starts = row_gather(after(grad_branch, made_rows[0]))
     made_rows.append(swap(after(made_buffers[1], *branch_pieces).reshape(swapped_dims)))
     made_sums = [combine(slots_by_token, [made_rows[0]], 0, width, [grad_branch])]
+    grad_projection = projection_grad(branch_starts, branch_pieces, mixed, made_sums)
     grad_mixed = mix_back(
-        branch_starts, branch_pieces, projection_full, made_sums + [router_swapped]
-    )
-    grad_projection = projection_grad(branch_starts, branch_pieces, mixed, [grad_mixed])
+        branch_starts, branch_pieces, projection_full, [grad_projection, router_swapped]
+    )
+    projection_sum = core_sum(grad_projection)
     grad_raw, head_gain_grads, along = attend_back(
         heads, grad_mixed, mixed, sums, segment, low, high, raw, cosine, sine, head_gains,
-        [grad_projection],
+        [projection_sum],
     )
     from_experts = [scatter_back(made_sums[0])]
-    grad_raw = after(grad_raw, made_rows[1], from_experts[0])
-    grad_first, sent = row_scatter(grad_raw, row_scatter_order(qkv_full))
+    grad_raw = after(grad_raw, made_rows[1], from_experts[0], grad_router)
+    grad_first, sent, received = row_scatter(grad_raw, row_scatter_order(qkv_full))
     from_experts.append(
         scatter_back(combine(slots_by_token, [made_rows[1]], 0, width, sent))
     )
@@ -1020,7 +1062,7 @@
     small = jnp.sum(small_row_gather(small), axis=0)
     first_inner = small[:-2].reshape(-1, 1) / first_factor
     head_gain_grads = small[-2:]
-    grad_qkv = dot(after(normed_one, *sent), grad_raw, 0, 0).astype(BF)
+    grad_qkv = dot(after(normed_one, *received), grad_raw, 0, 0).astype(BF)
     scaled_one = grad_first * first_gain
     grad_input = (
         grad_middle + scaled_one * first_factor - residual * first_factor**3 * first_inner / D
@@ -1030,8 +1072,8 @@
     grad_attention_gain, grad_feedforward_gain, head_gain_grads = lax.psum(
         (grad_attention_gain, grad_feedforward_gain, head_gain_grads), TOKENS_AXES
     )
-    grad_projection = token_scatter(grad_projection).astype(F32)
-    grad_qkv = token_scatter(grad_qkv).astype(F32)
+    grad_projection = z_scatter(projection_sum).astype(F32)
+    grad_qkv = z_scatter(core_sum(grad_qkv)).astype(F32)
     from_experts = jnp.concatenate(from_experts, axis=1).astype(F32)
     output = (after(middle, grad_first) + from_experts).astype(BF)
     return (
@@ -1045,7 +1087,7 @@
         head_gain_grads[0],
         head_gain_grads[1],
         grad_feedforward_gain,
-        grad_router,
+        grad_router.T,
         grad_gate,
         grad_up,
         grad_down,

time: 1600 us -> 1600 us (level)
    all_gather x1, waiting for transfers between devices: 51.2 us -> 0.01 us  [per_device(): spread_rows = lax.all_gather(normed_two, 'z', axis=0)]
    all_to_all x8, waiting for transfers between devices: 215 us -> 175 us  [swap(): lax.all_to_all(rows, SWAP_AXES, split_axis=0, concat_axis=0, tiled=True)]
    ppermute x32 -> x33, waiting for transfers between devices: 239 us -> 272 us  [permute(): return lax.ppermute(values, 'row', [(i, i ^ mask) for i in range(4)])]
    reduce_scatter x4, waiting for transfers between devices: 29.3 us -> 58.1 us  [scatter_back(): lax.psum_scatter(summed, 'z', scatter_dimension=0, tiled=True)]
    reduce_scatter x2, waiting for transfers between devices: 0.02 us -> 26.9 us  [z_scatter(): return lax.psum_scatter(values, 'z', scatter_dimension=0, tiled=True)]
    reduce_scatter x1, waiting for transfers between devices: 26.1 us -> 0.01 us  [per_device(): lax.psum_scatter(jnp.swapaxes(router_swapped, 0, 1).reshape(experts_here,...]
    ppermute x32 -> x33, starting transfers between devices: 35.2 us -> 39.2 us  [permute(): return lax.ppermute(values, 'row', [(i, i ^ mask) for i in range(4)])]
  transfers between devices with their start and end apart: 55 -> 57, of which waited for: 34 -> 36; matrix products, arithmetic and copies ran while one was open for 11% -> 12% of each run, Pallas kernels for 30% -> 31%
where the time goes in v4:
time: 1600 us; the launch traced here: 1580 us
  Pallas kernels  633 us (40%)
  waiting for transfers between devices  560 us (35%)
  other arithmetic  96.9 us (6%)
  starting transfers between devices  88.8 us (6%)
  blocking collectives  80.3 us (5%)
  matrix products  61.1 us (4%)
  local copies, waits for them, and re-layouts  45.6 us (3%)
    pallas_call x17, Pallas kernels, call(): return lambda *args: kernel(*args[:prefetch], *deps, *args[prefetch:])  535 us
    ppermute x33, waiting for transfers between devices, permute(): return lax.ppermute(values, 'row', [(i, i ^ mask) for i in range(4)])  272 us
    all_to_all x8, waiting for transfers between devices, swap(): lax.all_to_all(rows, SWAP_AXES, split_axis=0, concat_axis=0, tiled=True)  175 us
    pallas_call x4, Pallas kernels, rows_back(): pl.pallas_call(rows_back_body, out_shape=shape(dims, BF), grid=(cores, ro...  61.7 us
    reduce_scatter x4, waiting for transfers between devices, scatter_back(): lax.psum_scatter(summed, 'z', scatter_dimension=0, tiled=True)  58.1 us
    dot_general x12, matrix products, dot(): lax.dot_general(left, right, (((left_dim,), (right_dim,)), ((), ())), pre...  57.3 us
    all_to_all x8, starting transfers between devices, swap(): lax.all_to_all(rows, SWAP_AXES, split_axis=0, concat_axis=0, tiled=True)  40.3 us
    ppermute x33, starting transfers between devices, permute(): return lax.ppermute(values, 'row', [(i, i ^ mask) for i in range(4)])  39.2 us
  transfers between devices with their start and end apart: 57, of which 36 were waited for; matrix products, arithmetic and copies ran while one was open for 12% of the time, Pallas kernels for 31%

profile of v4, /device:TPU:0, one launch (start us, length us, event | category | flops | bytes accessed | tf_op | source)
XLA Modules:
  0.0 1581.6 jit_solution(5152104040012732807)
XLA Ops:
  19.7 20.6 %collective-permute-done.3.refs_5_.refs_13_.refs_1_ = bf16[2064,256]{1,0:T(8,128)(2,1)S(1)} collective-permute-done((bf16[2064,256]{1,0:T(8,128)(2,1)S(1)}, bf16[2064,256]{1,0:T(8,128)(2,1)S(1)}, u32[]{:S(2)}, u32[]{:S(2)}) %collective-permute-start.3) | collective-permute-done | bytes 1056800 | tf_op jit(solution)/shard_map/ppermute | solution.py:206
  42.4 19.9 %collective-permute-done.4.refs_6_.refs_14_.refs_2_ = bf16[2064,256]{1,0:T(8,128)(2,1)} collective-permute-done((bf16[2064,256]{1,0:T(8,128)(2,1)S(1)}, bf16[2064,256]{1,0:T(8,128)(2,1)}, u32[]{:S(2)}, u32[]{:S(2)}) %collective-permute-start.4) | collective-permute-done | bytes 1056800 | tf_op jit(solution)/shard_map/ppermute | solution.py:206
  118.3 31.1 %project.1 = (bf16[2048,2048]{1,0:T(8,128)(2,1)}, bf16[2048,1536]{1,0:T(8,128)(2,1)}, f32[2048,1024]{1,0:T(8,128)}, f32[2048,1]{1,0:T(8,128)}) custom-call(s32[8]{0:T(128)} %stack.101.refs_0_, s32[4,4,4,2048]{3,2,1,0:T(4,128)} %convert_element_type.133.refs_1_, bf16[64,512]{1,0:T(8,128)(2,1)} %bitcast.143, bf16[2064,256]{1,0:T(8,128)(2,1)} %copy-done.24, ...), custom_call_target="tpu_custom_call" | custom-call | tf_op jit(solution)/shard_map/project/pallas_call | solution.py:49
  149.5 29.1 %attend.1 = (bf16[2048,512]{1,0:T(8,128)(2,1)}, f32[4,2048,1]{2,1,0:T(8,128)}) custom-call(s32[8]{0:T(128)} %get-tuple-element.67.refs_0_, s32[8]{0:T(128)} %get-tuple-element.66.refs_1_, bf16[2048,1536]{1,0:T(8,128)(2,1)} %get-tuple-element.38.refs_2_.refs_3_.refs_4_.refs_5_, bf16[2048,1536]{1,0:T(8,128)(2,1)} %get-tuple-element.38.refs_2_.refs_3_.refs_4_.refs_5_, ...), custom_call_target="tpu_custom_call" | custom-call | tf_op jit(solution)/shard_map/attend/pallas_call | solution.py:49
  198.6 27.9 %dispatch.4.refs_1_.refs_0_ = bf16[8,2,4,256,256]{4,3,2,1,0:T(8,128)(2,1)} custom-call(s32[4,8,2,2048]{3,2,1,0:T(2,128)} %reshape.211.refs_0_.refs_1_, bf16[4,2048,256]{2,1,0:T(8,128)(2,1)} %bitcast.127), custom_call_target="tpu_custom_call" | custom-call | tf_op jit(solution)/shard_map/dispatch/pallas_call | solution.py:49
  241.7 19.6 %collective-permute-done.12 = bf16[2048,256]{1,0:T(8,128)(2,1)S(1)} collective-permute-done((bf16[2048,256]{1,0:T(8,128)(2,1)}, bf16[2048,256]{1,0:T(8,128)(2,1)S(1)}, u32[]{:S(2)}, u32[]{:S(2)}) %collective-permute-start.12) | collective-permute-done | bytes 1048608 | tf_op jit(solution)/shard_map/ppermute | solution.py:206
  285.8 27.8 %dispatch.6.refs_0_ = bf16[8,2,4,256,256]{4,3,2,1,0:T(8,128)(2,1)} custom-call(bf16[2048,512]{1,0:T(8,128)(2,1)} %multiply_convert_fusion.refs_1_.refs_0_, s32[4,8,2,2048]{3,2,1,0:T(2,128)} %reshape.211.refs_0_.refs_1_, bf16[4,2048,256]{2,1,0:T(8,128)(2,1)} %bitcast.132), custom_call_target="tpu_custom_call" | custom-call | tf_op jit(solution)/shard_map/dispatch/pallas_call | solution.py:49
  313.6 65.7 %all-to-all-done.1 = bf16[8,2,4,256,256]{4,3,2,1,0:T(8,128)(2,1)} async-done(((bf16[8,2,4,256,256]{4,3,2,1,0:T(8,128)(2,1)}), bf16[8,2,4,256,256]{4,3,2,1,0:T(8,128)(2,1)}, u32[]{:S(2)}, u32[]{:S(2)}) %all-to-all-start.1) | async-done | bytes 8388640 | tf_op jit(solution)/shard_map/all_to_all | solution.py:821
  388.6 94.4 %collective-permute-done.13 = f32[64,1024]{1,0:T(8,128)S(1)} collective-permute-done((f32[64,1024]{1,0:T(8,128)S(1)}, f32[64,1024]{1,0:T(8,128)S(1)}, u32[]{:S(2)}, u32[]{:S(2)}) %collective-permute-start.13) | collective-permute-done | bytes 262176 | tf_op jit(solution)/shard_map/ppermute | solution.py:206
  493.0 28.7 %dispatch.5.refs_0_ = bf16[8,1,4,256,512]{4,3,2,1,0:T(8,128)(2,1)} custom-call(bf16[4,2,2,4,256,256]{5,4,3,2,1,0:T(8,128)(2,1)} %bitcast.27.refs_0_.refs_1_.refs_3_, s32[4,8,1,2048]{3,2,1,0:T(1,128)} %get-tuple-element.111.refs_1_, bf16[4,2048,512]{2,1,0:T(8,128)(2,1)} %bitcast.118), custom_call_target="tpu_custom_call" | custom-call | tf_op jit(solution)/shard_map/dispatch/pallas_call | solution.py:49
  526.7 28.7 %dispatch.7.refs_0_ = bf16[8,1,4,256,512]{4,3,2,1,0:T(8,128)(2,1)} custom-call(bf16[4,2,2,4,256,256]{5,4,3,2,1,0:T(8,128)(2,1)} %bitcast.27.refs_0_.refs_1_.refs_3_, s32[4,8,1,2048]{3,2,1,0:T(1,128)} %get-tuple-element.112.refs_1_, bf16[4,2048,512]{2,1,0:T(8,128)(2,1)} %bitcast.119), custom_call_target="tpu_custom_call" | custom-call | tf_op jit(solution)/shard_map/dispatch/pallas_call | solution.py:49
  555.4 65.3 %all-to-all-done.3 = bf16[8,1,4,256,512]{4,3,2,1,0:T(8,128)(2,1)} async-done(((bf16[8,1,4,256,512]{4,3,2,1,0:T(8,128)(2,1)}), bf16[8,1,4,256,512]{4,3,2,1,0:T(8,128)(2,1)}, u32[]{:S(2)}, u32[]{:S(2)}) %all-to-all-start.3) | async-done | bytes 8388640 | tf_op jit(solution)/shard_map/all_to_all | solution.py:821
  648.6 37.4 %expert.2 = (bf16[2048,1024]{1,0:T(8,128)(2,1)}, bf16[2048,1024]{1,0:T(8,128)(2,1)}, bf16[2048,1024]{1,0:T(8,128)(2,1)}) custom-call(bf16[4,2,1,4,256,512]{5,4,3,2,1,0:T(8,128)(2,1)} %bitcast.31.refs_0_.refs_3_.refs_1_, bf16[4,2,2,4,256,256]{5,4,3,2,1,0:T(8,128)(2,1)} %bitcast.27.refs_0_.refs_1_.refs_3_, ...), custom_call_target="tpu_custom_call" | custom-call | tf_op jit(solution)/shard_map/expert/pallas_call | solution.py:49
  701.4 18.5 %all-to-all-done.4 = bf16[8,1,4,256,512]{4,3,2,1,0:T(8,128)(2,1)} async-done(((bf16[8,1,4,256,512]{4,3,2,1,0:T(8,128)(2,1)}), bf16[8,1,4,256,512]{4,3,2,1,0:T(8,128)(2,1)}, u32[]{:S(2)}, u32[]{:S(2)}) %all-to-all-start.4) | async-done | bytes 8388640 | tf_op jit(solution)/shard_map/all_to_all | solution.py:821
  720.0 37.1 %expert.3 = (bf16[2048,1024]{1,0:T(8,128)(2,1)}, bf16[2048,1024]{1,0:T(8,128)(2,1)}, bf16[2048,1024]{1,0:T(8,128)(2,1)}) custom-call(bf16[4,2,1,4,256,512]{5,4,3,2,1,0:T(8,128)(2,1)} %bitcast.34.refs_0_.refs_2_, bf16[4,2,2,4,256,256]{5,4,3,2,1,0:T(8,128)(2,1)} %bitcast.27.refs_0_.refs_1_.refs_3_, ...), custom_call_target="tpu_custom_call" | custom-call | tf_op jit(solution)/shard_map/expert/pallas_call | solution.py:49
  780.9 17.7 %produce.2 = (bf16[4,2,2,4,256,256]{5,4,3,2,1,0:T(8,128)(2,1)}, bf16[4,2,2,4,256,256]{5,4,3,2,1,0:T(8,128)(2,1)}, f32[2048,1]{1,0:T(8,128)}) custom-call(bf16[2048,1024]{1,0:T(8,128)(2,1)} %get-tuple-element.40.act_ref.refs_5_, bf16[2,2048,1024]{2,1,0:T(8,128)(2,1)} %w_ref.3, f32[2,2048,1]{2,1,0:T(8,128)} %reshape.281.refs_6_.prob_ref.refs_2_, ...), custom_call_target="tpu_custom_call" | custom-call | flops 8589934592 | bytes 37748736 | tf_op jit(solution)/shard_map/produce/pallas_call | solution.py:670
  815.6 17.7 %produce.3 = (bf16[4,2,2,4,256,256]{5,4,3,2,1,0:T(8,128)(2,1)}, bf16[4,2,2,4,256,256]{5,4,3,2,1,0:T(8,128)(2,1)}, f32[2048,1]{1,0:T(8,128)}) custom-call(bf16[2048,1024]{1,0:T(8,128)(2,1)} %get-tuple-element.42.act_ref.refs_6_, bf16[2,2048,1024]{2,1,0:T(8,128)(2,1)} %w_ref.3, ...), custom_call_target="tpu_custom_call", output_to_operand_aliasing={{0}: (5, {}), {1}: (6, {})} | custom-call | flops 8589934592 | bytes 37748736 | tf_op jit(solution)/shard_map/produce/pallas_call | solution.py:670
  851.0 30.6 %down_grad.1.refs_0_.refs_1_ = f32[2,2048,1024]{2,1,0:T(8,128)} custom-call(f32[2048,1]{1,0:T(8,128)} %get-tuple-element.41.refs_0_, f32[2048,1]{1,0:T(8,128)} %get-tuple-element.45.refs_1_, f32[2,2048,1]{2,1,0:T(8,128)} %reshape.281.refs_6_.prob_ref.refs_2_, bf16[4,2,2,4,256,256]{5,4,3,2,1,0:T(8,128)(2,1)} %bitcast.27.refs_0_.refs_1_.refs_3_, ...), custom_call_target="tpu_custom_call" | custom-call | flops 17179869184 | tf_op jit(solution)/shard_map/down_grad/pallas_call | solution.py:49
  881.6 31.3 %combine.4.refs_0_ = bf16[4,2048,256]{2,1,0:T(8,128)(2,1)} custom-call(f32[2,2048,1024]{2,1,0:T(8,128)} %down_grad.1.refs_0_.refs_1_, f32[8,512]{1,0:T(8,128)} %after.24.refs_1_, s32[4,2048,16]{2,1,0:T(8,128)} %bitcast.128, bf16[8,2,4,256,256]{4,3,2,1,0:T(8,128)(2,1)} %all-to-all-done.5.refs_1_.refs_3_), custom_call_target="tpu_custom_call" | custom-call | flops 17179869184 | tf_op jit(solution)/shard_map/combine/pallas_call | solution.py:49
  939.0 45.8 %gate_grad.1 = (f32[2,2048,1024]{2,1,0:T(8,128)}, f32[2,2048,1024]{2,1,0:T(8,128)}) custom-call(bf16[4,2048,256]{2,1,0:T(8,128)(2,1)} %combine.4.refs_0_, bf16[4,2,1,4,256,512]{5,4,3,2,1,0:T(8,128)(2,1)} %bitcast.31.refs_0_.refs_3_.refs_1_, bf16[4,2,1,4,256,512]{5,4,3,2,1,0:T(8,128)(2,1)} %bitcast.34.refs_0_.refs_2_, ...), custom_call_target="tpu_custom_call" | custom-call | tf_op jit(solution)/shard_map/gate_grad/pallas_call | solution.py:49
  984.9 19.9 %select_reduce_fusion = f32[64,2048]{1,0:T(8,128)S(1)} fusion(f32[64,256]{1,0:T(8,128)S(1)} %copy-done.50, f32[64,2048]{1,0:T(8,128)S(1)} %copy-done.44, f32[256]{0:T(256)S(1)} %copy-done.71), kind=kLoop, calls=%fused_computation.4 | loop fusion | flops 100532224 | bytes 1115136 | tf_op jit(solution)/shard_map/reduce_sum | solution.py:1005
  1007.6 25.4 %all-to-all-done.7.refs_4_.refs_1_ = bf16[8,2,4,256,256]{4,3,2,1,0:T(8,128)(2,1)} async-done(((bf16[8,2,4,256,256]{4,3,2,1,0:T(8,128)(2,1)}), bf16[8,2,4,256,256]{4,3,2,1,0:T(8,128)(2,1)}, u32[]{:S(2)}, u32[]{:S(2)}) %all-to-all-start.7) | async-done | bytes 8388640 | tf_op jit(solution)/shard_map/all_to_all | solution.py:821
  1033.0 30.9 %combine.5 = bf16[4,2048,256]{2,1,0:T(8,128)(2,1)} custom-call(f32[2,2048,1024]{2,1,0:T(8,128)} %get-tuple-element.35.refs_0_, bf16[2048,256]{1,0:T(8,128)(2,1)} %bitcast.135, f32[2048,512]{1,0:T(8,128)} %fusion.75.refs_2_, s32[4,2048,16]{2,1,0:T(8,128)} %bitcast.129, bf16[8,2,4,256,256]{4,3,2,1,0:T(8,128)(2,1)} %all-to-all-done.7.refs_4_.refs_1_), custom_call_target="tpu_custom_call" | custom-call | flops 17179869184 | tf_op jit(solution)/shard_map/combine/pallas_call | solution.py:49
  1079.2 58.0 %reduce-scatter.10.cloned.1.call-done = bf16[1,2048,256]{2,1,0:T(8,128)(2,1)} async-done(((bf16[4,2048,256]{2,1,0:T(8,128)(2,1)}), bf16[1,2048,256]{2,1,0:T(8,128)(2,1)}) %reduce-scatter.10.cloned.1.call-update) | async-done | bytes 1048592 | tf_op jit(solution)/shard_map/reduce_scatter | solution.py:901
  1142.4 33.1 %psum.36 = f32[2048]{0:T(1024)S(1)} all-reduce(f32[2048]{0:T(1024)S(1)} %get-tuple-element.62), channel_id=1, replica_groups=mesh['row'=4,'z'=4,'core'=2] {'row'}, use_global_device_ids=true, to_apply=%region_12.14 | all-reduce | flops 2048 | bytes 16384 | tf_op jit(solution)/shard_map/psum | solution.py:1033
  1181.7 30.9 %combine.6.refs_1_ = bf16[4,2048,256]{2,1,0:T(8,128)(2,1)} custom-call(bf16[2048,512]{1,0:T(8,128)(2,1)} %get-tuple-element.71.refs_0_, s32[4,2048,16]{2,1,0:T(8,128)} %bitcast.130, bf16[8,2,4,256,256]{4,3,2,1,0:T(8,128)(2,1)} %all-to-all-done.9.refs_2_.refs_1_), custom_call_target="tpu_custom_call" | custom-call | flops 17179869184 | tf_op jit(solution)/shard_map/combine/pallas_call | solution.py:49
  1219.3 21.3 %collective-permute-done.20.refs_4_.refs_5_.refs_3_ = bf16[2048,256]{1,0:T(8,128)(2,1)} collective-permute-done((bf16[2048,256]{1,0:T(8,128)(2,1)S(1)}, bf16[2048,256]{1,0:T(8,128)(2,1)}, u32[]{:S(2)}, u32[]{:S(2)}) %collective-permute-start.20) | collective-permute-done | bytes 1048608 | tf_op jit(solution)/shard_map/ppermute | solution.py:206
  1242.6 20.4 %collective-permute-done.21.refs_5_.refs_6_.refs_4_ = bf16[2048,256]{1,0:T(8,128)(2,1)} collective-permute-done((bf16[2048,256]{1,0:T(8,128)(2,1)S(1)}, bf16[2048,256]{1,0:T(8,128)(2,1)}, u32[]{:S(2)}, u32[]{:S(2)}) %collective-permute-start.21) | collective-permute-done | bytes 1048608 | tf_op jit(solution)/shard_map/ppermute | solution.py:206
  1264.5 19.9 %collective-permute-done.24.refs_8_.refs_9_.refs_7_ = bf16[2048,256]{1,0:T(8,128)(2,1)} collective-permute-done((bf16[2048,256]{1,0:T(8,128)(2,1)}, bf16[2048,256]{1,0:T(8,128)(2,1)}, u32[]{:S(2)}, u32[]{:S(2)}) %collective-permute-start.24) | collective-permute-done | bytes 1048608 | tf_op jit(solution)/shard_map/ppermute | solution.py:206
  1320.2 66.0 %attend_back.1 = (bf16[2048,1536]{1,0:T(8,128)(2,1)}, f32[2,128]{1,0:T(2,128)}, f32[2048,1]{1,0:T(8,128)}) custom-call(s32[8]{0:T(128)} %get-tuple-element.67.refs_0_, s32[8]{0:T(128)} %get-tuple-element.66.refs_1_, bf16[1024,512]{1,0:T(8,128)(2,1)} %bitcast.124, bf16[2048,1536]{1,0:T(8,128)(2,1)} %get-tuple-element.38.refs_2_.refs_3_.refs_4_.refs_5_, ...), custom_call_target="tpu_custom_call" | custom-call | tf_op jit(solution)/shard_map/attend_back/pallas_call | solution.py:49
  1404.2 30.9 %combine.7 = bf16[4,2048,256]{2,1,0:T(8,128)(2,1)} custom-call(bf16[2048,512]{1,0:T(8,128)(2,1)} %convolution_convert_fusion.2.refs_0_, bf16[2048,512]{1,0:T(8,128)(2,1)} %convolution_convert_fusion.1.refs_1_, s32[4,2048,16]{2,1,0:T(8,128)} %bitcast.131, bf16[8,2,4,256,256]{4,3,2,1,0:T(8,128)(2,1)} %all-to-all-done.10.refs_1_.refs_3_), custom_call_target="tpu_custom_call" | custom-call | flops 17179869184 | tf_op jit(solution)/shard_map/combine/pallas_call | solution.py:49
  1545.1 26.9 %reduce-scatter.18.cloned.1.call-done = bf16[256,1536]{1,0:T(8,128)(2,1)} async-done(((bf16[1024,1536]{1,0:T(8,128)(2,1)}), bf16[256,1536]{1,0:T(8,128)(2,1)}) %reduce-scatter.18.cloned.1.call-update) | async-done | bytes 786448 | tf_op jit(solution)/shard_map/reduce_scatter | solution.py:253
  (417 shorter events, 487.2 us)
Async XLA Ops:
  7.2 83.5 %all-gather.10.cloned.1.call-start = ((), (), s32[]{:S(2)}) async-start(), calls=%async_computation.18 | async-start | bytes 2949120 | tf_op jit(solution)/shard_map/all_gather | solution.py:878
  9.9 107.8 %all-gather.12.cloned.1.call-start = ((), (), s32[]{:S(2)}) async-start(), calls=%async_computation.19 | async-start | bytes 7077888 | tf_op jit(solution)/shard_map/all_gather | solution.py:872
  12.1 186.6 %all-gather.14.cloned.1.call-start = ((), (), s32[]{:S(2)}) async-start(), calls=%async_computation.27 | async-start | bytes 5242880 | tf_op jit(solution)/shard_map/all_gather | solution.py:906
  17.7 44.6 %collective-permute-start.4 = (bf16[2064,256]{1,0:T(8,128)(2,1)S(1)}, bf16[2064,256]{1,0:T(8,128)(2,1)}, u32[]{:S(2)}, u32[]{:S(2)}) collective-permute-start(bf16[2064,256]{1,0:T(8,128)(2,1)S(1)} %get-tuple-element.94.refs_4_.refs_12_), channel_id=1, source_target_pairs={{0,8},{8,0},{16,24},{24,16},{1,9},{9,1},{17,25},{25,17},{2,10},{10... | collective-permute-start | bytes 3170312 | tf_op jit(solution)/shard_map/ppermute | solution.py:206
  18.2 45.5 %collective-permute-start.5 = (bf16[2064,256]{1,0:T(8,128)(2,1)S(1)}, bf16[2064,256]{1,0:T(8,128)(2,1)}, u32[]{:S(2)}, u32[]{:S(2)}) collective-permute-start(bf16[2064,256]{1,0:T(8,128)(2,1)S(1)} %get-tuple-element.95.refs_3_.refs_11_), channel_id=1, source_target_pairs={{0,16},{8,24},{16,0},{24,8},{1,17},{9,25},{17,1},{25,9},{2,18},{10... | collective-permute-start | bytes 3170312 | tf_op jit(solution)/shard_map/ppermute | solution.py:206
  74.1 211.7 %all-gather.18.cloned.1.call-start = ((), (), s32[]{:S(2)}) async-start(), calls=%async_computation.29 | async-start | bytes 5242880 | tf_op jit(solution)/shard_map/all_gather | solution.py:906
  182.9 44.8 %collective-permute-start.11 = (bf16[2048,512]{1,0:T(8,128)(2,1)}, bf16[2048,512]{1,0:T(8,128)(2,1)}, u32[]{:S(2)}, u32[]{:S(2)}) collective-permute-start(bf16[2048,512]{1,0:T(8,128)(2,1)} %convolution_convert_fusion.3), channel_id=1, source_target_pairs={{0,16},{8,24},{16,0},{24,8},{1,17},{9,25},{17,1},{25,9},{2,18},{10... | collective-permute-start | bytes 6291464 | tf_op jit(solution)/shard_map/ppermute | solution.py:206
  187.0 43.0 %collective-permute-start.9 = (bf16[2048,512]{1,0:T(8,128)(2,1)}, bf16[2048,512]{1,0:T(8,128)(2,1)}, u32[]{:S(2)}, u32[]{:S(2)}) collective-permute-start(bf16[2048,512]{1,0:T(8,128)(2,1)} %convolution_convert_fusion.4), channel_id=1, source_target_pairs={{0,8},{8,0},{16,24},{24,16},{1,9},{9,1},{17,25},{25,17},{2,10},{10... | collective-permute-start | bytes 6291464 | tf_op jit(solution)/shard_map/ppermute | solution.py:206
  280.2 99.0 %all-to-all-start.1 = ((bf16[8,2,4,256,256]{4,3,2,1,0:T(8,128)(2,1)}), bf16[8,2,4,256,256]{4,3,2,1,0:T(8,128)(2,1)}, u32[]{:S(2)}, u32[]{:S(2)}) async-start(bf16[8,2,4,256,256]{4,3,2,1,0:T(8,128)(2,1)} %after.19), calls=%async_computation.1 | async-start | bytes 16777216 | tf_op jit(solution)/shard_map/all_to_all | solution.py:821
  285.2 207.8 %all-gather.16.cloned.1.call-start = ((), (), s32[]{:S(2)}) async-start(), calls=%async_computation.28 | async-start | bytes 10485760 | tf_op jit(solution)/shard_map/all_gather | solution.py:948
  379.2 142.5 %all-to-all-start.2 = ((bf16[8,2,4,256,256]{4,3,2,1,0:T(8,128)(2,1)}), bf16[8,2,4,256,256]{4,3,2,1,0:T(8,128)(2,1)}, u32[]{:S(2)}, u32[]{:S(2)}) async-start(bf16[8,2,4,256,256]{4,3,2,1,0:T(8,128)(2,1)} %after.21), calls=%async_computation.2 | async-start | bytes 16777216 | tf_op jit(solution)/shard_map/all_to_all | solution.py:821
  385.1 97.8 %collective-permute-start.13 = (f32[64,1024]{1,0:T(8,128)S(1)}, f32[64,1024]{1,0:T(8,128)S(1)}, u32[]{:S(2)}, u32[]{:S(2)}) collective-permute-start(f32[64,1024]{1,0:T(8,128)S(1)} %get-tuple-element.117), channel_id=1, source_target_pairs={{0,8},{8,0},{16,24},{24,16},{1,9},{9,1},{17,25},{25,17},{2,10},{10... | collective-permute-start | bytes 786440 | tf_op jit(solution)/shard_map/ppermute | solution.py:206
  387.1 95.9 %collective-permute-start.15 = (f32[64,1024]{1,0:T(8,128)S(1)}, f32[64,1024]{1,0:T(8,128)S(1)}, u32[]{:S(2)}, u32[]{:S(2)}) collective-permute-start(f32[64,1024]{1,0:T(8,128)S(1)} %get-tuple-element.118), channel_id=1, source_target_pairs={{0,16},{8,24},{16,0},{24,8},{1,17},{9,25},{17,1},{25,9},{2,18},{10... | collective-permute-start | bytes 786440 | tf_op jit(solution)/shard_map/ppermute | solution.py:206
  521.7 99.0 %all-to-all-start.3 = ((bf16[8,1,4,256,512]{4,3,2,1,0:T(8,128)(2,1)}), bf16[8,1,4,256,512]{4,3,2,1,0:T(8,128)(2,1)}, u32[]{:S(2)}, u32[]{:S(2)}) async-start(bf16[8,1,4,256,512]{4,3,2,1,0:T(8,128)(2,1)} %after.22), calls=%async_computation.3 | async-start | bytes 16777216 | tf_op jit(solution)/shard_map/all_to_all | solution.py:821
  620.7 99.2 %all-to-all-start.4 = ((bf16[8,1,4,256,512]{4,3,2,1,0:T(8,128)(2,1)}), bf16[8,1,4,256,512]{4,3,2,1,0:T(8,128)(2,1)}, u32[]{:S(2)}, u32[]{:S(2)}) async-start(bf16[8,1,4,256,512]{4,3,2,1,0:T(8,128)(2,1)} %after.23), calls=%async_computation.4 | async-start | bytes 16777216 | tf_op jit(solution)/shard_map/all_to_all | solution.py:821
  772.5 109.1 %all-to-all-start.5 = ((bf16[8,2,4,256,256]{4,3,2,1,0:T(8,128)(2,1)}), bf16[8,2,4,256,256]{4,3,2,1,0:T(8,128)(2,1)}, u32[]{:S(2)}, u32[]{:S(2)}) async-start(bf16[8,2,4,256,256]{4,3,2,1,0:T(8,128)(2,1)} %bitcast.115), calls=%async_computation.5 | async-start | bytes 16777216 | tf_op jit(solution)/shard_map/all_to_all | solution.py:821
  777.6 255.4 %reduce-scatter.8.cloned.1.call-start = ((), (), s32[]{:S(2)}) async-start(), calls=%async_computation.20 | async-start | bytes 5242880 | tf_op jit(solution)/shard_map/reduce_scatter | solution.py:901
  934.0 99.0 %all-to-all-start.7 = ((bf16[8,2,4,256,256]{4,3,2,1,0:T(8,128)(2,1)}), bf16[8,2,4,256,256]{4,3,2,1,0:T(8,128)(2,1)}, u32[]{:S(2)}, u32[]{:S(2)}) async-start(bf16[8,2,4,256,256]{4,3,2,1,0:T(8,128)(2,1)} %bitcast.114), calls=%async_computation.8 | async-start | bytes 16777216 | tf_op jit(solution)/shard_map/all_to_all | solution.py:821
  939.0 198.2 %reduce-scatter.10.cloned.1.call-start = ((), (), s32[]{:S(2)}) async-start(), calls=%async_computation.21 | async-start | bytes 5242880 | tf_op jit(solution)/shard_map/reduce_scatter | solution.py:901
  1074.0 107.7 %all-to-all-start.9 = ((bf16[8,2,4,256,256]{4,3,2,1,0:T(8,128)(2,1)}), bf16[8,2,4,256,256]{4,3,2,1,0:T(8,128)(2,1)}, u32[]{:S(2)}, u32[]{:S(2)}) async-start(bf16[8,2,4,256,256]{4,3,2,1,0:T(8,128)(2,1)} %bitcast.116), calls=%async_computation.11 | async-start | bytes 16777216 | tf_op jit(solution)/shard_map/all_to_all | solution.py:821
  1079.1 307.2 %reduce-scatter.14.cloned.1.call-start = ((), (), s32[]{:S(2)}) async-start(), calls=%async_computation.23 | async-start | bytes 147456 | tf_op jit(solution)/shard_map/reduce_scatter | solution.py:1025
  1217.2 169.1 %reduce-scatter.12.cloned.1.call-start = ((), (), s32[]{:S(2)}) async-start(), calls=%async_computation.22 | async-start | bytes 5242880 | tf_op jit(solution)/shard_map/reduce_scatter | solution.py:901
  1217.2 45.8 %collective-permute-start.21 = (bf16[2048,256]{1,0:T(8,128)(2,1)S(1)}, bf16[2048,256]{1,0:T(8,128)(2,1)}, u32[]{:S(2)}, u32[]{:S(2)}) collective-permute-start(bf16[2048,256]{1,0:T(8,128)(2,1)S(1)} %get-tuple-element.96.refs_3_.refs_4_.refs_2_), channel_id=1, source_target_pairs={{0,8},{8,0},{16,24},{24,16},{1,9},{9,1},{17,25},{25,17},{2,10},{10... | collective-permute-start | bytes 3145736 | tf_op jit(solution)/shard_map/ppermute | solution.py:206
  1218.8 45.7 %collective-permute-start.22 = (bf16[2048,256]{1,0:T(8,128)(2,1)S(1)}, bf16[2048,256]{1,0:T(8,128)(2,1)}, u32[]{:S(2)}, u32[]{:S(2)}) collective-permute-start(bf16[2048,256]{1,0:T(8,128)(2,1)S(1)} %get-tuple-element.97.refs_2_.refs_3_.refs_1_), channel_id=1, source_target_pairs={{0,16},{8,24},{16,0},{24,8},{1,17},{9,25},{17,1},{25,9},{2,18},{10... | collective-permute-start | bytes 3145736 | tf_op jit(solution)/shard_map/ppermute | solution.py:206
  1240.5 43.8 %collective-permute-start.24 = (bf16[2048,256]{1,0:T(8,128)(2,1)}, bf16[2048,256]{1,0:T(8,128)(2,1)}, u32[]{:S(2)}, u32[]{:S(2)}) collective-permute-start(bf16[2048,256]{1,0:T(8,128)(2,1)} %collective-permute-done.20.refs_4_.refs_5_.refs_3_), channel_id=1, source_target_pairs={{0,16},{8,24},{16,0},{24,8},{1,17},{9,25},{17,1},{25,9},{2,18},{10... | collective-permute-start | bytes 3145736 | tf_op jit(solution)/shard_map/ppermute | solution.py:206
  1242.1 42.3 %collective-permute-start.25 = (bf16[2048,256]{1,0:T(8,128)(2,1)}, bf16[2048,256]{1,0:T(8,128)(2,1)}, u32[]{:S(2)}, u32[]{:S(2)}) collective-permute-start(bf16[2048,256]{1,0:T(8,128)(2,1)} %collective-permute-done.23.refs_7_.refs_8_.refs_6_), channel_id=1, source_target_pairs={{0,8},{8,0},{16,24},{24,16},{1,9},{9,1},{17,25},{25,17},{2,10},{10... | collective-permute-start | bytes 3145736 | tf_op jit(solution)/shard_map/ppermute | solution.py:206
  1284.4 101.9 %all-to-all-start.10 = ((bf16[8,2,4,256,256]{4,3,2,1,0:T(8,128)(2,1)}), bf16[8,2,4,256,256]{4,3,2,1,0:T(8,128)(2,1)}, u32[]{:S(2)}, u32[]{:S(2)}) async-start(bf16[8,2,4,256,256]{4,3,2,1,0:T(8,128)(2,1)} %bitcast.117), calls=%async_computation.12 | async-start | bytes 16777216 | tf_op jit(solution)/shard_map/all_to_all | solution.py:821
  1289.4 205.8 %reduce-scatter.20.cloned.1.call-start = ((), (), s32[]{:S(2)}) async-start(), calls=%async_computation.26 | async-start | bytes 1310720 | tf_op jit(solution)/shard_map/reduce_scatter | solution.py:253
  1320.2 220.4 %reduce-scatter.16.cloned.1.call-start = ((), (), s32[]{:S(2)}) async-start(), calls=%async_computation.24 | async-start | bytes 5242880 | tf_op jit(solution)/shard_map/reduce_scatter | solution.py:901
  1395.7 41.7 %collective-permute-start.29 = (bf16[2048,512]{1,0:T(8,128)(2,1)}, bf16[2048,512]{1,0:T(8,128)(2,1)S(1)}, u32[]{:S(2)}, u32[]{:S(2)}) collective-permute-start(bf16[2048,512]{1,0:T(8,128)(2,1)} %convolution_convert_fusion.1.refs_1_), channel_id=1, source_target_pairs={{0,16},{8,24},{16,0},{24,8},{1,17},{9,25},{17,1},{25,9},{2,18},{10... | collective-permute-start | bytes 6291464 | tf_op jit(solution)/shard_map/ppermute | solution.py:206
  1402.7 42.2 %collective-permute-start.27 = (bf16[2048,512]{1,0:T(8,128)(2,1)}, bf16[2048,512]{1,0:T(8,128)(2,1)}, u32[]{:S(2)}, u32[]{:S(2)}) collective-permute-start(bf16[2048,512]{1,0:T(8,128)(2,1)} %convolution_convert_fusion.2.refs_0_), channel_id=1, source_target_pairs={{0,8},{8,0},{16,24},{24,16},{1,9},{9,1},{17,25},{25,17},{2,10},{10... | collective-permute-start | bytes 6291464 | tf_op jit(solution)/shard_map/ppermute | solution.py:206
  1435.1 136.9 %reduce-scatter.18.cloned.1.call-start = ((), (), s32[]{:S(2)}) async-start(), calls=%async_computation.25 | async-start | bytes 3932160 | tf_op jit(solution)/shard_map/reduce_scatter | solution.py:253
  (104 other events, 2027.9 us)
Sparse Core Ops, SparseCore 0:
  10.2 36.4 all-gather.9
  48.3 69.3 all-gather.11
  119.3 79.3 all-gather.13
  200.0 79.2 all-gather.17
  287.3 148.7 all-gather.15
  913.0 76.0 reduce-scatter.7
  1064.0 73.1 reduce-scatter.9
  1217.3 27.8 reduce-scatter.13
  1247.5 74.9 reduce-scatter.11
  1324.6 27.8 reduce-scatter.19
  1435.2 73.0 reduce-scatter.15
  1510.5 61.4 reduce-scatter.17

commit v5 on v4

--- a/solution.py
+++ b/solution.py
@@ -937,19 +937,19 @@
     ]
     normed_two = (middle * second_factor * second_gain).astype(BF)
 
-    logits = row_sum(dot(router_here, normed_two, 1, 1))
+    later_picked = [dispatch(slots, spread, capacity, [normed_two]) for spread in spread_cots[1:]]
+    logits = row_sum(after(dot(router_here, normed_two, 1, 1), *later_picked))
     raised = jnp.exp(logits)
     router_probs = raised / jnp.sum(raised, axis=0, keepdims=True)
 
     cots = [swap(after(first_picked, normed_two)).reshape(dims)]
-    for spread in spread_cots[1:]:
-        picked = dispatch(slots, spread, capacity, [normed_two])
-        cots.append(swap(after(picked, cots[-1])).reshape(dims))
+    for picked in later_picked:
+        cots.append(swap(after(picked, cots[-1], logits)).reshape(dims))
     spread_rows = lax.all_gather(normed_two, "z", axis=0)
     rows = []
     for index in range(local):
         picked = dispatch(slots[:, :, index : index + 1], spread_rows, capacity, cots[:1])
-        rows.append(swap(after(picked, logits, cots[-1], *rows[-1:])).reshape(expert_dims))
+        rows.append(swap(after(picked, cots[-1], *rows[-1:])).reshape(expert_dims))
     own_slots = lax.dynamic_slice_in_dim(position, row_index * experts_here, experts_here, 0)
     own_probs = lax.dynamic_slice_in_dim(router_probs, row_index * experts_here, experts_here, 0)
     order = jnp.arange(capacity, dtype=jnp.int32).astype(F32)
@@ -996,12 +996,12 @@
         z_count * core_count, local * capacity
     )
     back_rows = [swap(buffers[0].reshape(swapped_dims))]
-    to_groups = after(to_groups, back_rows[0], buffers[1])
-    of_group = lax.all_to_all(to_groups, TOKENS_AXES, 0, 0, tiled=True).reshape(-1, capacity)
+    ready = after(buffers[1], *inners)
+    back_rows.append(swap(ready.reshape(swapped_dims)))
+    of_group = lax.all_to_all(
+        after(to_groups, *back_rows), TOKENS_AXES, 0, 0, tiled=True
+    ).reshape(-1, capacity)
     slot_grads = jnp.sum(small_row_gather(of_group).reshape(E, pieces, capacity), axis=1)
-    grad_down = down_grad(cots, prob, activated, inners)
-    ready = after(buffers[1], grad_down, slot_grads)
-    back_rows.append(swap(ready.reshape(swapped_dims)))
     grad_prob = jnp.sum(
         jnp.where(position[:, None, :] == order[None, :, None], slot_grads[:, :, None], 0.0), axis=1
     )
@@ -1009,13 +1009,13 @@
         router_probs * (grad_prob - jnp.sum(router_probs * grad_prob, axis=0, keepdims=True))
     ).astype(BF)
     from_router = dot(grad_logits, router_here, 0, 0)
-    first_sum = combine(slots_by_token, [back_rows[0]], 0, width, [grad_down, to_groups])
+    first_sum = combine(slots_by_token, [back_rows[0]], 0, width, [ready])
     grad_gate, grad_up = gate_grad(rows, grad_gate_pre, grad_up_pre, [first_sum])
     first_sum = scatter_back(first_sum)
-    second_sum = scatter_back(
-        combine(slots_by_token, [back_rows[1]], 0, width, [grad_gate, first_sum, from_router])
-    )
-    grad_normed_two = from_router + jnp.concatenate(
+    second_sum = combine(slots_by_token, [back_rows[1]], 0, width, [grad_gate, first_sum])
+    grad_down = down_grad(cots, prob, activated, [second_sum, slot_grads])
+    second_sum = scatter_back(second_sum)
+    grad_normed_two = after(from_router, grad_down) + jnp.concatenate(
         [first_sum, second_sum], axis=1
     ).astype(F32)
     router_part = dot(grad_logits, normed_two)
@@ -1039,8 +1039,8 @@
     grad_feedforward_gain = jnp.sum(grad_normed_two * middle * second_factor, axis=0)
 
     grad_branch = grad_middle.astype(BF)
-    made_rows = [swap(after(made_buffers[0], back_rows[1], router_swapped).reshape(swapped_dims))]
-    branch_pieces, branch_starts = row_gather(after(grad_branch, made_rows[0]))
+    made_rows = [swap(after(made_buffers[0], back_rows[1], slot_grads).reshape(swapped_dims))]
+    branch_pieces, branch_starts = row_gather(after(grad_branch, made_rows[0], router_swapped))
     made_rows.append(swap(after(made_buffers[1], *branch_pieces).reshape(swapped_dims)))
     made_sums = [combine(slots_by_token, [made_rows[0]], 0, width, [grad_branch])]
     grad_projection = projection_grad(branch_starts, branch_pieces, mixed, made_sums)
@@ -1052,12 +1052,10 @@
         heads, grad_mixed, mixed, sums, segment, low, high, raw, cosine, sine, head_gains,
         [projection_sum],
     )
-    from_experts = [scatter_back(made_sums[0])]
-    grad_raw = after(grad_raw, made_rows[1], from_experts[0], grad_router)
+    made_sums.append(combine(slots_by_token, [made_rows[1]], 0, width, [grad_raw]))
+    from_experts = [scatter_back(each) for each in made_sums]
+    grad_raw = after(grad_raw, made_sums[1], from_experts[0], grad_router)
     grad_first, sent, received = row_scatter(grad_raw, row_scatter_order(qkv_full))
-    from_experts.append(
-        scatter_back(combine(slots_by_token, [made_rows[1]], 0, width, sent))
-    )
     small = jnp.concatenate([along.reshape(-1, HS), head_gain_grads], axis=0)
     small = jnp.sum(small_row_gather(small), axis=0)
     first_inner = small[:-2].reshape(-1, 1) / first_factor

time: 1600 us -> 1560 us (0.975)
  waiting for transfers between devices: 560 us -> 523 us
    reduce_scatter x4, waiting for transfers between devices: 58.1 us -> 0.03 us  [scatter_back(): lax.psum_scatter(summed, 'z', scatter_dimension=0, tiled=True)]
    all_gather x1, waiting for transfers between devices: 0.01 us -> 34.7 us  [per_device(): spread_rows = lax.all_gather(normed_two, 'z', axis=0)]
    reduce_scatter x2, waiting for transfers between devices: 26.9 us -> 0.02 us  [z_scatter(): return lax.psum_scatter(values, 'z', scatter_dimension=0, tiled=True)]
  transfers between devices with their start and end apart: 57 -> 58, of which waited for: 36 -> 36; matrix products, arithmetic and copies ran while one was open for 12% -> 12% of each run, Pallas kernels for 31% -> 33%
where the time goes in v5:
time: 1560 us; the launch traced here: 1540 us
  Pallas kernels  629 us (40%)
  waiting for transfers between devices  523 us (34%)
  other arithmetic  95.3 us (6%)
  starting transfers between devices  94.3 us (6%)
  blocking collectives  74.7 us (5%)
  matrix products  62.5 us (4%)
  local copies, waits for them, and re-layouts  48.2 us (3%)
  between operations  15.7 us (1%)
    pallas_call x17, Pallas kernels, call(): return lambda *args: kernel(*args[:prefetch], *deps, *args[prefetch:])  532 us
    ppermute x33, waiting for transfers between devices, permute(): return lax.ppermute(values, 'row', [(i, i ^ mask) for i in range(4)])  273 us
    all_to_all x8, waiting for transfers between devices, swap(): lax.all_to_all(rows, SWAP_AXES, split_axis=0, concat_axis=0, tiled=True)  186 us
    pallas_call x4, Pallas kernels, rows_back(): pl.pallas_call(rows_back_body, out_shape=shape(dims, BF), grid=(cores, ro...  61.7 us
    dot_general x12, matrix products, dot(): lax.dot_general(left, right, (((left_dim,), (right_dim,)), ((), ())), pre...  58.7 us
    all_to_all x8, starting transfers between devices, swap(): lax.all_to_all(rows, SWAP_AXES, split_axis=0, concat_axis=0, tiled=True)  41.1 us
    ppermute x33, starting transfers between devices, permute(): return lax.ppermute(values, 'row', [(i, i ^ mask) for i in range(4)])  40.5 us
    psum x1, blocking collectives, per_device(): lax.psum(jnp.sum(scaled_two * middle, axis=1), 'row')[:, None]  35.7 us
  transfers between devices with their start and end apart: 58, of which 36 were waited for; matrix products, arithmetic and copies ran while one was open for 12% of the time, Pallas kernels for 33%

profile of v5, /device:TPU:0, one launch (start us, length us, event | category | flops | bytes accessed | tf_op | source)
XLA Modules:
  0.0 1542.2 jit_solution(13226587812870868976)
XLA Ops:
  19.7 20.6 %collective-permute-done.3.refs_5_.refs_13_.refs_1_ = bf16[2064,256]{1,0:T(8,128)(2,1)S(1)} collective-permute-done((bf16[2064,256]{1,0:T(8,128)(2,1)S(1)}, bf16[2064,256]{1,0:T(8,128)(2,1)S(1)}, u32[]{:S(2)}, u32[]{:S(2)}) %collective-permute-start.3) | collective-permute-done | bytes 1056800 | tf_op jit(solution)/shard_map/ppermute | solution.py:206
  42.4 19.9 %collective-permute-done.4.refs_6_.refs_14_.refs_2_ = bf16[2064,256]{1,0:T(8,128)(2,1)} collective-permute-done((bf16[2064,256]{1,0:T(8,128)(2,1)S(1)}, bf16[2064,256]{1,0:T(8,128)(2,1)}, u32[]{:S(2)}, u32[]{:S(2)}) %collective-permute-start.4) | collective-permute-done | bytes 1056800 | tf_op jit(solution)/shard_map/ppermute | solution.py:206
  118.3 31.2 %project.1 = (bf16[2048,2048]{1,0:T(8,128)(2,1)}, bf16[2048,1536]{1,0:T(8,128)(2,1)}, f32[2048,1024]{1,0:T(8,128)}, f32[2048,1]{1,0:T(8,128)}) custom-call(s32[8]{0:T(128)} %stack.101.refs_0_, s32[4,4,4,2048]{3,2,1,0:T(4,128)} %convert_element_type.133.refs_1_, bf16[64,512]{1,0:T(8,128)(2,1)} %bitcast.143, bf16[2064,256]{1,0:T(8,128)(2,1)} %copy-done.24, ...), custom_call_target="tpu_custom_call" | custom-call | tf_op jit(solution)/shard_map/project/pallas_call | solution.py:49
  149.5 27.9 %attend.1 = (bf16[2048,512]{1,0:T(8,128)(2,1)}, f32[4,2048,1]{2,1,0:T(8,128)}) custom-call(s32[8]{0:T(128)} %get-tuple-element.67.refs_0_, s32[8]{0:T(128)} %get-tuple-element.66.refs_1_, bf16[2048,1536]{1,0:T(8,128)(2,1)} %get-tuple-element.38.refs_2_.refs_3_.refs_4_.refs_5_, bf16[2048,1536]{1,0:T(8,128)(2,1)} %get-tuple-element.38.refs_2_.refs_3_.refs_4_.refs_5_, ...), custom_call_target="tpu_custom_call" | custom-call | tf_op jit(solution)/shard_map/attend/pallas_call | solution.py:49
  198.6 27.9 %dispatch.4.refs_1_.refs_0_ = bf16[8,2,4,256,256]{4,3,2,1,0:T(8,128)(2,1)} custom-call(s32[4,8,2,2048]{3,2,1,0:T(2,128)} %reshape.211.refs_0_.refs_1_, bf16[4,2048,256]{2,1,0:T(8,128)(2,1)} %bitcast.127), custom_call_target="tpu_custom_call" | custom-call | tf_op jit(solution)/shard_map/dispatch/pallas_call | solution.py:49
  241.7 19.6 %collective-permute-done.12 = bf16[2048,256]{1,0:T(8,128)(2,1)S(1)} collective-permute-done((bf16[2048,256]{1,0:T(8,128)(2,1)}, bf16[2048,256]{1,0:T(8,128)(2,1)S(1)}, u32[]{:S(2)}, u32[]{:S(2)}) %collective-permute-start.12) | collective-permute-done | bytes 1048608 | tf_op jit(solution)/shard_map/ppermute | solution.py:206
  285.8 27.9 %dispatch.5.refs_1_.refs_0_ = bf16[8,2,4,256,256]{4,3,2,1,0:T(8,128)(2,1)} custom-call(bf16[2048,512]{1,0:T(8,128)(2,1)} %multiply_convert_fusion.refs_0_.refs_1_, s32[4,8,2,2048]{3,2,1,0:T(2,128)} %reshape.211.refs_0_.refs_1_, bf16[4,2048,256]{2,1,0:T(8,128)(2,1)} %bitcast.132), custom_call_target="tpu_custom_call" | custom-call | tf_op jit(solution)/shard_map/dispatch/pallas_call | solution.py:49
  319.8 64.1 %collective-permute-done.13 = f32[64,1024]{1,0:T(8,128)S(1)} collective-permute-done((f32[64,1024]{1,0:T(8,128)S(1)}, f32[64,1024]{1,0:T(8,128)S(1)}, u32[]{:S(2)}, u32[]{:S(2)}) %collective-permute-start.13) | collective-permute-done | bytes 262176 | tf_op jit(solution)/shard_map/ppermute | solution.py:206
  401.3 34.7 %all-gather.18.cloned.1.call-done = bf16[8192,512]{1,0:T(8,128)(2,1)} async-done(((bf16[2048,512]{1,0:T(8,128)(2,1)}), bf16[8192,512]{1,0:T(8,128)(2,1)}) %all-gather.18.cloned.1.call-update) | async-done | bytes 8388624 | tf_op jit(solution)/shard_map/all_gather | solution.py:948
  435.9 28.7 %dispatch.6.refs_0_ = bf16[8,1,4,256,512]{4,3,2,1,0:T(8,128)(2,1)} custom-call(bf16[4,2,2,4,256,256]{5,4,3,2,1,0:T(8,128)(2,1)} %bitcast.28.refs_0_.refs_1_.refs_3_, s32[4,8,1,2048]{3,2,1,0:T(1,128)} %get-tuple-element.111.refs_1_, bf16[4,2048,512]{2,1,0:T(8,128)(2,1)} %bitcast.118), custom_call_target="tpu_custom_call" | custom-call | tf_op jit(solution)/shard_map/dispatch/pallas_call | solution.py:49
  464.7 29.4 %all-to-all-done.2 = bf16[8,2,4,256,256]{4,3,2,1,0:T(8,128)(2,1)} async-done(((bf16[8,2,4,256,256]{4,3,2,1,0:T(8,128)(2,1)}), bf16[8,2,4,256,256]{4,3,2,1,0:T(8,128)(2,1)}, u32[]{:S(2)}, u32[]{:S(2)}) %all-to-all-start.2) | async-done | bytes 8388640 | tf_op jit(solution)/shard_map/all_to_all | solution.py:821
  499.1 28.8 %dispatch.7.refs_0_ = bf16[8,1,4,256,512]{4,3,2,1,0:T(8,128)(2,1)} custom-call(bf16[4,2,2,4,256,256]{5,4,3,2,1,0:T(8,128)(2,1)} %bitcast.28.refs_0_.refs_1_.refs_3_, s32[4,8,1,2048]{3,2,1,0:T(1,128)} %get-tuple-element.112.refs_1_, bf16[4,2048,512]{2,1,0:T(8,128)(2,1)} %bitcast.119), custom_call_target="tpu_custom_call" | custom-call | tf_op jit(solution)/shard_map/dispatch/pallas_call | solution.py:49
  527.8 65.3 %all-to-all-done.3 = bf16[8,1,4,256,512]{4,3,2,1,0:T(8,128)(2,1)} async-done(((bf16[8,1,4,256,512]{4,3,2,1,0:T(8,128)(2,1)}), bf16[8,1,4,256,512]{4,3,2,1,0:T(8,128)(2,1)}, u32[]{:S(2)}, u32[]{:S(2)}) %all-to-all-start.3) | async-done | bytes 8388640 | tf_op jit(solution)/shard_map/all_to_all | solution.py:821
  621.0 37.2 %expert.2 = (bf16[2048,1024]{1,0:T(8,128)(2,1)}, bf16[2048,1024]{1,0:T(8,128)(2,1)}, bf16[2048,1024]{1,0:T(8,128)(2,1)}) custom-call(bf16[4,2,1,4,256,512]{5,4,3,2,1,0:T(8,128)(2,1)} %bitcast.31.refs_0_.refs_2_.refs_1_, bf16[4,2,2,4,256,256]{5,4,3,2,1,0:T(8,128)(2,1)} %bitcast.28.refs_0_.refs_1_.refs_3_, ...), custom_call_target="tpu_custom_call" | custom-call | tf_op jit(solution)/shard_map/expert/pallas_call | solution.py:49
  673.7 18.6 %all-to-all-done.4 = bf16[8,1,4,256,512]{4,3,2,1,0:T(8,128)(2,1)} async-done(((bf16[8,1,4,256,512]{4,3,2,1,0:T(8,128)(2,1)}), bf16[8,1,4,256,512]{4,3,2,1,0:T(8,128)(2,1)}, u32[]{:S(2)}, u32[]{:S(2)}) %all-to-all-start.4) | async-done | bytes 8388640 | tf_op jit(solution)/shard_map/all_to_all | solution.py:821
  692.3 37.0 %expert.3 = (bf16[2048,1024]{1,0:T(8,128)(2,1)}, bf16[2048,1024]{1,0:T(8,128)(2,1)}, bf16[2048,1024]{1,0:T(8,128)(2,1)}) custom-call(bf16[4,2,1,4,256,512]{5,4,3,2,1,0:T(8,128)(2,1)} %bitcast.34.refs_0_.refs_2_, bf16[4,2,2,4,256,256]{5,4,3,2,1,0:T(8,128)(2,1)} %bitcast.28.refs_0_.refs_1_.refs_3_, ...), custom_call_target="tpu_custom_call" | custom-call | tf_op jit(solution)/shard_map/expert/pallas_call | solution.py:49
  768.5 17.7 %produce.2 = (bf16[4,2,2,4,256,256]{5,4,3,2,1,0:T(8,128)(2,1)}, bf16[4,2,2,4,256,256]{5,4,3,2,1,0:T(8,128)(2,1)}, f32[2048,1]{1,0:T(8,128)}) custom-call(bf16[2048,1024]{1,0:T(8,128)(2,1)} %get-tuple-element.40.act_ref.refs_5_, bf16[2,2048,1024]{2,1,0:T(8,128)(2,1)} %w_ref.3, f32[2,2048,1]{2,1,0:T(8,128)} %reshape.281.refs_6_.prob_ref.refs_2_, ...), custom_call_target="tpu_custom_call" | custom-call | flops 8589934592 | bytes 37748736 | tf_op jit(solution)/shard_map/produce/pallas_call | solution.py:670
  819.4 24.5 %all-to-all-done.5.refs_1_.refs_2_ = bf16[8,2,4,256,256]{4,3,2,1,0:T(8,128)(2,1)} async-done(((bf16[8,2,4,256,256]{4,3,2,1,0:T(8,128)(2,1)}), bf16[8,2,4,256,256]{4,3,2,1,0:T(8,128)(2,1)}, u32[]{:S(2)}, u32[]{:S(2)}) %all-to-all-start.5) | async-done | bytes 8388640 | tf_op jit(solution)/shard_map/all_to_all | solution.py:821
  843.9 30.9 %combine.4.refs_0_ = bf16[4,2048,256]{2,1,0:T(8,128)(2,1)} custom-call(bf16[4,2,2,4,256,256]{5,4,3,2,1,0:T(8,128)(2,1)} %after.27.refs_0_, s32[4,2048,16]{2,1,0:T(8,128)} %bitcast.128, bf16[8,2,4,256,256]{4,3,2,1,0:T(8,128)(2,1)} %all-to-all-done.5.refs_1_.refs_2_), custom_call_target="tpu_custom_call" | custom-call | flops 17179869184 | tf_op jit(solution)/shard_map/combine/pallas_call | solution.py:49
  880.1 46.0 %gate_grad.1 = (f32[2,2048,1024]{2,1,0:T(8,128)}, f32[2,2048,1024]{2,1,0:T(8,128)}) custom-call(bf16[4,2048,256]{2,1,0:T(8,128)(2,1)} %combine.4.refs_0_, bf16[4,2,1,4,256,512]{5,4,3,2,1,0:T(8,128)(2,1)} %bitcast.31.refs_0_.refs_2_.refs_1_, bf16[4,2,1,4,256,512]{5,4,3,2,1,0:T(8,128)(2,1)} %bitcast.34.refs_0_.refs_2_, ...), custom_call_target="tpu_custom_call" | custom-call | tf_op jit(solution)/shard_map/gate_grad/pallas_call | solution.py:49
  926.1 48.0 %all-to-all-done.6.refs_2_.refs_3_.refs_1_ = bf16[8,2,4,256,256]{4,3,2,1,0:T(8,128)(2,1)} async-done(((bf16[8,2,4,256,256]{4,3,2,1,0:T(8,128)(2,1)}), bf16[8,2,4,256,256]{4,3,2,1,0:T(8,128)(2,1)}, u32[]{:S(2)}, u32[]{:S(2)}) %all-to-all-start.6) | async-done | bytes 8388640 | tf_op jit(solution)/shard_map/all_to_all | solution.py:821
  974.1 30.9 %combine.5.refs_0_ = bf16[4,2048,256]{2,1,0:T(8,128)(2,1)} custom-call(f32[2,2048,1024]{2,1,0:T(8,128)} %get-tuple-element.35.refs_0_, bf16[2048,256]{1,0:T(8,128)(2,1)} %bitcast.135, s32[4,2048,16]{2,1,0:T(8,128)} %bitcast.129, bf16[8,2,4,256,256]{4,3,2,1,0:T(8,128)(2,1)} %all-to-all-done.6.refs_2_.refs_3_.refs_1_), custom_call_target="tpu_custom_call" | custom-call | flops 17179869184 | tf_op jit(solution)/shard_map/combine/pallas_call | solution.py:49
  1032.2 19.9 %select_reduce_fusion = f32[64,2048]{1,0:T(8,128)S(1)} fusion(f32[64,256]{1,0:T(8,128)S(1)} %copy-done.53, f32[64,2048]{1,0:T(8,128)S(1)} %copy-done.47, f32[256]{0:T(256)S(1)} %copy-done.73), kind=kLoop, calls=%fused_computation.4 | loop fusion | flops 100532224 | bytes 1115136 | tf_op jit(solution)/shard_map/reduce_sum | solution.py:1005
  1056.1 30.5 %down_grad.1.refs_1_ = f32[2,2048,1024]{2,1,0:T(8,128)} custom-call(bf16[4,2048,256]{2,1,0:T(8,128)(2,1)} %combine.5.refs_0_, f32[64,256]{1,0:T(8,128)} %bitcast_select_fusion.refs_1_.refs_2_, f32[2,2048,1]{2,1,0:T(8,128)} %reshape.281.refs_6_.prob_ref.refs_2_, bf16[4,2,2,4,256,256]{5,4,3,2,1,0:T(8,128)(2,1)} %bitcast.28.refs_0_.refs_1_.refs_3_, ...), custom_call_target="tpu_custom_call" | custom-call | flops 17179869184 | tf_op jit(solution)/shard_map/down_grad/pallas_call | solution.py:49
  1093.0 35.7 %psum.36 = f32[2048]{0:T(1024)S(1)} all-reduce(f32[2048]{0:T(1024)S(1)} %get-tuple-element.62), channel_id=1, replica_groups=mesh['row'=4,'z'=4,'core'=2] {'row'}, use_global_device_ids=true, to_apply=%region_12.14 | all-reduce | flops 2048 | bytes 16384 | tf_op jit(solution)/shard_map/psum | solution.py:1033
  1138.2 30.9 %combine.6.refs_1_ = bf16[4,2048,256]{2,1,0:T(8,128)(2,1)} custom-call(bf16[2048,512]{1,0:T(8,128)(2,1)} %get-tuple-element.71.refs_0_, s32[4,2048,16]{2,1,0:T(8,128)} %bitcast.130, bf16[8,2,4,256,256]{4,3,2,1,0:T(8,128)(2,1)} %all-to-all-done.8.refs_2_.refs_1_), custom_call_target="tpu_custom_call" | custom-call | flops 17179869184 | tf_op jit(solution)/shard_map/combine/pallas_call | solution.py:49
  1176.5 21.3 %collective-permute-done.20.refs_4_.refs_5_.refs_3_ = bf16[2048,256]{1,0:T(8,128)(2,1)} collective-permute-done((bf16[2048,256]{1,0:T(8,128)(2,1)S(1)}, bf16[2048,256]{1,0:T(8,128)(2,1)}, u32[]{:S(2)}, u32[]{:S(2)}) %collective-permute-start.20) | collective-permute-done | bytes 1048608 | tf_op jit(solution)/shard_map/ppermute | solution.py:206
  1201.1 19.1 %collective-permute-done.21.refs_5_.refs_6_.refs_4_ = bf16[2048,256]{1,0:T(8,128)(2,1)} collective-permute-done((bf16[2048,256]{1,0:T(8,128)(2,1)S(1)}, bf16[2048,256]{1,0:T(8,128)(2,1)}, u32[]{:S(2)}, u32[]{:S(2)}) %collective-permute-start.21) | collective-permute-done | bytes 1048608 | tf_op jit(solution)/shard_map/ppermute | solution.py:206
  1222.1 19.6 %collective-permute-done.24.refs_8_.refs_9_.refs_7_ = bf16[2048,256]{1,0:T(8,128)(2,1)} collective-permute-done((bf16[2048,256]{1,0:T(8,128)(2,1)}, bf16[2048,256]{1,0:T(8,128)(2,1)}, u32[]{:S(2)}, u32[]{:S(2)}) %collective-permute-start.24) | collective-permute-done | bytes 1048608 | tf_op jit(solution)/shard_map/ppermute | solution.py:206
  1277.8 63.6 %attend_back.1 = (bf16[2048,1536]{1,0:T(8,128)(2,1)}, f32[2,128]{1,0:T(2,128)}, f32[2048,1]{1,0:T(8,128)}) custom-call(s32[8]{0:T(128)} %get-tuple-element.67.refs_0_, s32[8]{0:T(128)} %get-tuple-element.66.refs_1_, bf16[1024,512]{1,0:T(8,128)(2,1)} %bitcast.124, bf16[2048,1536]{1,0:T(8,128)(2,1)} %get-tuple-element.38.refs_2_.refs_3_.refs_4_.refs_5_, ...), custom_call_target="tpu_custom_call" | custom-call | tf_op jit(solution)/shard_map/attend_back/pallas_call | solution.py:49
  1341.5 30.9 %combine.7.refs_1_ = bf16[4,2048,256]{2,1,0:T(8,128)(2,1)} custom-call(bf16[2048,1536]{1,0:T(8,128)(2,1)} %get-tuple-element.54.refs_0_, s32[4,2048,16]{2,1,0:T(8,128)} %bitcast.131, bf16[8,2,4,256,256]{4,3,2,1,0:T(8,128)(2,1)} %all-to-all-done.10.refs_2_), custom_call_target="tpu_custom_call" | custom-call | flops 17179869184 | tf_op jit(solution)/shard_map/combine/pallas_call | solution.py:49
  1390.5 35.4 %collective-permute-done.29.refs_2_ = bf16[2048,512]{1,0:T(8,128)(2,1)S(1)} collective-permute-done((bf16[2048,512]{1,0:T(8,128)(2,1)}, bf16[2048,512]{1,0:T(8,128)(2,1)S(1)}, u32[]{:S(2)}, u32[]{:S(2)}) %collective-permute-start.29) | collective-permute-done | bytes 2097184 | tf_op jit(solution)/shard_map/ppermute | solution.py:206
  (424 shorter events, 502.8 us)
Async XLA Ops:
  7.2 83.5 %all-gather.10.cloned.1.call-start = ((), (), s32[]{:S(2)}) async-start(), calls=%async_computation.18 | async-start | bytes 2949120 | tf_op jit(solution)/shard_map/all_gather | solution.py:878
  9.9 107.8 %all-gather.12.cloned.1.call-start = ((), (), s32[]{:S(2)}) async-start(), calls=%async_computation.19 | async-start | bytes 7077888 | tf_op jit(solution)/shard_map/all_gather | solution.py:872
  12.1 186.6 %all-gather.14.cloned.1.call-start = ((), (), s32[]{:S(2)}) async-start(), calls=%async_computation.27 | async-start | bytes 5242880 | tf_op jit(solution)/shard_map/all_gather | solution.py:906
  17.7 44.6 %collective-permute-start.4 = (bf16[2064,256]{1,0:T(8,128)(2,1)S(1)}, bf16[2064,256]{1,0:T(8,128)(2,1)}, u32[]{:S(2)}, u32[]{:S(2)}) collective-permute-start(bf16[2064,256]{1,0:T(8,128)(2,1)S(1)} %get-tuple-element.94.refs_4_.refs_12_), channel_id=1, source_target_pairs={{0,8},{8,0},{16,24},{24,16},{1,9},{9,1},{17,25},{25,17},{2,10},{10... | collective-permute-start | bytes 3170312 | tf_op jit(solution)/shard_map/ppermute | solution.py:206
  18.2 45.5 %collective-permute-start.5 = (bf16[2064,256]{1,0:T(8,128)(2,1)S(1)}, bf16[2064,256]{1,0:T(8,128)(2,1)}, u32[]{:S(2)}, u32[]{:S(2)}) collective-permute-start(bf16[2064,256]{1,0:T(8,128)(2,1)S(1)} %get-tuple-element.95.refs_3_.refs_11_), channel_id=1, source_target_pairs={{0,16},{8,24},{16,0},{24,8},{1,17},{9,25},{17,1},{25,9},{2,18},{10... | collective-permute-start | bytes 3170312 | tf_op jit(solution)/shard_map/ppermute | solution.py:206
  74.1 211.7 %all-gather.16.cloned.1.call-start = ((), (), s32[]{:S(2)}) async-start(), calls=%async_computation.28 | async-start | bytes 5242880 | tf_op jit(solution)/shard_map/all_gather | solution.py:906
  181.8 46.0 %collective-permute-start.11 = (bf16[2048,512]{1,0:T(8,128)(2,1)}, bf16[2048,512]{1,0:T(8,128)(2,1)}, u32[]{:S(2)}, u32[]{:S(2)}) collective-permute-start(bf16[2048,512]{1,0:T(8,128)(2,1)} %convolution_convert_fusion.3), channel_id=1, source_target_pairs={{0,16},{8,24},{16,0},{24,8},{1,17},{9,25},{17,1},{25,9},{2,18},{10... | collective-permute-start | bytes 6291464 | tf_op jit(solution)/shard_map/ppermute | solution.py:206
  185.8 44.2 %collective-permute-start.9 = (bf16[2048,512]{1,0:T(8,128)(2,1)}, bf16[2048,512]{1,0:T(8,128)(2,1)}, u32[]{:S(2)}, u32[]{:S(2)}) collective-permute-start(bf16[2048,512]{1,0:T(8,128)(2,1)} %convolution_convert_fusion.4), channel_id=1, source_target_pairs={{0,8},{8,0},{16,24},{24,16},{1,9},{9,1},{17,25},{25,17},{2,10},{10... | collective-permute-start | bytes 6291464 | tf_op jit(solution)/shard_map/ppermute | solution.py:206
  280.2 114.8 %all-to-all-start.1 = ((bf16[8,2,4,256,256]{4,3,2,1,0:T(8,128)(2,1)}), bf16[8,2,4,256,256]{4,3,2,1,0:T(8,128)(2,1)}, u32[]{:S(2)}, u32[]{:S(2)}) async-start(bf16[8,2,4,256,256]{4,3,2,1,0:T(8,128)(2,1)} %after.23), calls=%async_computation.1 | async-start | bytes 16777216 | tf_op jit(solution)/shard_map/all_to_all | solution.py:821
  285.2 150.8 %all-gather.18.cloned.1.call-start = ((), (), s32[]{:S(2)}) async-start(), calls=%async_computation.29 | async-start | bytes 10485760 | tf_op jit(solution)/shard_map/all_gather | solution.py:948
  316.3 67.5 %collective-permute-start.13 = (f32[64,1024]{1,0:T(8,128)S(1)}, f32[64,1024]{1,0:T(8,128)S(1)}, u32[]{:S(2)}, u32[]{:S(2)}) collective-permute-start(f32[64,1024]{1,0:T(8,128)S(1)} %get-tuple-element.117), channel_id=1, source_target_pairs={{0,8},{8,0},{16,24},{24,16},{1,9},{9,1},{17,25},{25,17},{2,10},{10... | collective-permute-start | bytes 786440 | tf_op jit(solution)/shard_map/ppermute | solution.py:206
  318.3 65.6 %collective-permute-start.15 = (f32[64,1024]{1,0:T(8,128)S(1)}, f32[64,1024]{1,0:T(8,128)S(1)}, u32[]{:S(2)}, u32[]{:S(2)}) collective-permute-start(f32[64,1024]{1,0:T(8,128)S(1)} %get-tuple-element.118), channel_id=1, source_target_pairs={{0,16},{8,24},{16,0},{24,8},{1,17},{9,25},{17,1},{25,9},{2,18},{10... | collective-permute-start | bytes 786440 | tf_op jit(solution)/shard_map/ppermute | solution.py:206
  395.0 99.1 %all-to-all-start.2 = ((bf16[8,2,4,256,256]{4,3,2,1,0:T(8,128)(2,1)}), bf16[8,2,4,256,256]{4,3,2,1,0:T(8,128)(2,1)}, u32[]{:S(2)}, u32[]{:S(2)}) async-start(bf16[8,2,4,256,256]{4,3,2,1,0:T(8,128)(2,1)} %after.24), calls=%async_computation.2 | async-start | bytes 16777216 | tf_op jit(solution)/shard_map/all_to_all | solution.py:821
  494.1 99.0 %all-to-all-start.3 = ((bf16[8,1,4,256,512]{4,3,2,1,0:T(8,128)(2,1)}), bf16[8,1,4,256,512]{4,3,2,1,0:T(8,128)(2,1)}, u32[]{:S(2)}, u32[]{:S(2)}) async-start(bf16[8,1,4,256,512]{4,3,2,1,0:T(8,128)(2,1)} %after.25), calls=%async_computation.3 | async-start | bytes 16777216 | tf_op jit(solution)/shard_map/all_to_all | solution.py:821
  593.1 99.2 %all-to-all-start.4 = ((bf16[8,1,4,256,512]{4,3,2,1,0:T(8,128)(2,1)}), bf16[8,1,4,256,512]{4,3,2,1,0:T(8,128)(2,1)}, u32[]{:S(2)}, u32[]{:S(2)}) async-start(bf16[8,1,4,256,512]{4,3,2,1,0:T(8,128)(2,1)} %after.26), calls=%async_computation.4 | async-start | bytes 16777216 | tf_op jit(solution)/shard_map/all_to_all | solution.py:821
  744.8 99.1 %all-to-all-start.5 = ((bf16[8,2,4,256,256]{4,3,2,1,0:T(8,128)(2,1)}), bf16[8,2,4,256,256]{4,3,2,1,0:T(8,128)(2,1)}, u32[]{:S(2)}, u32[]{:S(2)}) async-start(bf16[8,2,4,256,256]{4,3,2,1,0:T(8,128)(2,1)} %bitcast.114), calls=%async_computation.5 | async-start | bytes 16777216 | tf_op jit(solution)/shard_map/all_to_all | solution.py:821
  749.9 224.2 %reduce-scatter.8.cloned.1.call-start = ((), (), s32[]{:S(2)}) async-start(), calls=%async_computation.20 | async-start | bytes 5242880 | tf_op jit(solution)/shard_map/reduce_scatter | solution.py:901
  874.8 99.3 %all-to-all-start.6 = ((bf16[8,2,4,256,256]{4,3,2,1,0:T(8,128)(2,1)}), bf16[8,2,4,256,256]{4,3,2,1,0:T(8,128)(2,1)}, u32[]{:S(2)}, u32[]{:S(2)}) async-start(bf16[8,2,4,256,256]{4,3,2,1,0:T(8,128)(2,1)} %bitcast.115), calls=%async_computation.6 | async-start | bytes 16777216 | tf_op jit(solution)/shard_map/all_to_all | solution.py:821
  880.1 206.6 %reduce-scatter.10.cloned.1.call-start = ((), (), s32[]{:S(2)}) async-start(), calls=%async_computation.21 | async-start | bytes 5242880 | tf_op jit(solution)/shard_map/reduce_scatter | solution.py:901
  1026.5 108.3 %all-to-all-start.8 = ((bf16[8,2,4,256,256]{4,3,2,1,0:T(8,128)(2,1)}), bf16[8,2,4,256,256]{4,3,2,1,0:T(8,128)(2,1)}, u32[]{:S(2)}, u32[]{:S(2)}) async-start(bf16[8,2,4,256,256]{4,3,2,1,0:T(8,128)(2,1)} %bitcast.116), calls=%async_computation.10 | async-start | bytes 16777216 | tf_op jit(solution)/shard_map/all_to_all | solution.py:821
  1138.2 234.2 %reduce-scatter.14.cloned.1.call-start = ((), (), s32[]{:S(2)}) async-start(), calls=%async_computation.23 | async-start | bytes 147456 | tf_op jit(solution)/shard_map/reduce_scatter | solution.py:1025
  1175.7 196.7 %reduce-scatter.12.cloned.1.call-start = ((), (), s32[]{:S(2)}) async-start(), calls=%async_computation.22 | async-start | bytes 5242880 | tf_op jit(solution)/shard_map/reduce_scatter | solution.py:901
  1175.7 44.5 %collective-permute-start.21 = (bf16[2048,256]{1,0:T(8,128)(2,1)S(1)}, bf16[2048,256]{1,0:T(8,128)(2,1)}, u32[]{:S(2)}, u32[]{:S(2)}) collective-permute-start(bf16[2048,256]{1,0:T(8,128)(2,1)S(1)} %get-tuple-element.96.refs_3_.refs_4_.refs_2_), channel_id=1, source_target_pairs={{0,8},{8,0},{16,24},{24,16},{1,9},{9,1},{17,25},{25,17},{2,10},{10... | collective-permute-start | bytes 3145736 | tf_op jit(solution)/shard_map/ppermute | solution.py:206
  1176.3 45.8 %collective-permute-start.22 = (bf16[2048,256]{1,0:T(8,128)(2,1)S(1)}, bf16[2048,256]{1,0:T(8,128)(2,1)}, u32[]{:S(2)}, u32[]{:S(2)}) collective-permute-start(bf16[2048,256]{1,0:T(8,128)(2,1)S(1)} %get-tuple-element.97.refs_2_.refs_3_.refs_1_), channel_id=1, source_target_pairs={{0,16},{8,24},{16,0},{24,8},{1,17},{9,25},{17,1},{25,9},{2,18},{10... | collective-permute-start | bytes 3145736 | tf_op jit(solution)/shard_map/ppermute | solution.py:206
  1197.7 44.0 %collective-permute-start.24 = (bf16[2048,256]{1,0:T(8,128)(2,1)}, bf16[2048,256]{1,0:T(8,128)(2,1)}, u32[]{:S(2)}, u32[]{:S(2)}) collective-permute-start(bf16[2048,256]{1,0:T(8,128)(2,1)} %collective-permute-done.20.refs_4_.refs_5_.refs_3_), channel_id=1, source_target_pairs={{0,16},{8,24},{16,0},{24,8},{1,17},{9,25},{17,1},{25,9},{2,18},{10... | collective-permute-start | bytes 3145736 | tf_op jit(solution)/shard_map/ppermute | solution.py:206
  1199.6 42.1 %collective-permute-start.25 = (bf16[2048,256]{1,0:T(8,128)(2,1)}, bf16[2048,256]{1,0:T(8,128)(2,1)}, u32[]{:S(2)}, u32[]{:S(2)}) collective-permute-start(bf16[2048,256]{1,0:T(8,128)(2,1)} %collective-permute-done.23.refs_7_.refs_8_.refs_6_), channel_id=1, source_target_pairs={{0,8},{8,0},{16,24},{24,16},{1,9},{9,1},{17,25},{25,17},{2,10},{10... | collective-permute-start | bytes 3145736 | tf_op jit(solution)/shard_map/ppermute | solution.py:206
  1241.8 99.7 %all-to-all-start.10 = ((bf16[8,2,4,256,256]{4,3,2,1,0:T(8,128)(2,1)}), bf16[8,2,4,256,256]{4,3,2,1,0:T(8,128)(2,1)}, u32[]{:S(2)}, u32[]{:S(2)}) async-start(bf16[8,2,4,256,256]{4,3,2,1,0:T(8,128)(2,1)} %bitcast.117), calls=%async_computation.12 | async-start | bytes 16777216 | tf_op jit(solution)/shard_map/all_to_all | solution.py:821
  1246.8 236.6 %reduce-scatter.20.cloned.1.call-start = ((), (), s32[]{:S(2)}) async-start(), calls=%async_computation.26 | async-start | bytes 1310720 | tf_op jit(solution)/shard_map/reduce_scatter | solution.py:253
  1277.8 250.5 %reduce-scatter.16.cloned.1.call-start = ((), (), s32[]{:S(2)}) async-start(), calls=%async_computation.24 | async-start | bytes 5242880 | tf_op jit(solution)/shard_map/reduce_scatter | solution.py:901
  1382.0 44.0 %collective-permute-start.29 = (bf16[2048,512]{1,0:T(8,128)(2,1)}, bf16[2048,512]{1,0:T(8,128)(2,1)S(1)}, u32[]{:S(2)}, u32[]{:S(2)}) collective-permute-start(bf16[2048,512]{1,0:T(8,128)(2,1)} %convolution_convert_fusion.1), channel_id=1, source_target_pairs={{0,16},{8,24},{16,0},{24,8},{1,17},{9,25},{17,1},{25,9},{2,18},{10... | collective-permute-start | bytes 6291464 | tf_op jit(solution)/shard_map/ppermute | solution.py:206
  1389.0 44.4 %collective-permute-start.27 = (bf16[2048,512]{1,0:T(8,128)(2,1)}, bf16[2048,512]{1,0:T(8,128)(2,1)}, u32[]{:S(2)}, u32[]{:S(2)}) collective-permute-start(bf16[2048,512]{1,0:T(8,128)(2,1)} %convolution_convert_fusion.2), channel_id=1, source_target_pairs={{0,8},{8,0},{16,24},{24,16},{1,9},{9,1},{17,25},{25,17},{2,10},{10... | collective-permute-start | bytes 6291464 | tf_op jit(solution)/shard_map/ppermute | solution.py:206
  1390.5 142.4 %reduce-scatter.18.cloned.1.call-start = ((), (), s32[]{:S(2)}) async-start(), calls=%async_computation.25 | async-start | bytes 3932160 | tf_op jit(solution)/shard_map/reduce_scatter | solution.py:253
  (107 other events, 1649.3 us)
Sparse Core Ops, SparseCore 0:
  10.2 36.4 all-gather.9
  48.3 69.3 all-gather.11
  119.3 79.3 all-gather.13
  200.0 79.2 all-gather.15
  287.2 148.6 all-gather.17
  874.9 73.5 reduce-scatter.7
  1005.2 73.4 reduce-scatter.9
  1175.8 27.1 reduce-scatter.13
  1205.3 74.8 reduce-scatter.11
  1282.3 27.7 reduce-scatter.19
  1390.6 73.0 reduce-scatter.15
  1465.9 61.3 reduce-scatter.17

commit v6 on v5

--- a/solution.py
+++ b/solution.py
@@ -1042,7 +1042,7 @@
     made_rows = [swap(after(made_buffers[0], back_rows[1], slot_grads).reshape(swapped_dims))]
     branch_pieces, branch_starts = row_gather(after(grad_branch, made_rows[0], router_swapped))
     made_rows.append(swap(after(made_buffers[1], *branch_pieces).reshape(swapped_dims)))
-    made_sums = [combine(slots_by_token, [made_rows[0]], 0, width, [grad_branch])]
+    made_sums = [combine(slots_by_token, [made_rows[0]], 0, width, branch_pieces[2:4])]
     grad_projection = projection_grad(branch_starts, branch_pieces, mixed, made_sums)
     grad_mixed = mix_back(
         branch_starts, branch_pieces, projection_full, [grad_projection, router_swapped]

time: 1560 us -> 1620 us (1.038)
  waiting for transfers between devices: 523 us -> 586 us
  blocking collectives: 74.7 us -> 93.1 us
    all_to_all x8, waiting for transfers between devices: 186 us -> 236 us  [swap(): lax.all_to_all(rows, SWAP_AXES, split_axis=0, concat_axis=0, tiled=True)]
    psum x1, blocking collectives: 35.7 us -> 54.2 us  [per_device(): lax.psum(jnp.sum(scaled_two * middle, axis=1), 'row')[:, None]]
  transfers between devices with their start and end apart: 58 -> 58, of which waited for: 36 -> 36; matrix products, arithmetic and copies ran while one was open for 12% -> 12% of each run, Pallas kernels for 33% -> 31%
where the time goes in v6:
time: 1620 us; the launch traced here: 1610 us
  Pallas kernels  619 us (38%)
  waiting for transfers between devices  586 us (36%)
  other arithmetic  94.6 us (6%)
  blocking collectives  93.1 us (6%)
  starting transfers between devices  90.6 us (6%)
  matrix products  62.4 us (4%)
  local copies, waits for them, and re-layouts  47.7 us (3%)
    pallas_call x17, Pallas kernels, call(): return lambda *args: kernel(*args[:prefetch], *deps, *args[prefetch:])  522 us
    ppermute x33, waiting for transfers between devices, permute(): return lax.ppermute(values, 'row', [(i, i ^ mask) for i in range(4)])  275 us
    all_to_all x8, waiting for transfers between devices, swap(): lax.all_to_all(rows, SWAP_AXES, split_axis=0, concat_axis=0, tiled=True)  236 us
    pallas_call x4, Pallas kernels, rows_back(): pl.pallas_call(rows_back_body, out_shape=shape(dims, BF), grid=(cores, ro...  61.7 us
    dot_general x12, matrix products, dot(): lax.dot_general(left, right, (((left_dim,), (right_dim,)), ((), ())), pre...  58.6 us
    psum x1, blocking collectives, per_device(): lax.psum(jnp.sum(scaled_two * middle, axis=1), 'row')[:, None]  54.2 us
    all_to_all x8, starting transfers between devices, swap(): lax.all_to_all(rows, SWAP_AXES, split_axis=0, concat_axis=0, tiled=True)  40.6 us
    ppermute x33, starting transfers between devices, permute(): return lax.ppermute(values, 'row', [(i, i ^ mask) for i in range(4)])  37.4 us
  transfers between devices with their start and end apart: 58, of which 36 were waited for; matrix products, arithmetic and copies ran while one was open for 12% of the time, Pallas kernels for 31%

profile of v6, /device:TPU:0, one launch (start us, length us, event | category | flops | bytes accessed | tf_op | source)
XLA Modules:
  0.0 1609.0 jit_solution(1154416877738709615)
XLA Ops:
  19.7 20.6 %collective-permute-done.3.refs_5_.refs_13_.refs_1_ = bf16[2064,256]{1,0:T(8,128)(2,1)S(1)} collective-permute-done((bf16[2064,256]{1,0:T(8,128)(2,1)S(1)}, bf16[2064,256]{1,0:T(8,128)(2,1)S(1)}, u32[]{:S(2)}, u32[]{:S(2)}) %collective-permute-start.3) | collective-permute-done | bytes 1056800 | tf_op jit(solution)/shard_map/ppermute | solution.py:206
  42.4 19.9 %collective-permute-done.4.refs_6_.refs_14_.refs_2_ = bf16[2064,256]{1,0:T(8,128)(2,1)} collective-permute-done((bf16[2064,256]{1,0:T(8,128)(2,1)S(1)}, bf16[2064,256]{1,0:T(8,128)(2,1)}, u32[]{:S(2)}, u32[]{:S(2)}) %collective-permute-start.4) | collective-permute-done | bytes 1056800 | tf_op jit(solution)/shard_map/ppermute | solution.py:206
  118.3 31.2 %project.1 = (bf16[2048,2048]{1,0:T(8,128)(2,1)}, bf16[2048,1536]{1,0:T(8,128)(2,1)}, f32[2048,1024]{1,0:T(8,128)}, f32[2048,1]{1,0:T(8,128)}) custom-call(s32[8]{0:T(128)} %stack.101.refs_0_, s32[4,4,4,2048]{3,2,1,0:T(4,128)} %convert_element_type.133.refs_1_, bf16[64,512]{1,0:T(8,128)(2,1)} %bitcast.143, bf16[2064,256]{1,0:T(8,128)(2,1)} %copy-done.24, ...), custom_call_target="tpu_custom_call" | custom-call | tf_op jit(solution)/shard_map/project/pallas_call | solution.py:49
  149.5 24.2 %attend.1 = (bf16[2048,512]{1,0:T(8,128)(2,1)}, f32[4,2048,1]{2,1,0:T(8,128)}) custom-call(s32[8]{0:T(128)} %get-tuple-element.67.refs_0_, s32[8]{0:T(128)} %get-tuple-element.66.refs_1_, bf16[2048,1536]{1,0:T(8,128)(2,1)} %get-tuple-element.38.refs_2_.refs_3_.refs_4_.refs_5_, bf16[2048,1536]{1,0:T(8,128)(2,1)} %get-tuple-element.38.refs_2_.refs_3_.refs_4_.refs_5_, ...), custom_call_target="tpu_custom_call" | custom-call | tf_op jit(solution)/shard_map/attend/pallas_call | solution.py:49
  198.6 27.9 %dispatch.4.refs_1_.refs_0_ = bf16[8,2,4,256,256]{4,3,2,1,0:T(8,128)(2,1)} custom-call(s32[4,8,2,2048]{3,2,1,0:T(2,128)} %reshape.211.refs_0_.refs_1_, bf16[4,2048,256]{2,1,0:T(8,128)(2,1)} %bitcast.127), custom_call_target="tpu_custom_call" | custom-call | tf_op jit(solution)/shard_map/dispatch/pallas_call | solution.py:49
  241.7 19.6 %collective-permute-done.12 = bf16[2048,256]{1,0:T(8,128)(2,1)S(1)} collective-permute-done((bf16[2048,256]{1,0:T(8,128)(2,1)}, bf16[2048,256]{1,0:T(8,128)(2,1)S(1)}, u32[]{:S(2)}, u32[]{:S(2)}) %collective-permute-start.12) | collective-permute-done | bytes 1048608 | tf_op jit(solution)/shard_map/ppermute | solution.py:206
  285.8 27.9 %dispatch.5.refs_1_.refs_0_ = bf16[8,2,4,256,256]{4,3,2,1,0:T(8,128)(2,1)} custom-call(bf16[2048,512]{1,0:T(8,128)(2,1)} %multiply_convert_fusion.refs_0_.refs_1_, s32[4,8,2,2048]{3,2,1,0:T(2,128)} %reshape.211.refs_0_.refs_1_, bf16[4,2048,256]{2,1,0:T(8,128)(2,1)} %bitcast.132), custom_call_target="tpu_custom_call" | custom-call | tf_op jit(solution)/shard_map/dispatch/pallas_call | solution.py:49
  319.8 64.1 %collective-permute-done.13 = f32[64,1024]{1,0:T(8,128)S(1)} collective-permute-done((f32[64,1024]{1,0:T(8,128)S(1)}, f32[64,1024]{1,0:T(8,128)S(1)}, u32[]{:S(2)}, u32[]{:S(2)}) %collective-permute-start.13) | collective-permute-done | bytes 262176 | tf_op jit(solution)/shard_map/ppermute | solution.py:206
  401.3 34.7 %all-gather.18.cloned.1.call-done = bf16[8192,512]{1,0:T(8,128)(2,1)} async-done(((bf16[2048,512]{1,0:T(8,128)(2,1)}), bf16[8192,512]{1,0:T(8,128)(2,1)}) %all-gather.18.cloned.1.call-update) | async-done | bytes 8388624 | tf_op jit(solution)/shard_map/all_gather | solution.py:948
  435.9 28.7 %dispatch.6.refs_0_ = bf16[8,1,4,256,512]{4,3,2,1,0:T(8,128)(2,1)} custom-call(bf16[4,2,2,4,256,256]{5,4,3,2,1,0:T(8,128)(2,1)} %bitcast.28.refs_0_.refs_1_.refs_3_, s32[4,8,1,2048]{3,2,1,0:T(1,128)} %get-tuple-element.111.refs_1_, bf16[4,2048,512]{2,1,0:T(8,128)(2,1)} %bitcast.118), custom_call_target="tpu_custom_call" | custom-call | tf_op jit(solution)/shard_map/dispatch/pallas_call | solution.py:49
  464.7 29.5 %all-to-all-done.2 = bf16[8,2,4,256,256]{4,3,2,1,0:T(8,128)(2,1)} async-done(((bf16[8,2,4,256,256]{4,3,2,1,0:T(8,128)(2,1)}), bf16[8,2,4,256,256]{4,3,2,1,0:T(8,128)(2,1)}, u32[]{:S(2)}, u32[]{:S(2)}) %all-to-all-start.2) | async-done | bytes 8388640 | tf_op jit(solution)/shard_map/all_to_all | solution.py:821
  499.1 28.7 %dispatch.7.refs_0_ = bf16[8,1,4,256,512]{4,3,2,1,0:T(8,128)(2,1)} custom-call(bf16[4,2,2,4,256,256]{5,4,3,2,1,0:T(8,128)(2,1)} %bitcast.28.refs_0_.refs_1_.refs_3_, s32[4,8,1,2048]{3,2,1,0:T(1,128)} %get-tuple-element.112.refs_1_, bf16[4,2048,512]{2,1,0:T(8,128)(2,1)} %bitcast.119), custom_call_target="tpu_custom_call" | custom-call | tf_op jit(solution)/shard_map/dispatch/pallas_call | solution.py:49
  527.8 65.3 %all-to-all-done.3 = bf16[8,1,4,256,512]{4,3,2,1,0:T(8,128)(2,1)} async-done(((bf16[8,1,4,256,512]{4,3,2,1,0:T(8,128)(2,1)}), bf16[8,1,4,256,512]{4,3,2,1,0:T(8,128)(2,1)}, u32[]{:S(2)}, u32[]{:S(2)}) %all-to-all-start.3) | async-done | bytes 8388640 | tf_op jit(solution)/shard_map/all_to_all | solution.py:821
  621.1 37.2 %expert.2 = (bf16[2048,1024]{1,0:T(8,128)(2,1)}, bf16[2048,1024]{1,0:T(8,128)(2,1)}, bf16[2048,1024]{1,0:T(8,128)(2,1)}) custom-call(bf16[4,2,1,4,256,512]{5,4,3,2,1,0:T(8,128)(2,1)} %bitcast.31.refs_0_.refs_2_.refs_1_, bf16[4,2,2,4,256,256]{5,4,3,2,1,0:T(8,128)(2,1)} %bitcast.28.refs_0_.refs_1_.refs_3_, ...), custom_call_target="tpu_custom_call" | custom-call | tf_op jit(solution)/shard_map/expert/pallas_call | solution.py:49
  673.7 18.6 %all-to-all-done.4 = bf16[8,1,4,256,512]{4,3,2,1,0:T(8,128)(2,1)} async-done(((bf16[8,1,4,256,512]{4,3,2,1,0:T(8,128)(2,1)}), bf16[8,1,4,256,512]{4,3,2,1,0:T(8,128)(2,1)}, u32[]{:S(2)}, u32[]{:S(2)}) %all-to-all-start.4) | async-done | bytes 8388640 | tf_op jit(solution)/shard_map/all_to_all | solution.py:821
  692.4 37.1 %expert.3 = (bf16[2048,1024]{1,0:T(8,128)(2,1)}, bf16[2048,1024]{1,0:T(8,128)(2,1)}, bf16[2048,1024]{1,0:T(8,128)(2,1)}) custom-call(bf16[4,2,1,4,256,512]{5,4,3,2,1,0:T(8,128)(2,1)} %bitcast.34.refs_0_.refs_2_, bf16[4,2,2,4,256,256]{5,4,3,2,1,0:T(8,128)(2,1)} %bitcast.28.refs_0_.refs_1_.refs_3_, ...), custom_call_target="tpu_custom_call" | custom-call | tf_op jit(solution)/shard_map/expert/pallas_call | solution.py:49
  801.7 17.7 %produce.3 = (bf16[4,2,2,4,256,256]{5,4,3,2,1,0:T(8,128)(2,1)}, bf16[4,2,2,4,256,256]{5,4,3,2,1,0:T(8,128)(2,1)}, f32[2048,1]{1,0:T(8,128)}) custom-call(bf16[2048,1024]{1,0:T(8,128)(2,1)} %get-tuple-element.42.act_ref.refs_6_, bf16[2,2048,1024]{2,1,0:T(8,128)(2,1)} %w_ref.3, ...), custom_call_target="tpu_custom_call", output_to_operand_aliasing={{0}: (5, {}), {1}: (6, {})} | custom-call | flops 8589934592 | bytes 37748736 | tf_op jit(solution)/shard_map/produce/pallas_call | solution.py:670
  819.5 24.5 %all-to-all-done.5.refs_1_.refs_2_ = bf16[8,2,4,256,256]{4,3,2,1,0:T(8,128)(2,1)} async-done(((bf16[8,2,4,256,256]{4,3,2,1,0:T(8,128)(2,1)}), bf16[8,2,4,256,256]{4,3,2,1,0:T(8,128)(2,1)}, u32[]{:S(2)}, u32[]{:S(2)}) %all-to-all-start.5) | async-done | bytes 8388640 | tf_op jit(solution)/shard_map/all_to_all | solution.py:821
  844.0 30.9 %combine.4.refs_0_ = bf16[4,2048,256]{2,1,0:T(8,128)(2,1)} custom-call(bf16[4,2,2,4,256,256]{5,4,3,2,1,0:T(8,128)(2,1)} %after.27.refs_0_, s32[4,2048,16]{2,1,0:T(8,128)} %bitcast.128, bf16[8,2,4,256,256]{4,3,2,1,0:T(8,128)(2,1)} %all-to-all-done.5.refs_1_.refs_2_), custom_call_target="tpu_custom_call" | custom-call | flops 17179869184 | tf_op jit(solution)/shard_map/combine/pallas_call | solution.py:49
  881.7 92.7 %all-to-all-done.6.refs_2_.refs_3_.refs_1_ = bf16[8,2,4,256,256]{4,3,2,1,0:T(8,128)(2,1)} async-done(((bf16[8,2,4,256,256]{4,3,2,1,0:T(8,128)(2,1)}), bf16[8,2,4,256,256]{4,3,2,1,0:T(8,128)(2,1)}, u32[]{:S(2)}, u32[]{:S(2)}) %all-to-all-start.6) | async-done | bytes 8388640 | tf_op jit(solution)/shard_map/all_to_all | solution.py:821
  988.5 46.1 %gate_grad.1 = (f32[2,2048,1024]{2,1,0:T(8,128)}, f32[2,2048,1024]{2,1,0:T(8,128)}) custom-call(bf16[4,2048,256]{2,1,0:T(8,128)(2,1)} %combine.4.refs_0_, bf16[4,2,1,4,256,512]{5,4,3,2,1,0:T(8,128)(2,1)} %bitcast.31.refs_0_.refs_2_.refs_1_, bf16[4,2,1,4,256,512]{5,4,3,2,1,0:T(8,128)(2,1)} %bitcast.34.refs_0_.refs_2_, ...), custom_call_target="tpu_custom_call" | custom-call | tf_op jit(solution)/shard_map/gate_grad/pallas_call | solution.py:49
  1035.3 30.9 %combine.5.refs_0_ = bf16[4,2048,256]{2,1,0:T(8,128)(2,1)} custom-call(f32[2,2048,1024]{2,1,0:T(8,128)} %get-tuple-element.35.refs_0_, bf16[2048,256]{1,0:T(8,128)(2,1)} %bitcast.135, s32[4,2048,16]{2,1,0:T(8,128)} %bitcast.129, bf16[8,2,4,256,256]{4,3,2,1,0:T(8,128)(2,1)} %all-to-all-done.6.refs_2_.refs_3_.refs_1_), custom_call_target="tpu_custom_call" | custom-call | flops 17179869184 | tf_op jit(solution)/shard_map/combine/pallas_call | solution.py:49
  1067.3 19.9 %select_reduce_fusion = f32[64,2048]{1,0:T(8,128)S(1)} fusion(f32[64,256]{1,0:T(8,128)S(1)} %bitcast_select_fusion.refs_1_.refs_2_, f32[64,2048]{1,0:T(8,128)S(1)} %copy-done.48, f32[256]{0:T(256)S(1)} %copy-done.74), kind=kLoop, calls=%fused_computation.4 | loop fusion | flops 100532224 | bytes 1115136 | tf_op jit(solution)/shard_map/reduce_sum | solution.py:1005
  1105.1 30.8 %down_grad.1.refs_1_ = f32[2,2048,1024]{2,1,0:T(8,128)} custom-call(bf16[4,2048,256]{2,1,0:T(8,128)(2,1)} %combine.5.refs_0_, f32[64,256]{1,0:T(8,128)} %copy-done.54, f32[2,2048,1]{2,1,0:T(8,128)} %reshape.281.refs_6_.prob_ref.refs_2_, bf16[4,2,2,4,256,256]{5,4,3,2,1,0:T(8,128)(2,1)} %bitcast.28.refs_0_.refs_1_.refs_3_, ...), custom_call_target="tpu_custom_call" | custom-call | flops 17179869184 | tf_op jit(solution)/shard_map/down_grad/pallas_call | solution.py:49
  1144.7 54.2 %psum.36 = f32[2048]{0:T(1024)S(1)} all-reduce(f32[2048]{0:T(1024)S(1)} %get-tuple-element.62), channel_id=1, replica_groups=mesh['row'=4,'z'=4,'core'=2] {'row'}, use_global_device_ids=true, to_apply=%region_12.14 | all-reduce | flops 2048 | bytes 16384 | tf_op jit(solution)/shard_map/psum | solution.py:1033
  1211.6 21.3 %collective-permute-done.20.refs_0_.refs_4_.refs_5_.refs_3_ = bf16[2048,256]{1,0:T(8,128)(2,1)} collective-permute-done((bf16[2048,256]{1,0:T(8,128)(2,1)S(1)}, bf16[2048,256]{1,0:T(8,128)(2,1)}, u32[]{:S(2)}, u32[]{:S(2)}) %collective-permute-start.20) | collective-permute-done | bytes 1048608 | tf_op jit(solution)/shard_map/ppermute | solution.py:206
  1232.9 20.2 %collective-permute-done.21.refs_1_.refs_5_.refs_6_.refs_4_ = bf16[2048,256]{1,0:T(8,128)(2,1)} collective-permute-done((bf16[2048,256]{1,0:T(8,128)(2,1)S(1)}, bf16[2048,256]{1,0:T(8,128)(2,1)}, u32[]{:S(2)}, u32[]{:S(2)}) %collective-permute-start.21) | collective-permute-done | bytes 1048608 | tf_op jit(solution)/shard_map/ppermute | solution.py:206
  1253.1 30.9 %combine.6.refs_1_ = bf16[4,2048,256]{2,1,0:T(8,128)(2,1)} custom-call(bf16[2048,256]{1,0:T(8,128)(2,1)} %collective-permute-done.20.refs_0_.refs_4_.refs_5_.refs_3_, bf16[2048,256]{1,0:T(8,128)(2,1)} %collective-permute-done.21.refs_1_.refs_5_.refs_6_.refs_4_, s32[4,2048,16]{2,1,0:T(8,128)} %bitcast.130, ...), custom_call_target="tpu_custom_call" | custom-call | flops 17179869184 | tf_op jit(solution)/shard_map/combine/pallas_call | solution.py:49
  1286.3 21.0 %collective-permute-done.24.refs_8_.refs_9_.refs_7_ = bf16[2048,256]{1,0:T(8,128)(2,1)} collective-permute-done((bf16[2048,256]{1,0:T(8,128)(2,1)}, bf16[2048,256]{1,0:T(8,128)(2,1)}, u32[]{:S(2)}, u32[]{:S(2)}) %collective-permute-start.24) | collective-permute-done | bytes 1048608 | tf_op jit(solution)/shard_map/ppermute | solution.py:206
  1344.6 57.4 %attend_back.1 = (bf16[2048,1536]{1,0:T(8,128)(2,1)}, f32[2,128]{1,0:T(2,128)}, f32[2048,1]{1,0:T(8,128)}) custom-call(s32[8]{0:T(128)} %get-tuple-element.67.refs_0_, s32[8]{0:T(128)} %get-tuple-element.66.refs_1_, bf16[1024,512]{1,0:T(8,128)(2,1)} %bitcast.124, bf16[2048,1536]{1,0:T(8,128)(2,1)} %get-tuple-element.38.refs_2_.refs_3_.refs_4_.refs_5_, ...), custom_call_target="tpu_custom_call" | custom-call | tf_op jit(solution)/shard_map/attend_back/pallas_call | solution.py:49
  1407.8 30.9 %combine.7.refs_1_ = bf16[4,2048,256]{2,1,0:T(8,128)(2,1)} custom-call(bf16[2048,1536]{1,0:T(8,128)(2,1)} %get-tuple-element.54.refs_0_, s32[4,2048,16]{2,1,0:T(8,128)} %bitcast.131, bf16[8,2,4,256,256]{4,3,2,1,0:T(8,128)(2,1)} %all-to-all-done.10.refs_2_), custom_call_target="tpu_custom_call" | custom-call | flops 17179869184 | tf_op jit(solution)/shard_map/combine/pallas_call | solution.py:49
  1454.8 38.1 %collective-permute-done.29.refs_2_ = bf16[2048,512]{1,0:T(8,128)(2,1)S(1)} collective-permute-done((bf16[2048,512]{1,0:T(8,128)(2,1)}, bf16[2048,512]{1,0:T(8,128)(2,1)S(1)}, u32[]{:S(2)}, u32[]{:S(2)}) %collective-permute-start.29) | collective-permute-done | bytes 2097184 | tf_op jit(solution)/shard_map/ppermute | solution.py:206
  (426 shorter events, 510.8 us)
Async XLA Ops:
  7.2 83.5 %all-gather.10.cloned.1.call-start = ((), (), s32[]{:S(2)}) async-start(), calls=%async_computation.18 | async-start | bytes 2949120 | tf_op jit(solution)/shard_map/all_gather | solution.py:878
  9.9 107.8 %all-gather.12.cloned.1.call-start = ((), (), s32[]{:S(2)}) async-start(), calls=%async_computation.19 | async-start | bytes 7077888 | tf_op jit(solution)/shard_map/all_gather | solution.py:872
  12.1 186.6 %all-gather.14.cloned.1.call-start = ((), (), s32[]{:S(2)}) async-start(), calls=%async_computation.27 | async-start | bytes 5242880 | tf_op jit(solution)/shard_map/all_gather | solution.py:906
  18.2 45.5 %collective-permute-start.5 = (bf16[2064,256]{1,0:T(8,128)(2,1)S(1)}, bf16[2064,256]{1,0:T(8,128)(2,1)}, u32[]{:S(2)}, u32[]{:S(2)}) collective-permute-start(bf16[2064,256]{1,0:T(8,128)(2,1)S(1)} %get-tuple-element.95.refs_3_.refs_11_), channel_id=1, source_target_pairs={{0,16},{8,24},{16,0},{24,8},{1,17},{9,25},{17,1},{25,9},{2,18},{10... | collective-permute-start | bytes 3170312 | tf_op jit(solution)/shard_map/ppermute | solution.py:206
  74.1 211.7 %all-gather.16.cloned.1.call-start = ((), (), s32[]{:S(2)}) async-start(), calls=%async_computation.28 | async-start | bytes 5242880 | tf_op jit(solution)/shard_map/all_gather | solution.py:906
  178.1 49.7 %collective-permute-start.11 = (bf16[2048,512]{1,0:T(8,128)(2,1)}, bf16[2048,512]{1,0:T(8,128)(2,1)}, u32[]{:S(2)}, u32[]{:S(2)}) collective-permute-start(bf16[2048,512]{1,0:T(8,128)(2,1)} %convolution_convert_fusion.3), channel_id=1, source_target_pairs={{0,16},{8,24},{16,0},{24,8},{1,17},{9,25},{17,1},{25,9},{2,18},{10... | collective-permute-start | bytes 6291464 | tf_op jit(solution)/shard_map/ppermute | solution.py:206
  182.1 47.9 %collective-permute-start.9 = (bf16[2048,512]{1,0:T(8,128)(2,1)}, bf16[2048,512]{1,0:T(8,128)(2,1)}, u32[]{:S(2)}, u32[]{:S(2)}) collective-permute-start(bf16[2048,512]{1,0:T(8,128)(2,1)} %convolution_convert_fusion.4), channel_id=1, source_target_pairs={{0,8},{8,0},{16,24},{24,16},{1,9},{9,1},{17,25},{25,17},{2,10},{10... | collective-permute-start | bytes 6291464 | tf_op jit(solution)/shard_map/ppermute | solution.py:206
  280.2 114.8 %all-to-all-start.1 = ((bf16[8,2,4,256,256]{4,3,2,1,0:T(8,128)(2,1)}), bf16[8,2,4,256,256]{4,3,2,1,0:T(8,128)(2,1)}, u32[]{:S(2)}, u32[]{:S(2)}) async-start(bf16[8,2,4,256,256]{4,3,2,1,0:T(8,128)(2,1)} %after.23), calls=%async_computation.1 | async-start | bytes 16777216 | tf_op jit(solution)/shard_map/all_to_all | solution.py:821
  285.2 150.8 %all-gather.18.cloned.1.call-start = ((), (), s32[]{:S(2)}) async-start(), calls=%async_computation.29 | async-start | bytes 10485760 | tf_op jit(solution)/shard_map/all_gather | solution.py:948
  316.4 67.5 %collective-permute-start.13 = (f32[64,1024]{1,0:T(8,128)S(1)}, f32[64,1024]{1,0:T(8,128)S(1)}, u32[]{:S(2)}, u32[]{:S(2)}) collective-permute-start(f32[64,1024]{1,0:T(8,128)S(1)} %get-tuple-element.117), channel_id=1, source_target_pairs={{0,8},{8,0},{16,24},{24,16},{1,9},{9,1},{17,25},{25,17},{2,10},{10... | collective-permute-start | bytes 786440 | tf_op jit(solution)/shard_map/ppermute | solution.py:206
  318.3 65.6 %collective-permute-start.15 = (f32[64,1024]{1,0:T(8,128)S(1)}, f32[64,1024]{1,0:T(8,128)S(1)}, u32[]{:S(2)}, u32[]{:S(2)}) collective-permute-start(f32[64,1024]{1,0:T(8,128)S(1)} %get-tuple-element.118), channel_id=1, source_target_pairs={{0,16},{8,24},{16,0},{24,8},{1,17},{9,25},{17,1},{25,9},{2,18},{10... | collective-permute-start | bytes 786440 | tf_op jit(solution)/shard_map/ppermute | solution.py:206
  395.0 99.1 %all-to-all-start.2 = ((bf16[8,2,4,256,256]{4,3,2,1,0:T(8,128)(2,1)}), bf16[8,2,4,256,256]{4,3,2,1,0:T(8,128)(2,1)}, u32[]{:S(2)}, u32[]{:S(2)}) async-start(bf16[8,2,4,256,256]{4,3,2,1,0:T(8,128)(2,1)} %after.24), calls=%async_computation.2 | async-start | bytes 16777216 | tf_op jit(solution)/shard_map/all_to_all | solution.py:821
  494.1 99.0 %all-to-all-start.3 = ((bf16[8,1,4,256,512]{4,3,2,1,0:T(8,128)(2,1)}), bf16[8,1,4,256,512]{4,3,2,1,0:T(8,128)(2,1)}, u32[]{:S(2)}, u32[]{:S(2)}) async-start(bf16[8,1,4,256,512]{4,3,2,1,0:T(8,128)(2,1)} %after.25), calls=%async_computation.3 | async-start | bytes 16777216 | tf_op jit(solution)/shard_map/all_to_all | solution.py:821
  593.1 99.3 %all-to-all-start.4 = ((bf16[8,1,4,256,512]{4,3,2,1,0:T(8,128)(2,1)}), bf16[8,1,4,256,512]{4,3,2,1,0:T(8,128)(2,1)}, u32[]{:S(2)}, u32[]{:S(2)}) async-start(bf16[8,1,4,256,512]{4,3,2,1,0:T(8,128)(2,1)} %after.26), calls=%async_computation.4 | async-start | bytes 16777216 | tf_op jit(solution)/shard_map/all_to_all | solution.py:821
  744.9 99.1 %all-to-all-start.5 = ((bf16[8,2,4,256,256]{4,3,2,1,0:T(8,128)(2,1)}), bf16[8,2,4,256,256]{4,3,2,1,0:T(8,128)(2,1)}, u32[]{:S(2)}, u32[]{:S(2)}) async-start(bf16[8,2,4,256,256]{4,3,2,1,0:T(8,128)(2,1)} %bitcast.114), calls=%async_computation.5 | async-start | bytes 16777216 | tf_op jit(solution)/shard_map/all_to_all | solution.py:821
  750.0 285.3 %reduce-scatter.8.cloned.1.call-start = ((), (), s32[]{:S(2)}) async-start(), calls=%async_computation.20 | async-start | bytes 5242880 | tf_op jit(solution)/shard_map/reduce_scatter | solution.py:901
  874.9 99.4 %all-to-all-start.6 = ((bf16[8,2,4,256,256]{4,3,2,1,0:T(8,128)(2,1)}), bf16[8,2,4,256,256]{4,3,2,1,0:T(8,128)(2,1)}, u32[]{:S(2)}, u32[]{:S(2)}) async-start(bf16[8,2,4,256,256]{4,3,2,1,0:T(8,128)(2,1)} %bitcast.115), calls=%async_computation.6 | async-start | bytes 16777216 | tf_op jit(solution)/shard_map/all_to_all | solution.py:821
  979.1 160.5 %reduce-scatter.10.cloned.1.call-start = ((), (), s32[]{:S(2)}) async-start(), calls=%async_computation.21 | async-start | bytes 5242880 | tf_op jit(solution)/shard_map/reduce_scatter | solution.py:901
  984.7 49.9 %collective-permute-start.17 = (f32[16,256]{1,0:T(8,128)S(1)}, f32[16,256]{1,0:T(8,128)S(1)}, u32[]{:S(2)}, u32[]{:S(2)}) collective-permute-start(f32[16,256]{1,0:T(8,128)S(1)} %reshape.220), channel_id=1, source_target_pairs={{0,8},{8,0},{16,24},{24,16},{1,9},{9,1},{17,25},{25,17},{2,10},{10... | collective-permute-start | bytes 49160 | tf_op jit(solution)/shard_map/ppermute | solution.py:206
  985.3 49.3 %collective-permute-start.18 = (f32[16,256]{1,0:T(8,128)S(1)}, f32[16,256]{1,0:T(8,128)S(1)}, u32[]{:S(2)}, u32[]{:S(2)}) collective-permute-start(f32[16,256]{1,0:T(8,128)S(1)} %reshape.220), channel_id=1, source_target_pairs={{0,16},{8,24},{16,0},{24,8},{1,17},{9,25},{17,1},{25,9},{2,18},{10... | collective-permute-start | bytes 49160 | tf_op jit(solution)/shard_map/ppermute | solution.py:206
  985.9 48.7 %collective-permute-start.19 = (f32[16,256]{1,0:T(8,128)S(1)}, f32[16,256]{1,0:T(8,128)S(1)}, u32[]{:S(2)}, u32[]{:S(2)}) collective-permute-start(f32[16,256]{1,0:T(8,128)S(1)} %reshape.220), channel_id=1, source_target_pairs={{0,24},{8,16},{16,8},{24,0},{1,25},{9,17},{17,9},{25,1},{2,26},{10... | collective-permute-start | bytes 49160 | tf_op jit(solution)/shard_map/ppermute | solution.py:206
  1097.4 107.5 %all-to-all-start.8 = ((bf16[8,2,4,256,256]{4,3,2,1,0:T(8,128)(2,1)}), bf16[8,2,4,256,256]{4,3,2,1,0:T(8,128)(2,1)}, u32[]{:S(2)}, u32[]{:S(2)}) async-start(bf16[8,2,4,256,256]{4,3,2,1,0:T(8,128)(2,1)} %bitcast.116), calls=%async_computation.10 | async-start | bytes 16777216 | tf_op jit(solution)/shard_map/all_to_all | solution.py:821
  1102.4 336.3 %reduce-scatter.14.cloned.1.call-start = ((), (), s32[]{:S(2)}) async-start(), calls=%async_computation.23 | async-start | bytes 147456 | tf_op jit(solution)/shard_map/reduce_scatter | solution.py:1025
  1208.2 44.9 %collective-permute-start.21 = (bf16[2048,256]{1,0:T(8,128)(2,1)S(1)}, bf16[2048,256]{1,0:T(8,128)(2,1)}, u32[]{:S(2)}, u32[]{:S(2)}) collective-permute-start(bf16[2048,256]{1,0:T(8,128)(2,1)S(1)} %get-tuple-element.96.refs_3_.refs_4_.refs_2_), channel_id=1, source_target_pairs={{0,8},{8,0},{16,24},{24,16},{1,9},{9,1},{17,25},{25,17},{2,10},{10... | collective-permute-start | bytes 3145736 | tf_op jit(solution)/shard_map/ppermute | solution.py:206
  1209.5 229.2 %reduce-scatter.12.cloned.1.call-start = ((), (), s32[]{:S(2)}) async-start(), calls=%async_computation.22 | async-start | bytes 5242880 | tf_op jit(solution)/shard_map/reduce_scatter | solution.py:901
  1209.5 75.8 %collective-permute-start.23 = (bf16[2048,256]{1,0:T(8,128)(2,1)S(1)}, bf16[2048,256]{1,0:T(8,128)(2,1)}, u32[]{:S(2)}, u32[]{:S(2)}) collective-permute-start(bf16[2048,256]{1,0:T(8,128)(2,1)S(1)} %get-tuple-element.96.refs_3_.refs_4_.refs_2_), channel_id=1, source_target_pairs={{0,16},{8,24},{16,0},{24,8},{1,17},{9,25},{17,1},{25,9},{2,18},{10... | collective-permute-start | bytes 3145736 | tf_op jit(solution)/shard_map/ppermute | solution.py:206
  1211.1 75.1 %collective-permute-start.22 = (bf16[2048,256]{1,0:T(8,128)(2,1)S(1)}, bf16[2048,256]{1,0:T(8,128)(2,1)}, u32[]{:S(2)}, u32[]{:S(2)}) collective-permute-start(bf16[2048,256]{1,0:T(8,128)(2,1)S(1)} %get-tuple-element.97.refs_2_.refs_3_.refs_1_), channel_id=1, source_target_pairs={{0,16},{8,24},{16,0},{24,8},{1,17},{9,25},{17,1},{25,9},{2,18},{10... | collective-permute-start | bytes 3145736 | tf_op jit(solution)/shard_map/ppermute | solution.py:206
  1308.8 99.0 %all-to-all-start.10 = ((bf16[8,2,4,256,256]{4,3,2,1,0:T(8,128)(2,1)}), bf16[8,2,4,256,256]{4,3,2,1,0:T(8,128)(2,1)}, u32[]{:S(2)}, u32[]{:S(2)}) async-start(bf16[8,2,4,256,256]{4,3,2,1,0:T(8,128)(2,1)} %bitcast.117), calls=%async_computation.12 | async-start | bytes 16777216 | tf_op jit(solution)/shard_map/all_to_all | solution.py:821
  1313.8 236.5 %reduce-scatter.20.cloned.1.call-start = ((), (), s32[]{:S(2)}) async-start(), calls=%async_computation.26 | async-start | bytes 1310720 | tf_op jit(solution)/shard_map/reduce_scatter | solution.py:253
  1344.6 250.6 %reduce-scatter.16.cloned.1.call-start = ((), (), s32[]{:S(2)}) async-start(), calls=%async_computation.24 | async-start | bytes 5242880 | tf_op jit(solution)/shard_map/reduce_scatter | solution.py:901
  1454.1 46.2 %collective-permute-start.27 = (bf16[2048,512]{1,0:T(8,128)(2,1)}, bf16[2048,512]{1,0:T(8,128)(2,1)}, u32[]{:S(2)}, u32[]{:S(2)}) collective-permute-start(bf16[2048,512]{1,0:T(8,128)(2,1)} %convolution_convert_fusion.2), channel_id=1, source_target_pairs={{0,8},{8,0},{16,24},{24,16},{1,9},{9,1},{17,25},{25,17},{2,10},{10... | collective-permute-start | bytes 6291464 | tf_op jit(solution)/shard_map/ppermute | solution.py:206
  1454.8 144.9 %reduce-scatter.18.cloned.1.call-start = ((), (), s32[]{:S(2)}) async-start(), calls=%async_computation.25 | async-start | bytes 3932160 | tf_op jit(solution)/shard_map/reduce_scatter | solution.py:253
  (108 other events, 1804.3 us)
Sparse Core Ops, SparseCore 0:
  10.2 36.4 all-gather.9
  48.3 69.3 all-gather.11
  119.3 79.3 all-gather.13
  200.0 79.2 all-gather.15
  287.3 148.6 all-gather.17
  875.0 73.5 reduce-scatter.7
  1066.4 73.1 reduce-scatter.9
  1209.6 27.9 reduce-scatter.13
  1284.1 74.1 reduce-scatter.11
  1360.5 27.8 reduce-scatter.19
  1454.9 74.9 reduce-scatter.15
  1532.0 61.3 reduce-scatter.17
